TPU v7x, 256 devices: a whole 4x4x8 slice. The times are simulated.
256 devices in a mesh: orb: 16 (over z, x_hi), cell: 16 (over y, x_lo, core).
Axes of the slice: x: 4 (x_hi: 2, x_lo: 2; x = x_hi * 2 + x_lo), y: 4, z: 8, core: 2. Of those that a mesh axis runs over, the one named last changes fastest.
Arguments:
- potentials: bfloat16 [192, 65536], P(None, 'cell'), may hold values from -6 to 6
- orbitals: bfloat16 [512, 65536], P('orb', 'cell'), may hold values from -6 to 6
- levels: float32 [512], replicated, may hold values from 0.2 to 4
- occ_index: int32 [128], replicated, may hold values from 0 to 511, as said below
- coul_rows: float32 [256, 256], replicated, may hold values from -0.375 to 0.375
- coul_cols: float32 [256, 256], replicated, may hold values from -0.375 to 0.375
Outputs:
- screened: float32 [192, 256, 256], P('orb', 'cell')
Inputs may be any that keep to these rules, and one draw needn't show every extreme that they name: `occ_index`: 128 distinct orbital numbers.
All inputs are finite; a program needn't handle non-finite values.
Results may differ from a plain program's by a relative error of at most 0.004.
Values may be sent and summed in bfloat16 or wider, within the bound.
No kernel may reach another device: no remote copies, remote signals or barrier semaphores. Data moves between devices by JAX's collectives and lax.ppermute only.
A program may use at most 64 MiB of HBM per device.

v0:
```python
import jax
import jax.numpy as jnp
from jax import lax
from jax.sharding import Mesh
from jax.sharding import PartitionSpec as P

SIDE = 256
CELL = ("cell_0", "cell_1", "cell_2")
ORB = ("orb_0", "orb_1")


def whole_of(shard, axes, dim):
    for axis in reversed(axes):
        shard = lax.all_gather(shard, axis, axis=dim, tiled=True)
    return shard


def rows_for(lines, count):
    spare = -lines.shape[0] % count
    if not spare:
        return lines
    return jnp.concatenate([lines, jnp.zeros((spare, *lines.shape[1:]), lines.dtype)])


def copy_for_each(shard, axis):
    copies = jnp.broadcast_to(shard, (lax.axis_size(axis), *shard.shape))
    return lax.all_to_all(copies, axis, split_axis=0, concat_axis=0, tiled=True)


def joined_along(parts, dim):
    parts = jnp.moveaxis(parts, 0, dim)
    dims = parts.shape
    return parts.reshape(*dims[:dim], dims[dim] * dims[dim + 1], *dims[dim + 2 :])


def gather_axes(shard, axes, dim):
    far, near = axes
    parts = copy_for_each(copy_for_each(shard, far), near)
    return joined_along(parts.swapaxes(0, 1).reshape(-1, *shard.shape), dim)


def in_blocks(shard, dim, count):
    dims = shard.shape
    parts = shard.reshape(*dims[:dim], count, dims[dim] // count, *dims[dim + 1 :])
    return jnp.moveaxis(parts, dim, 0)


def sent_and_summed(shard, axis, dim):
    parts = in_blocks(shard, dim, lax.axis_size(axis))
    arrived = lax.all_to_all(parts, axis, split_axis=0, concat_axis=0, tiled=True)
    return arrived.sum(axis=0)


def sum_in_two_steps(shard, axes, dim):
    far, near = axes
    own = sent_and_summed(in_blocks(shard, dim, lax.axis_size(far)), near, dim + 1)
    return jnp.sum(lax.all_to_all(own, far, 0, 0, tiled=True), axis=0)


def total_of(shard, axes):
    lines = shard.reshape(-1, shard.shape[-1])
    padded = rows_for(lines, lax.axis_size(axes[0]) * lax.axis_size(axes[1]))
    whole = gather_axes(sum_in_two_steps(padded, axes, 0), axes, 0)
    return lax.slice_in_dim(whole, 0, len(lines)).reshape(shard.shape)


def summed_rows(shard, axes, dim):
    if not axes:
        return shard
    nearer = lax.psum_scatter(shard, axes[0], scatter_dimension=dim, tiled=True)
    return summed_rows(nearer, axes[1:], dim)


def pair_block(occ_block, basis):
    joined = occ_block.astype(jnp.float32)[:, None, :] * basis.astype(jnp.float32)[None, :, :]
    return joined.reshape(-1, basis.shape[1]).astype(jnp.bfloat16)


def body(potentials, orbitals, levels, occ_index, coul_rows, coul_cols):
    points_dev = orbitals.shape[1]
    volume = points_dev * lax.axis_size(CELL)
    orb_count = lax.axis_size(ORB)
    my_rank = lax.axis_index(ORB)
    labels = jnp.arange(levels.shape[0], dtype=jnp.int32)
    marked = jnp.any(occ_index[:, None] == labels[None, :], axis=0)
    empty_all = 1.0 - marked.astype(jnp.float32)
    slot_count = occ_index.shape[0] // orb_count
    everything = whole_of(orbitals, ORB, 0)
    own_slots = lax.dynamic_slice_in_dim(occ_index, my_rank * slot_count, slot_count)
    occ_rows = jnp.take(everything, own_slots, axis=0).reshape(slot_count, 1, points_dev)
    occ_level = levels[own_slots].reshape(slot_count, 1)
    weights = -2.0 * empty_all[None, None, :] / (occ_level[:, :, None] + levels[None, None, :])
    weights = (weights / volume).reshape(slot_count, -1)

    def intersection_step(unused_carry, occ_block):
        products = pair_block(occ_block, everything)
        partial_value = lax.dot_general(
            products, potentials, (((1,), (1,)), ((), ())), preferred_element_type=jnp.float32
        )
        return (unused_carry, partial_value)

    _, intersections = lax.scan(intersection_step, jnp.zeros((), jnp.float32), occ_rows)
    intersections = total_of(intersections, (("cell_0", "cell_1"), "cell_2"))
    guesses = (intersections * weights[:, :, None]).astype(jnp.bfloat16)

    def response_step(running, pieces):
        occ_block, guess_block = pieces
        products = pair_block(occ_block, everything)
        running = running + lax.dot_general(
            guess_block, products, (((0,), (0,)), ((), ())), preferred_element_type=jnp.float32
        )
        return (running, None)

    response, _ = lax.scan(
        response_step,
        jnp.zeros((potentials.shape[0], points_dev), jnp.float32),
        (occ_rows, guesses),
    )
    owned_sum = summed_rows(response, ORB, 0)
    row_count = points_dev // SIDE
    plane_rows = owned_sum.reshape(owned_sum.shape[0], row_count, SIDE)
    by_columns = jnp.einsum("vrc,dc->vrd", plane_rows, coul_cols, precision=lax.Precision.HIGHEST)
    mixed_rows = jnp.einsum(
        "ab,vbc->vac",
        coul_rows,
        lax.all_to_all(by_columns, CELL, split_axis=2, concat_axis=1, tiled=True),
        precision=lax.Precision.HIGHEST,
    )
    return lax.all_to_all(mixed_rows, CELL, split_axis=1, concat_axis=2, tiled=True)


def solution(mesh):
    torus = Mesh(
        mesh.devices.reshape(8, 2, 4, 2, 2), ("orb_0", "orb_1", "cell_0", "cell_1", "cell_2")
    )
    return jax.shard_map(
        body,
        mesh=torus,
        in_specs=(P(None, CELL), P(ORB, CELL), P(), P(), P(), P()),
        out_specs=P(ORB, CELL, None),
        check_vma=False,
    )
```

profile of v0, /device:TPU:1, one launch (start us, length us, event | category | flops | bytes accessed | tf_op | source)
XLA Modules:
  0.0 336.5 jit_solution(8384014790015756396)
XLA Ops:
  6.5 11.7 %all_gather.6 = bf16[64,4096]{1,0:T(8,128)(2,1)} all-gather(bf16[32,4096]{1,0:T(8,128)(2,1)} %param.11), channel_id=1, replica_groups=mesh['orb_0'=8,'orb_1'=2,'cell_0'=4,'cell_1'=2,'cell_2'=2] {'orb_1'}, dimensions={0}, use_global_device_ids=true | all-gather | bytes 786432 | tf_op jit(solution)/shard_map/all_gather | solution.py:14
  19.1 56.7 %all-gather.2.cloned.1.call-done = bf16[512,4096]{1,0:T(8,128)(2,1)} async-done(((bf16[64,4096]{1,0:T(8,128)(2,1)}), bf16[512,4096]{1,0:T(8,128)(2,1)}) %all-gather.2.cloned.1.call-update) | async-done | bytes 4194320 | tf_op jit(solution)/shard_map/all_gather | solution.py:14
  75.7 3.4 %gather_fusion = bf16[8,4096]{1,0:T(8,128)(2,1)S(1)} fusion(bf16[512,4096]{1,0:T(8,128)(2,1)} %all-gather.2.cloned.1.call-done, s32[1024]{0:T(1024)S(1)} %pad_clamp_fusion), kind=kCustom, calls=%fused_computation | custom fusion | bytes 131104 | tf_op jit(solution)/shard_map/jit(_take)/gather | solution.py:90
  79.3 40.0 %while.21 = (s32[]{:T(128)}, f32[8,512,192]{1,2,0:T(8,128)}, bf16[8,1,4096]{2,1,0:T(2,128)(2,1)S(1)}, bf16[512,4096]{1,0:T(8,128)(2,1)}, bf16[192,4096]{1,0:T(8,128)(2,1)}, /*index=5*/s32[]{:T(128)}) while((s32[]{:T(128)}, f32[8,512,192]{1,2,0:T(8,128)}, bf16[8,1,4096]{2,1,0:T(2,128)(2,1)S(1)}, bf16[512,4096]{1,0:T(8,128)(2,1)}, ...), condition=%wide.region_1.2_spmd, body=%wide.region_0.0_spmd.sunk | while | flops 811601920 | bytes 6201929 | solution.py:102
  79.4 5.0 %fusion.20 = f32[8,512,192]{1,2,0:T(8,128)} fusion(f32[8,512,192]{1,2,0:T(8,128)} %get-tuple-element.220, s32[]{:T(128)} %get-tuple-element.219, bf16[192,4096]{1,0:T(8,128)(2,1)} %get-tuple-element.229, bf16[512,4096]{1,0:T(8,128)(2,1)} %get-tuple-element.228, f32[4096]{0:T(1024)S(1)} %bitcast.72), kind=kOutput, calls=%fused_computation.6.clone.1 | convolution fusion | flops 811597824 | bytes 6177280 | tf_op jit(solution)/shard_map/while/body/eval_jaxpr/dot_general | solution.py:97
  84.4 5.0 %fusion.20 = f32[8,512,192]{1,2,0:T(8,128)} fusion(f32[8,512,192]{1,2,0:T(8,128)} %get-tuple-element.220, s32[]{:T(128)} %get-tuple-element.219, bf16[192,4096]{1,0:T(8,128)(2,1)} %get-tuple-element.229, bf16[512,4096]{1,0:T(8,128)(2,1)} %get-tuple-element.228, f32[4096]{0:T(1024)S(1)} %bitcast.72), kind=kOutput, calls=%fused_computation.6.clone.1 | convolution fusion | flops 811597824 | bytes 6177280 | tf_op jit(solution)/shard_map/while/body/eval_jaxpr/dot_general | solution.py:97
  89.4 5.0 %fusion.20 = f32[8,512,192]{1,2,0:T(8,128)} fusion(f32[8,512,192]{1,2,0:T(8,128)} %get-tuple-element.220, s32[]{:T(128)} %get-tuple-element.219, bf16[192,4096]{1,0:T(8,128)(2,1)} %get-tuple-element.229, bf16[512,4096]{1,0:T(8,128)(2,1)} %get-tuple-element.228, f32[4096]{0:T(1024)S(1)} %bitcast.72), kind=kOutput, calls=%fused_computation.6.clone.1 | convolution fusion | flops 811597824 | bytes 6177280 | tf_op jit(solution)/shard_map/while/body/eval_jaxpr/dot_general | solution.py:97
  94.3 5.0 %fusion.20 = f32[8,512,192]{1,2,0:T(8,128)} fusion(f32[8,512,192]{1,2,0:T(8,128)} %get-tuple-element.220, s32[]{:T(128)} %get-tuple-element.219, bf16[192,4096]{1,0:T(8,128)(2,1)} %get-tuple-element.229, bf16[512,4096]{1,0:T(8,128)(2,1)} %get-tuple-element.228, f32[4096]{0:T(1024)S(1)} %bitcast.72), kind=kOutput, calls=%fused_computation.6.clone.1 | convolution fusion | flops 811597824 | bytes 6177280 | tf_op jit(solution)/shard_map/while/body/eval_jaxpr/dot_general | solution.py:97
  99.4 5.0 %fusion.20 = f32[8,512,192]{1,2,0:T(8,128)} fusion(f32[8,512,192]{1,2,0:T(8,128)} %get-tuple-element.220, s32[]{:T(128)} %get-tuple-element.219, bf16[192,4096]{1,0:T(8,128)(2,1)} %get-tuple-element.229, bf16[512,4096]{1,0:T(8,128)(2,1)} %get-tuple-element.228, f32[4096]{0:T(1024)S(1)} %bitcast.72), kind=kOutput, calls=%fused_computation.6.clone.1 | convolution fusion | flops 811597824 | bytes 6177280 | tf_op jit(solution)/shard_map/while/body/eval_jaxpr/dot_general | solution.py:97
  104.3 5.0 %fusion.20 = f32[8,512,192]{1,2,0:T(8,128)} fusion(f32[8,512,192]{1,2,0:T(8,128)} %get-tuple-element.220, s32[]{:T(128)} %get-tuple-element.219, bf16[192,4096]{1,0:T(8,128)(2,1)} %get-tuple-element.229, bf16[512,4096]{1,0:T(8,128)(2,1)} %get-tuple-element.228, f32[4096]{0:T(1024)S(1)} %bitcast.72), kind=kOutput, calls=%fused_computation.6.clone.1 | convolution fusion | flops 811597824 | bytes 6177280 | tf_op jit(solution)/shard_map/while/body/eval_jaxpr/dot_general | solution.py:97
  109.3 5.0 %fusion.20 = f32[8,512,192]{1,2,0:T(8,128)} fusion(f32[8,512,192]{1,2,0:T(8,128)} %get-tuple-element.220, s32[]{:T(128)} %get-tuple-element.219, bf16[192,4096]{1,0:T(8,128)(2,1)} %get-tuple-element.229, bf16[512,4096]{1,0:T(8,128)(2,1)} %get-tuple-element.228, f32[4096]{0:T(1024)S(1)} %bitcast.72), kind=kOutput, calls=%fused_computation.6.clone.1 | convolution fusion | flops 811597824 | bytes 6177280 | tf_op jit(solution)/shard_map/while/body/eval_jaxpr/dot_general | solution.py:97
  114.4 5.0 %fusion.20 = f32[8,512,192]{1,2,0:T(8,128)} fusion(f32[8,512,192]{1,2,0:T(8,128)} %get-tuple-element.220, s32[]{:T(128)} %get-tuple-element.219, bf16[192,4096]{1,0:T(8,128)(2,1)} %get-tuple-element.229, bf16[512,4096]{1,0:T(8,128)(2,1)} %get-tuple-element.228, f32[4096]{0:T(1024)S(1)} %bitcast.72), kind=kOutput, calls=%fused_computation.6.clone.1 | convolution fusion | flops 811597824 | bytes 6177280 | tf_op jit(solution)/shard_map/while/body/eval_jaxpr/dot_general | solution.py:97
  119.3 3.8 %reshape_reshape_reshape.6 = f32[8,2,256,192]{2,1,3,0:T(2,128)S(1)} reshape(f32[8,512,192]{1,2,0:T(8,128)} %get-tuple-element.59) | data formatting | bytes 6291456 | tf_op jit(solution)/shard_map/reshape;reshape;reshape | solution.py:44
  123.5 6.7 %all_to_all.56 = f32[2,8,256,192]{2,3,1,0:T(8,128)S(1)} all-to-all(f32[2,8,256,192]{2,3,1,0:T(8,128)S(1)} %copy.33), channel_id=1, replica_groups=mesh['orb_0'=8,'orb_1'=2,'cell_0'=4,'cell_1'=2,'cell_2'=2] {'cell_2'}, dimensions={0} | all-to-all | bytes 6291456 | tf_op jit(solution)/shard_map/all_to_all | solution.py:50
  131.8 25.4 %all_to_all.57 = f32[8,256,192]{1,2,0:T(8,128)S(1)} all-to-all(f32[8,256,192]{1,2,0:T(8,128)} %reduce_sum.18), channel_id=1, replica_groups=mesh['orb_0'=8,'orb_1'=2,'cell_0'=4,'cell_1'=2,'cell_2'=2] {'cell_0','ce..., dimensions={0} | all-to-all | bytes 3145728 | tf_op jit(solution)/shard_map/all_to_all | solution.py:57
  158.6 4.3 %all-to-all-start.2 = ((f32[8,256,192]{1,2,0:T(8,128)}), f32[8,256,192]{1,2,0:T(8,128)}, u32[]{:S(2)}, u32[]{:S(2)}) async-start(f32[8,256,192]{1,2,0:T(8,128)} %broadcast_in_dim.42), calls=%async_computation.2 | async-start | bytes 3145728 | tf_op jit(solution)/shard_map/all_to_all | solution.py:27
  165.1 17.1 %all-to-all-done.2 = f32[8,256,192]{1,2,0:T(8,128)} async-done(((f32[8,256,192]{1,2,0:T(8,128)}), f32[8,256,192]{1,2,0:T(8,128)}, u32[]{:S(2)}, u32[]{:S(2)}) %all-to-all-start.2) | async-done | bytes 1572896 | tf_op jit(solution)/shard_map/all_to_all | solution.py:27
  183.9 8.8 %all_to_all.58 = f32[2,8,256,192]{2,3,1,0:T(8,128)S(1)} all-to-all(f32[2,8,256,192]{2,3,1,0:T(8,128)S(1)} %broadcast_in_dim.43), channel_id=1, replica_groups=mesh['orb_0'=8,'orb_1'=2,'cell_0'=4,'cell_1'=2,'cell_2'=2] {'cell_2'}, dimensions={0} | all-to-all | bytes 6291456 | tf_op jit(solution)/shard_map/all_to_all | solution.py:27
  195.1 31.1 %while.22 = (s32[]{:T(128)}, f32[192,4096]{1,0:T(8,128)S(1)}, bf16[8,512,192]{1,2,0:T(8,128)(2,1)}, bf16[8,1,4096]{2,1,0:T(2,128)(2,1)S(1)}, bf16[512,4096]{1,0:T(8,128)(2,1)}, /*index=5*/s32[]{:T(128)}, s32[]{:T(128)}) while((s32[]{:T(128)}, f32[192,4096]{1,0:T(8,128)S(1)}, bf16[8,512,192]{1,2,0:T(8,128)(2,1)}, ...), condition=%wide.region_6.7_spmd.clone, body=%wide.region_5.6_spmd.clone.sunk | while | flops 813174784 | bytes 10723931 | solution.py:114
  195.2 3.8 %convolution_add_fusion.2 = f32[192,4096]{1,0:T(8,128)S(1)} fusion(bf16[512,4096]{1,0:T(8,128)(2,1)} %get-tuple-element.249, f32[4096]{0:T(1024)S(1)} %bitcast.69, f32[192,4096]{1,0:T(8,128)S(1)} %get-tuple-element.239, pred[]{:T(512)S(6)} %compare.3, bf16[8,512,192]{1,2,0:T(8,128)(2,1)} %get-tuple-element.247, s32[]{:T(128)} %get-tuple-element.238), kind=kOutput, calls=%fused_computation.9.clone.1 | convolution fusion | flops 813170688 | bytes 10699265 | tf_op jit(solution)/shard_map/while/body/eval_jaxpr/dot_general | solution.py:109
  199.1 3.8 %convolution_add_fusion.2 = f32[192,4096]{1,0:T(8,128)S(1)} fusion(bf16[512,4096]{1,0:T(8,128)(2,1)} %get-tuple-element.249, f32[4096]{0:T(1024)S(1)} %bitcast.69, f32[192,4096]{1,0:T(8,128)S(1)} %get-tuple-element.239, pred[]{:T(512)S(6)} %compare.3, bf16[8,512,192]{1,2,0:T(8,128)(2,1)} %get-tuple-element.247, s32[]{:T(128)} %get-tuple-element.238), kind=kOutput, calls=%fused_computation.9.clone.1 | convolution fusion | flops 813170688 | bytes 10699265 | tf_op jit(solution)/shard_map/while/body/eval_jaxpr/dot_general | solution.py:109
  202.9 3.8 %convolution_add_fusion.2 = f32[192,4096]{1,0:T(8,128)S(1)} fusion(bf16[512,4096]{1,0:T(8,128)(2,1)} %get-tuple-element.249, f32[4096]{0:T(1024)S(1)} %bitcast.69, f32[192,4096]{1,0:T(8,128)S(1)} %get-tuple-element.239, pred[]{:T(512)S(6)} %compare.3, bf16[8,512,192]{1,2,0:T(8,128)(2,1)} %get-tuple-element.247, s32[]{:T(128)} %get-tuple-element.238), kind=kOutput, calls=%fused_computation.9.clone.1 | convolution fusion | flops 813170688 | bytes 10699265 | tf_op jit(solution)/shard_map/while/body/eval_jaxpr/dot_general | solution.py:109
  206.8 3.8 %convolution_add_fusion.2 = f32[192,4096]{1,0:T(8,128)S(1)} fusion(bf16[512,4096]{1,0:T(8,128)(2,1)} %get-tuple-element.249, f32[4096]{0:T(1024)S(1)} %bitcast.69, f32[192,4096]{1,0:T(8,128)S(1)} %get-tuple-element.239, pred[]{:T(512)S(6)} %compare.3, bf16[8,512,192]{1,2,0:T(8,128)(2,1)} %get-tuple-element.247, s32[]{:T(128)} %get-tuple-element.238), kind=kOutput, calls=%fused_computation.9.clone.1 | convolution fusion | flops 813170688 | bytes 10699265 | tf_op jit(solution)/shard_map/while/body/eval_jaxpr/dot_general | solution.py:109
  210.7 3.8 %convolution_add_fusion.2 = f32[192,4096]{1,0:T(8,128)S(1)} fusion(bf16[512,4096]{1,0:T(8,128)(2,1)} %get-tuple-element.249, f32[4096]{0:T(1024)S(1)} %bitcast.69, f32[192,4096]{1,0:T(8,128)S(1)} %get-tuple-element.239, pred[]{:T(512)S(6)} %compare.3, bf16[8,512,192]{1,2,0:T(8,128)(2,1)} %get-tuple-element.247, s32[]{:T(128)} %get-tuple-element.238), kind=kOutput, calls=%fused_computation.9.clone.1 | convolution fusion | flops 813170688 | bytes 10699265 | tf_op jit(solution)/shard_map/while/body/eval_jaxpr/dot_general | solution.py:109
  214.6 3.8 %convolution_add_fusion.2 = f32[192,4096]{1,0:T(8,128)S(1)} fusion(bf16[512,4096]{1,0:T(8,128)(2,1)} %get-tuple-element.249, f32[4096]{0:T(1024)S(1)} %bitcast.69, f32[192,4096]{1,0:T(8,128)S(1)} %get-tuple-element.239, pred[]{:T(512)S(6)} %compare.3, bf16[8,512,192]{1,2,0:T(8,128)(2,1)} %get-tuple-element.247, s32[]{:T(128)} %get-tuple-element.238), kind=kOutput, calls=%fused_computation.9.clone.1 | convolution fusion | flops 813170688 | bytes 10699265 | tf_op jit(solution)/shard_map/while/body/eval_jaxpr/dot_general | solution.py:109
  218.5 3.8 %convolution_add_fusion.2 = f32[192,4096]{1,0:T(8,128)S(1)} fusion(bf16[512,4096]{1,0:T(8,128)(2,1)} %get-tuple-element.249, f32[4096]{0:T(1024)S(1)} %bitcast.69, f32[192,4096]{1,0:T(8,128)S(1)} %get-tuple-element.239, pred[]{:T(512)S(6)} %compare.3, bf16[8,512,192]{1,2,0:T(8,128)(2,1)} %get-tuple-element.247, s32[]{:T(128)} %get-tuple-element.238), kind=kOutput, calls=%fused_computation.9.clone.1 | convolution fusion | flops 813170688 | bytes 10699265 | tf_op jit(solution)/shard_map/while/body/eval_jaxpr/dot_general | solution.py:109
  222.4 3.8 %convolution_add_fusion.2 = f32[192,4096]{1,0:T(8,128)S(1)} fusion(bf16[512,4096]{1,0:T(8,128)(2,1)} %get-tuple-element.249, f32[4096]{0:T(1024)S(1)} %bitcast.69, f32[192,4096]{1,0:T(8,128)S(1)} %get-tuple-element.239, pred[]{:T(512)S(6)} %compare.3, bf16[8,512,192]{1,2,0:T(8,128)(2,1)} %get-tuple-element.247, s32[]{:T(128)} %get-tuple-element.238), kind=kOutput, calls=%fused_computation.9.clone.1 | convolution fusion | flops 813170688 | bytes 10699265 | tf_op jit(solution)/shard_map/while/body/eval_jaxpr/dot_general | solution.py:109
  227.9 39.9 %reduce-scatter.4.cloned.1.call-done = f32[24,4096]{1,0:T(8,128)} async-done(((f32[192,4096]{1,0:T(8,128)}), f32[24,4096]{1,0:T(8,128)}) %reduce-scatter.4.cloned.1.call-update) | async-done | bytes 393232 | tf_op jit(solution)/shard_map/reduce_scatter | solution.py:70
  267.9 11.8 %fusion = f32[16,4096]{1,0:T(8,128)S(1)} fusion(f32[24,4096]{1,0:T(8,128)} %reduce-scatter.4.cloned.1.call-done), kind=kCustom, calls=%all-reduce-scatter | all-reduce-scatter fusion | flops 131073 | bytes 656384
  286.2 17.7 %all_to_all.59 = f32[16,1,3072]{2,1,0:T(1,128)S(1)} all-to-all(f32[16,1,3072]{2,1,0:T(1,128)S(1)} %reshape.154), channel_id=1, replica_groups=mesh['orb_0'=8,'orb_1'=2,'cell_0'=4,'cell_1'=2,'cell_2'=2] {'cell_0','ce..., dimensions={0} | all-to-all | bytes 393216 | tf_op jit(solution)/shard_map/all_to_all | solution.py:126
  313.0 9.9 %all_to_all.60 = f32[16,1,3072]{2,1,0:T(1,128)S(1)} all-to-all(f32[16,1,3072]{2,1,0:T(1,128)S(1)} %reshape.156), channel_id=1, replica_groups=mesh['orb_0'=8,'orb_1'=2,'cell_0'=4,'cell_1'=2,'cell_2'=2] {'cell_0','ce..., dimensions={0} | all-to-all | bytes 393216 | tf_op jit(solution)/shard_map/all_to_all | solution.py:129
  327.0 2.6 all_to_all.49
  (70 shorter events, 31.5 us)
Async XLA Ops:
  6.5 277.2 %copy-start = (f32[256,256]{1,0:T(8,128)S(1)}, f32[256,256]{1,0:T(8,128)}, u32[]{:S(2)}) copy-start(f32[256,256]{1,0:T(8,128)} %param.15) | copy-start | bytes 786436
  6.5 69.2 %all-gather.2.cloned.1.call-start = ((), (), s32[]{:S(2)}) async-start(), calls=%async_computation.7 | async-start | bytes 4718592 | tf_op jit(solution)/shard_map/all_gather | solution.py:14
  157.1 5.8 %copy-start.2 = (f32[512]{0:T(512)S(1)}, f32[512]{0:T(512)}, u32[]{:S(2)}) copy-start(f32[512]{0:T(512)} %param.12) | copy-start | bytes 6148
  158.6 23.6 %all-to-all-start.2 = ((f32[8,256,192]{1,2,0:T(8,128)}), f32[8,256,192]{1,2,0:T(8,128)}, u32[]{:S(2)}, u32[]{:S(2)}) async-start(f32[8,256,192]{1,2,0:T(8,128)} %broadcast_in_dim.42), calls=%async_computation.2 | async-start | bytes 3145728 | tf_op jit(solution)/shard_map/all_to_all | solution.py:27
  162.9 105.0 %reduce-scatter.4.cloned.1.call-start = ((), (), s32[]{:S(2)}) async-start(), calls=%async_computation.8 | async-start | bytes 3538944 | tf_op jit(solution)/shard_map/reduce_scatter | solution.py:70
  192.8 0.7 copy-start.4
  226.2 1.7 copy-start.1
  226.3 55.7 %copy-start.5 = (u32[256]{0:T(256)S(1)}, u32[256]{0:T(256)}, u32[]{:S(2)}) copy-start(u32[256]{0:T(256)} %constant.69) | copy-start | bytes 3076
  279.7 3.6 %collective-permute-start = (f32[4,4096]{1,0:T(4,128)S(1)}, f32[4,4096]{1,0:T(4,128)S(1)}, u32[]{:S(2)}, u32[]{:S(2)}) collective-permute-start(f32[4,4096]{1,0:T(4,128)S(1)} %slice.4), channel_id=1, source_target_pairs={{0,16},{1,17},{2,18},{3,19},{4,20},{5,21},{6,22},{7,23},{8,24},{9,... | collective-permute-start | bytes 196616
  306.4 4.1 %copy-start.3 = (f32[256,256]{1,0:T(8,128)S(1)}, f32[256,256]{1,0:T(8,128)}, u32[]{:S(2)}) copy-start(f32[256,256]{1,0:T(8,128)} %param.14) | copy-start | bytes 786436
Sparse Core Ops, SparseCore 0:
  18.4 57.2 all-gather.1
  228.1 39.7 reduce-scatter.3
where the time goes:
time: 338 us; the launch traced here: 336 us
  waiting for transfers between devices  114 us (34%)
  blocking collectives  92 us (27%)
  matrix products  71.3 us (21%)
  local copies, waits for them, and re-layouts  29.9 us (9%)
  between operations  14.3 us (4%)
  other arithmetic  8.13 us (2%)
  starting transfers between devices  6.59 us (2%)
    all_gather x1, waiting for transfers between devices, whole_of(): shard = lax.all_gather(shard, axis, axis=dim, tiled=True)  56.7 us
    reduce_scatter x1, waiting for transfers between devices, summed_rows(): nearer = lax.psum_scatter(shard, axes[0], scatter_dimension=dim, tiled=True)  39.9 us
    dot_general x8, matrix products, intersection_step(): lax.dot_general(products, potentials, (((1,), (1,)), ((), ())), preferred...  39.8 us
    dot_general x8, matrix products, response_step(): lax.dot_general(guess_block, products, (((0,), (0,)), ((), ())), preferre...  30.7 us
    all_to_all x1, blocking collectives, sum_in_two_steps(): return jnp.sum(lax.all_to_all(own, far, 0, 0, tiled=True), axis=0)  25.4 us
    all_to_all x1, blocking collectives, body(): lax.all_to_all(by_columns, CELL, split_axis=2, concat_axis=1, tiled=True)  17.7 us
    all_to_all x1, waiting for transfers between devices, copy_for_each(): return lax.all_to_all(copies, axis, split_axis=0, concat_axis=0, tiled=True)  17.1 us
    unnamed x1, blocking collectives  11.8 us
  transfers between devices with their start and end apart: 4, of which 4 were waited for; matrix products, arithmetic and copies ran while one was open for 1% of the time, Pallas kernels for 0%

commit v1 on v0

v1 whole, which is shorter than its diff:
```python
import functools

import jax
import jax.numpy as jnp
from jax import lax
from jax.experimental import pallas as pl
from jax.experimental.pallas import tpu as pltpu
from jax.sharding import Mesh
from jax.sharding import PartitionSpec as P

SIDE = 256
Z, XH, Y, XL, CORE = "z", "x_hi", "y", "x_lo", "core"
CELL = (Y, XL, CORE)
ORB = (Z, XH)
CHIP = (Y, XL)
F32, BF16 = jnp.float32, jnp.bfloat16
HIGH = lax.Precision.HIGHEST
SWAP = ((0, 1), (1, 0))


def swapped(shard, axis):
    return lax.ppermute(shard, axis, SWAP)


def exchanged(parts, axes):
    return lax.all_to_all(parts, axes, split_axis=0, concat_axis=0, tiled=True)


def products(occ, basis, first, count):
    rows = [occ[first + n : first + n + 1, :] * basis for n in range(count)]
    return jnp.concatenate(rows, axis=0)


def project_kernel(occ_ref, basis_ref, pot_ref, far_ref, near_ref, *, group):
    step, half = pl.program_id(0), pl.num_programs(0) // 2
    blocks, count, width = occ_ref.shape
    parts = []
    for first in range(0, count, group):
        total = None
        for k in range(blocks):
            cut = slice(k * width, (k + 1) * width)
            pairs = products(occ_ref[k], basis_ref[:, cut], first, group)
            term = lax.dot_general(
                pot_ref[:, cut], pairs, (((1,), (1,)), ((), ())), preferred_element_type=F32
            )
            total = term if total is None else total + term
        parts.append(total)

    @pl.when(step < half)
    def _():
        for n, total in enumerate(parts):
            far_ref[n] = total

    @pl.when(step >= half)
    def _():
        for n, total in enumerate(parts):
            near_ref[n] = total


def project(occ, basis, pot, group, per_step):
    blocks, slots, width = occ.shape
    rows, points = basis.shape
    nv = pot.shape[0]
    steps = slots // per_step
    half = steps // 2
    out_count = per_step // group
    lanes = group * rows
    out = jax.ShapeDtypeStruct((slots // 2 // group, nv, lanes), F32)
    return pl.pallas_call(
        functools.partial(project_kernel, group=group),
        grid=(steps,),
        in_specs=[
            pl.BlockSpec((blocks, per_step, width), lambda t: (0, t, 0)),
            pl.BlockSpec((rows, points), lambda t: (0, 0)),
            pl.BlockSpec((nv, points), lambda t: (0, 0)),
        ],
        out_specs=[
            pl.BlockSpec((out_count, nv, lanes), lambda t: (jnp.minimum(t, half - 1), 0, 0)),
            pl.BlockSpec((out_count, nv, lanes), lambda t: (jnp.maximum(t - half, 0), 0, 0)),
        ],
        out_shape=[out, out],
        cost_estimate=pl.CostEstimate(
            flops=2 * slots * rows * points * nv, bytes_accessed=10_000_000, transcendentals=0
        ),
        name="project",
    )(occ, basis, pot)


def respond_kernel(occ_ref, basis_ref, far_ref, near_ref, out_ref, *, group):
    blocks, nv, lanes = far_ref.shape
    total = None
    for h, ref in enumerate((far_ref, near_ref)):
        for b in range(blocks):
            pairs = products(occ_ref[0], basis_ref[...], (h * blocks + b) * group, group)
            term = jnp.dot(ref[b], pairs, preferred_element_type=F32)
            total = term if total is None else total + term
    owners, lines, per_owner, side = out_ref.shape
    for n in range(owners):
        for r in range(lines):
            piece = total[n * per_owner : (n + 1) * per_owner, r * side : (r + 1) * side]
            out_ref[n, r] = piece.astype(out_ref.dtype)


def respond(occ, basis, far, near, group, owners):
    blocks, slots, width = occ.shape
    rows, points = basis.shape
    count, nv, lanes = far.shape
    lines = width // SIDE
    return pl.pallas_call(
        functools.partial(respond_kernel, group=group),
        grid=(blocks,),
        in_specs=[
            pl.BlockSpec((1, slots, width), lambda k: (k, 0, 0)),
            pl.BlockSpec((rows, width), lambda k: (0, k)),
            pl.BlockSpec((count, nv, lanes), lambda k: (0, 0, 0)),
            pl.BlockSpec((count, nv, lanes), lambda k: (0, 0, 0)),
        ],
        out_specs=pl.BlockSpec((owners, lines, nv // owners, SIDE), lambda k: (0, k, 0, 0)),
        out_shape=jax.ShapeDtypeStruct((owners, points // SIDE, nv // owners, SIDE), BF16),
        cost_estimate=pl.CostEstimate(
            flops=2 * slots * rows * points * nv, bytes_accessed=6_000_000, transcendentals=0
        ),
        name="respond",
    )(occ, basis, far, near)


def columns_kernel(plane_ref, cols_ref, out_ref):
    nv, lines, side = plane_ref.shape
    mixed = lax.dot_general(
        plane_ref[...].reshape(nv * lines, side),
        cols_ref[...],
        (((1,), (1,)), ((), ())),
        precision=HIGH,
        preferred_element_type=F32,
    ).reshape(nv, lines, side)
    per_dest = out_ref.shape[2] // 128
    for u in range(nv * side // 128):
        piece = mixed[u // 2, :, (u % 2) * 128 : (u % 2 + 1) * 128]
        at = u % per_dest * 128
        out_ref[u // per_dest, :, at : at + 128] = piece.astype(out_ref.dtype)


def rows_kernel(near_ref, far_ref, mix_near_ref, mix_far_ref, out_ref):
    chips, lines, width = near_ref.shape
    total = None
    for ref, mix in ((near_ref, mix_near_ref), (far_ref, mix_far_ref)):
        block = ref[...].astype(F32).reshape(chips * lines, width)
        term = jnp.dot(mix[...], block, precision=HIGH, preferred_element_type=F32)
        total = term if total is None else total + term
    out_ref[...] = total.reshape(chips, lines, width).astype(out_ref.dtype)


def final_kernel(parts_ref, out_ref):
    nv, lines, side = out_ref.shape
    per_dest = parts_ref.shape[2] // 128
    for u in range(nv * side // 128):
        at = u % per_dest * 128
        piece = parts_ref[u // per_dest, :, at : at + 128]
        out_ref[u // 2, :, (u % 2) * 128 : (u % 2 + 1) * 128] = piece.astype(F32)


def small_call(kernel, out, *args):
    return pl.pallas_call(kernel, out_shape=out, name=kernel.__name__)(*args)


def body(potentials, orbitals, levels, occ_index, coul_rows, coul_cols):
    nv, points = potentials.shape
    mine = orbitals.shape[0]
    norb, nocc = levels.shape[0], occ_index.shape[0]
    nz, nx, ny, nl, nc = (lax.axis_size(a) for a in (Z, XH, Y, XL, CORE))
    z, xh, y, xl, core = (lax.axis_index(a) for a in (Z, XH, Y, XL, CORE))
    chips = ny * nl
    chip = y * nl + xl
    width = points // nz
    slots = nocc // nx
    group = slots // (nc * chips)
    volume = points * chips * nc

    basis = jnp.concatenate([orbitals, swapped(orbitals, XH)], axis=0)

    by_points = exchanged(jnp.moveaxis(orbitals.reshape(mine, nz, width), 1, 0), Z)
    by_points = by_points.reshape(nz * mine, width)
    held = jnp.arange(nz * mine, dtype=jnp.int32)
    held = (held // mine * nx + xh) * mine + held % mine
    place = jnp.arange(slots, dtype=jnp.int32)
    place = (place + (1 - core) * (slots // 2)) % slots
    kept_occ = occ_index[xh * slots + place]
    sent_occ = occ_index[(1 - xh) * slots + place]

    def selected(wanted):
        chosen = (wanted[:, None] == held[None, :]).astype(BF16)
        return jnp.dot(chosen, by_points, preferred_element_type=F32).astype(BF16)

    occ_part = selected(kept_occ) + swapped(selected(sent_occ), XH)
    occ = exchanged(jnp.broadcast_to(occ_part, (nz, *occ_part.shape)), Z)

    far, near = project(occ, basis, potentials, group, 16)
    summed = (near + swapped(far, CORE)).astype(BF16)
    arrived = exchanged(summed, CHIP)
    intersection = jnp.sum(arrived.astype(F32), axis=0)

    labels = jnp.arange(norb, dtype=jnp.int32)
    empty = 1.0 - jnp.any(occ_index[:, None] == labels[None, :], axis=0).astype(F32)
    lane = jnp.arange(group * nx * mine, dtype=jnp.int32)
    slot = xh * slots + core * (slots // 2) + chip * group + lane // (nx * mine)
    partner = lane % (nx * mine) // mine
    other = (z * nx + (xh + partner) % nx) * mine + lane % mine
    weight = -2.0 * empty[other] / (levels[occ_index[slot]] + levels[other]) / volume
    guess = (intersection * weight[None, :]).astype(BF16)

    near_guess = exchanged(jnp.broadcast_to(guess, (chips, *guess.shape)), CHIP)
    far_guess = swapped(near_guess, CORE)
    response = respond(occ, basis, far_guess, near_guess, group, nz)

    owned = jnp.sum(exchanged(response, Z).astype(F32), axis=0)
    count = nv // (nz * nx)
    low, high = owned[:, :count], owned[:, count:]
    kept = jnp.where(xh == 0, low, high)
    sent = jnp.where(xh == 0, high, low).astype(BF16)
    plane = jnp.swapaxes(kept + swapped(sent, XH).astype(F32), 0, 1)

    lines = points // SIDE
    out = jax.ShapeDtypeStruct((chips, lines, count * SIDE // chips), BF16)
    columns = small_call(columns_kernel, out, plane, coul_cols)
    near_cols = exchanged(columns, CHIP)
    far_cols = swapped(near_cols, CORE)
    mix = coul_rows.reshape(chips, nc, lines, chips, nc, lines)
    mix = lax.dynamic_index_in_dim(mix, core, 1, keepdims=False)
    mix_near = lax.dynamic_index_in_dim(mix, core, 3, keepdims=False)
    mix_far = lax.dynamic_index_in_dim(mix, 1 - core, 3, keepdims=False)
    side = chips * lines
    mixed = small_call(
        rows_kernel,
        jax.ShapeDtypeStruct(columns.shape, F32),
        near_cols,
        far_cols,
        mix_near.reshape(side, side),
        mix_far.reshape(side, side),
    )
    parts = exchanged(mixed, CHIP)
    return small_call(final_kernel, jax.ShapeDtypeStruct((count, lines, SIDE), F32), parts)


def solution(mesh):
    torus = Mesh(mesh.devices.reshape(8, 2, 4, 2, 2), (Z, XH, Y, XL, CORE))
    return jax.shard_map(
        body,
        mesh=torus,
        in_specs=(P(None, CELL), P(ORB, CELL), P(), P(), P(), P()),
        out_specs=P(ORB, CELL, None),
        check_vma=False,
    )
```

time: 338 us -> 201 us (0.59)
  matrix products: 71.3 us -> 0.4 us
  blocking collectives: 92 us -> 26.2 us
  waiting for transfers between devices: 114 us -> 74.4 us
  starting transfers between devices: 6.59 us -> 43.8 us
  Pallas kernels: 0 us -> 30.5 us
  between operations: 14.3 us -> 0.26 us
  local copies, waits for them, and re-layouts: 29.9 us -> 19.9 us
  other arithmetic: 8.13 us -> 4.28 us
    dot_general x18 -> x2, matrix products: 71.3 us -> 0.4 us  [selected(): return jnp.dot(chosen, by_points, preferred_element_type=F32).astype(BF16)]
    all_gather x1 -> x0, waiting for transfers between devices: 56.7 us -> none  [whole_of(): shard = lax.all_gather(shard, axis, axis=dim, tiled=True)]
    all_to_all x1 -> x5, waiting for transfers between devices: 17.1 us -> 63.6 us  [exchanged(): return lax.all_to_all(parts, axes, split_axis=0, concat_axis=0, tiled=True)]
    all_to_all x5 -> x2, blocking collectives: 68.5 us -> 26.2 us  [exchanged(): return lax.all_to_all(parts, axes, split_axis=0, concat_axis=0, tiled=True)]
    reduce_scatter x1 -> x0, waiting for transfers between devices: 39.9 us -> none  [summed_rows(): nearer = lax.psum_scatter(shard, axes[0], scatter_dimension=dim, tiled=True)]
    pallas_call x0 -> x5, Pallas kernels: none -> 30.5 us  [the longest x1 14.5 us: project(): pl.pallas_call(functools.partial(project_kernel, group=group), grid=(step...]
    all_to_all x1 -> x5, starting transfers between devices: 4.29 us -> 24.6 us  [exchanged(): return lax.all_to_all(parts, axes, split_axis=0, concat_axis=0, tiled=True)]
    ppermute x0 -> x6, starting transfers between devices: none -> 19.3 us  [swapped(): return lax.ppermute(shard, axis, SWAP)]
  transfers between devices with their start and end apart: 4 -> 11, of which waited for: 4 -> 10; matrix products, arithmetic and copies ran while one was open for 1% -> 8% of each run, Pallas kernels for 0% -> 0%
where the time goes in v1:
time: 201 us; the launch traced here: 200 us
  waiting for transfers between devices  74.4 us (37%)
  starting transfers between devices  43.8 us (22%)
  Pallas kernels  30.5 us (15%)
  blocking collectives  26.2 us (13%)
  local copies, waits for them, and re-layouts  19.9 us (10%)
  other arithmetic  4.28 us (2%)
    all_to_all x5, waiting for transfers between devices, exchanged(): return lax.all_to_all(parts, axes, split_axis=0, concat_axis=0, tiled=True)  63.6 us
    all_to_all x2, blocking collectives, exchanged(): return lax.all_to_all(parts, axes, split_axis=0, concat_axis=0, tiled=True)  26.2 us
    all_to_all x5, starting transfers between devices, exchanged(): return lax.all_to_all(parts, axes, split_axis=0, concat_axis=0, tiled=True)  24.6 us
    ppermute x6, starting transfers between devices, swapped(): return lax.ppermute(shard, axis, SWAP)  19.3 us
    pallas_call x1, Pallas kernels, project(): pl.pallas_call(functools.partial(project_kernel, group=group), grid=(step...  14.5 us
    ppermute x6, waiting for transfers between devices, swapped(): return lax.ppermute(shard, axis, SWAP)  10.8 us
    pallas_call x1, Pallas kernels, respond(): pl.pallas_call(functools.partial(respond_kernel, group=group), grid=(bloc...  10.2 us
    pallas_call x3, Pallas kernels, small_call(): return pl.pallas_call(kernel, out_shape=out, name=kernel.__name__)(*args)  5.84 us
  transfers between devices with their start and end apart: 11, of which 10 were waited for; matrix products, arithmetic and copies ran while one was open for 8% of the time, Pallas kernels for 0%

profile of v1, /device:TPU:1, one launch (start us, length us, event | category | flops | bytes accessed | tf_op | source)
XLA Modules:
  0.0 199.9 jit_solution(6190630318771021376)
XLA Ops:
  1.8 9.0 %all-to-all-start = ((bf16[8,32,512]{2,1,0:T(8,128)(2,1)}), bf16[8,32,512]{2,1,0:T(8,128)(2,1)S(1)}, u32[]{:S(2)}, u32[]{:S(2)}) async-start(bf16[8,32,512]{2,1,0:T(8,128)(2,1)} %copy.19), calls=%async_computation | async-start | bytes 524288 | tf_op jit(solution)/shard_map/all_to_all | solution.py:26
  11.7 9.6 %all-to-all-done = bf16[8,32,512]{2,1,0:T(8,128)(2,1)S(1)} async-done(((bf16[8,32,512]{2,1,0:T(8,128)(2,1)}), bf16[8,32,512]{2,1,0:T(8,128)(2,1)S(1)}, u32[]{:S(2)}, u32[]{:S(2)}) %all-to-all-start) | async-done | bytes 262176 | tf_op jit(solution)/shard_map/all_to_all | solution.py:26
  21.5 2.8 %collective-permute-start = (bf16[64,512]{1,0:T(8,128)(2,1)S(1)}, bf16[64,512]{1,0:T(8,128)(2,1)S(1)}, u32[]{:S(2)}, u32[]{:S(2)}) collective-permute-start(bf16[64,512]{1,0:T(8,128)(2,1)S(1)} %convolution_convert_fusion), channel_id=1, source_target_pairs={{0,16},{16,0},{1,17},{17,1},{2,18},{18,2},{3,19},{19,3},{4,20},{20... | collective-permute-start | bytes 196616 | tf_op jit(solution)/shard_map/ppermute | solution.py:22
  27.3 3.5 %all-to-all-start.1 = ((bf16[8,64,512]{2,1,0:T(8,128)(2,1)}), bf16[8,64,512]{2,1,0:T(8,128)(2,1)S(1)}, u32[]{:S(2)}, u32[]{:S(2)}) async-start(bf16[8,64,512]{2,1,0:T(8,128)(2,1)} %broadcast_in_dim.4), calls=%async_computation.1 | async-start | bytes 1048576 | tf_op jit(solution)/shard_map/all_to_all | solution.py:26
  30.8 2.8 %collective-permute-start.1 = (bf16[32,4096]{1,0:T(8,128)(2,1)S(1)}, bf16[32,4096]{1,0:T(8,128)(2,1)S(1)}, u32[]{:S(2)}, u32[]{:S(2)}) collective-permute-start(bf16[32,4096]{1,0:T(8,128)(2,1)S(1)} %copy-done.2), channel_id=1, source_target_pairs={{0,16},{16,0},{1,17},{17,1},{2,18},{18,2},{3,19},{19,3},{4,20},{20... | collective-permute-start | bytes 786440 | tf_op jit(solution)/shard_map/ppermute | solution.py:22
  33.7 4.0 %collective-permute-done.1 = bf16[32,4096]{1,0:T(8,128)(2,1)S(1)} collective-permute-done((bf16[32,4096]{1,0:T(8,128)(2,1)S(1)}, bf16[32,4096]{1,0:T(8,128)(2,1)S(1)}, u32[]{:S(2)}, u32[]{:S(2)}) %collective-permute-start.1) | collective-permute-done | bytes 262176 | tf_op jit(solution)/shard_map/ppermute | solution.py:22
  37.7 7.3 %all-to-all-done.1.occ_ref = bf16[8,64,512]{2,1,0:T(8,128)(2,1)S(1)} async-done(((bf16[8,64,512]{2,1,0:T(8,128)(2,1)}), bf16[8,64,512]{2,1,0:T(8,128)(2,1)S(1)}, u32[]{:S(2)}, u32[]{:S(2)}) %all-to-all-start.1) | async-done | bytes 524320 | tf_op jit(solution)/shard_map/all_to_all | solution.py:26
  45.8 14.5 %project.1 = (f32[8,192,256]{2,1,0:T(8,128)}, f32[8,192,256]{2,1,0:T(8,128)}) custom-call(bf16[8,64,512]{2,1,0:T(8,128)(2,1)} %copy-done.4, bf16[64,4096]{1,0:T(8,128)(2,1)} %copy-done.7, bf16[192,4096]{1,0:T(8,128)(2,1)} %pot_ref.1), custom_call_target="tpu_custom_call" | custom-call | flops 6442450944 | bytes 10000000 | tf_op jit(solution)/shard_map/project/pallas_call | solution.py:69
  60.2 4.2 %collective-permute-start.2 = (f32[8,192,256]{2,1,0:T(8,128)}, f32[8,192,256]{2,1,0:T(8,128)S(1)}, u32[]{:S(2)}, u32[]{:S(2)}) collective-permute-start(f32[8,192,256]{2,1,0:T(8,128)} %get-tuple-element.8), channel_id=1, source_target_pairs={{0,1},{1,0},{2,3},{3,2},{4,5},{5,4},{6,7},{7,6},{8,9},{9,8},{10,11... | collective-permute-start | bytes 4718600 | tf_op jit(solution)/shard_map/ppermute | solution.py:22
  64.4 1.9 gather_fusion.3
  67.7 2.6 %add_convert_fusion = bf16[8,192,256]{2,1,0:T(8,128)(2,1)} fusion(f32[8,192,256]{2,1,0:T(8,128)} %get-tuple-element.7, f32[8,192,256]{2,1,0:T(8,128)S(1)} %collective-permute-done.2), kind=kLoop, calls=%fused_computation.8 | loop fusion | flops 786432 | bytes 3932160 | tf_op jit(solution)/shard_map/convert_element_type | solution.py:198
  70.3 5.1 %all-to-all-start.2 = ((bf16[8,192,256]{2,1,0:T(8,128)(2,1)}), bf16[8,192,256]{2,1,0:T(8,128)(2,1)S(1)}, u32[]{:S(2)}, u32[]{:S(2)}) async-start(bf16[8,192,256]{2,1,0:T(8,128)(2,1)} %add_convert_fusion), calls=%async_computation.2 | async-start | bytes 1572864 | tf_op jit(solution)/shard_map/all_to_all | solution.py:26
  75.4 1.9 gather_fusion.4
  77.4 1.9 gather_fusion.5
  79.5 1.9 gather_fusion.2
  81.4 6.0 %all-to-all-done.2 = bf16[8,192,256]{2,1,0:T(8,128)(2,1)S(1)} async-done(((bf16[8,192,256]{2,1,0:T(8,128)(2,1)}), bf16[8,192,256]{2,1,0:T(8,128)(2,1)S(1)}, u32[]{:S(2)}, u32[]{:S(2)}) %all-to-all-start.2) | async-done | bytes 786464 | tf_op jit(solution)/shard_map/all_to_all | solution.py:26
  87.6 15.6 %all_to_all.35.near_ref = bf16[8,192,256]{2,1,0:T(8,128)(2,1)S(1)} all-to-all(bf16[8,192,256]{2,1,0:T(8,128)(2,1)S(1)} %broadcast_in_dim.5), channel_id=1, replica_groups=mesh['z'=8,'x_hi'=2,'y'=4,'x_lo'=2,'core'=2] {'y','x_lo'}, dimensions={0} | all-to-all | bytes 1572864 | tf_op jit(solution)/shard_map/all_to_all | solution.py:26
  103.2 1.9 collective-permute-start.3
  105.1 1.9 collective-permute-done.3.far_ref
  107.9 10.2 %respond.1 = bf16[8,16,24,256]{3,2,1,0:T(8,128)(2,1)} custom-call(bf16[8,64,512]{2,1,0:T(8,128)(2,1)} %copy-done.4, bf16[64,4096]{1,0:T(8,128)(2,1)} %copy-done.7, bf16[8,192,256]{2,1,0:T(8,128)(2,1)} %copy-done.9, bf16[8,192,256]{2,1,0:T(8,128)(2,1)} %copy-done.3), custom_call_target="tpu_custom_call" | custom-call | flops 6442450944 | bytes 6000000 | tf_op jit(solution)/shard_map/respond/pallas_call | solution.py:109
  118.1 3.6 %all-to-all-start.4 = ((bf16[8,16,24,256]{3,2,1,0:T(8,128)(2,1)}), bf16[8,16,24,256]{3,2,1,0:T(8,128)(2,1)S(1)}, u32[]{:S(2)}, u32[]{:S(2)}) async-start(bf16[8,16,24,256]{3,2,1,0:T(8,128)(2,1)} %respond.1), calls=%async_computation.4 | async-start | bytes 3145728 | tf_op jit(solution)/shard_map/all_to_all | solution.py:26
  121.7 38.2 %all-to-all-done.4 = bf16[8,16,24,256]{3,2,1,0:T(8,128)(2,1)S(1)} async-done(((bf16[8,16,24,256]{3,2,1,0:T(8,128)(2,1)}), bf16[8,16,24,256]{3,2,1,0:T(8,128)(2,1)S(1)}, u32[]{:S(2)}, u32[]{:S(2)}) %all-to-all-start.4) | async-done | bytes 1572896 | tf_op jit(solution)/shard_map/all_to_all | solution.py:26
  160.4 2.5 %collective-permute-start.4 = (bf16[16,12,256]{2,0,1:T(8,128)(2,1)S(1)}, bf16[16,12,256]{2,0,1:T(8,128)(2,1)S(1)}, u32[]{:S(2)}, u32[]{:S(2)}) collective-permute-start(bf16[16,12,256]{2,0,1:T(8,128)(2,1)S(1)} %select_convert_fusion), channel_id=1, source_target_pairs={{0,16},{16,0},{1,17},{17,1},{2,18},{18,2},{3,19},{19,3},{4,20},{20... | collective-permute-start | bytes 294920 | tf_op jit(solution)/shard_map/ppermute | solution.py:22
  162.9 2.5 %collective-permute-done.4 = bf16[16,12,256]{2,0,1:T(8,128)(2,1)S(1)} collective-permute-done((bf16[16,12,256]{2,0,1:T(8,128)(2,1)S(1)}, bf16[16,12,256]{2,0,1:T(8,128)(2,1)S(1)}, u32[]{:S(2)}, u32[]{:S(2)}) %collective-permute-start.4) | collective-permute-done | bytes 98336 | tf_op jit(solution)/shard_map/ppermute | solution.py:22
  166.4 2.1 %columns_kernel.1 = bf16[8,16,384]{2,1,0:T(8,128)(2,1)} custom-call(f32[12,16,256]{2,1,0:T(8,128)} %add_bitcast_fusion.plane_ref, f32[256,256]{1,0:T(8,128)} %cols_ref.1), custom_call_target="tpu_custom_call" | custom-call | tf_op jit(solution)/shard_map/columns_kernel/pallas_call | solution.py:163
  168.5 3.4 %all-to-all-start.5 = ((bf16[8,16,384]{2,1,0:T(8,128)(2,1)}), bf16[8,16,384]{2,1,0:T(8,128)(2,1)S(1)}, u32[]{:S(2)}, u32[]{:S(2)}) async-start(bf16[8,16,384]{2,1,0:T(8,128)(2,1)} %columns_kernel.1), calls=%async_computation.5 | async-start | bytes 196608 | tf_op jit(solution)/shard_map/all_to_all | solution.py:26
  171.9 2.8 %reshape.322 = f32[8,2,16,8,2,16]{5,4,3,2,1,0:T(2,128)S(1)} reshape(f32[256,256]{1,0:T(8,128)S(1)} %copy-done.6) | data formatting | bytes 524288 | tf_op jit(solution)/shard_map/reshape | solution.py:227
  174.6 2.5 %all-to-all-done.5.near_ref = bf16[8,16,384]{2,1,0:T(8,128)(2,1)S(1)} async-done(((bf16[8,16,384]{2,1,0:T(8,128)(2,1)}), bf16[8,16,384]{2,1,0:T(8,128)(2,1)S(1)}, u32[]{:S(2)}, u32[]{:S(2)}) %all-to-all-start.5) | async-done | bytes 98336 | tf_op jit(solution)/shard_map/all_to_all | solution.py:26
  177.2 5.0 %collective-permute-start.5 = (bf16[8,16,384]{2,1,0:T(8,128)(2,1)S(1)}, bf16[8,16,384]{2,1,0:T(8,128)(2,1)S(1)}, u32[]{:S(2)}, u32[]{:S(2)}) collective-permute-start(bf16[8,16,384]{2,1,0:T(8,128)(2,1)S(1)} %all-to-all-done.5.near_ref), channel_id=1, source_target_pairs={{0,1},{1,0},{2,3},{3,2},{4,5},{5,4},{6,7},{7,6},{8,9},{9,8},{10,11... | collective-permute-start | bytes 294920 | tf_op jit(solution)/shard_map/ppermute | solution.py:22
  185.5 2.1 %rows_kernel.1 = f32[8,16,384]{2,1,0:T(8,128)} custom-call(bf16[8,16,384]{2,1,0:T(8,128)(2,1)} %copy-done.5, bf16[8,16,384]{2,1,0:T(8,128)(2,1)} %copy-done.8, f32[128,128]{1,0:T(8,128)} %reshape.323.mix_near_ref, f32[128,128]{1,0:T(8,128)} %reshape.324.mix_far_ref), custom_call_target="tpu_custom_call" | custom-call | tf_op jit(solution)/shard_map/rows_kernel/pallas_call | solution.py:163
  187.6 10.7 %all_to_all.36.parts_ref = f32[8,16,384]{2,1,0:T(8,128)} all-to-all(f32[8,16,384]{2,1,0:T(8,128)} %rows_kernel.1), channel_id=1, replica_groups=mesh['z'=8,'x_hi'=2,'y'=4,'x_lo'=2,'core'=2] {'y','x_lo'}, dimensions={0} | all-to-all | bytes 393216 | tf_op jit(solution)/shard_map/all_to_all | solution.py:26
  198.3 1.6 final_kernel.1
  (55 shorter events, 13.9 us)
Async XLA Ops:
  0.0 75.4 %copy-start = (f32[512]{0:T(512)S(1)}, f32[512]{0:T(512)}, u32[]{:S(2)}) copy-start(f32[512]{0:T(512)} %param.8) | copy-start | bytes 6148
  0.0 10.9 %copy-start.1 = (s32[128]{0:T(128)S(1)}, s32[128]{0:T(128)}, u32[]{:S(2)}) copy-start(s32[128]{0:T(128)} %param.9) | copy-start | bytes 1540
  1.8 19.5 %all-to-all-start = ((bf16[8,32,512]{2,1,0:T(8,128)(2,1)}), bf16[8,32,512]{2,1,0:T(8,128)(2,1)S(1)}, u32[]{:S(2)}, u32[]{:S(2)}) async-start(bf16[8,32,512]{2,1,0:T(8,128)(2,1)} %copy.19), calls=%async_computation | async-start | bytes 524288 | tf_op jit(solution)/shard_map/all_to_all | solution.py:26
  11.7 19.2 %copy-start.2 = (bf16[32,4096]{1,0:T(8,128)(2,1)S(1)}, bf16[32,4096]{1,0:T(8,128)(2,1)}, u32[]{:S(2)}) copy-start(bf16[32,4096]{1,0:T(8,128)(2,1)} %param.7) | copy-start | bytes 786436
  21.5 4.7 %collective-permute-start = (bf16[64,512]{1,0:T(8,128)(2,1)S(1)}, bf16[64,512]{1,0:T(8,128)(2,1)S(1)}, u32[]{:S(2)}, u32[]{:S(2)}) collective-permute-start(bf16[64,512]{1,0:T(8,128)(2,1)S(1)} %convolution_convert_fusion), channel_id=1, source_target_pairs={{0,16},{16,0},{1,17},{17,1},{2,18},{18,2},{3,19},{19,3},{4,20},{20... | collective-permute-start | bytes 196616 | tf_op jit(solution)/shard_map/ppermute | solution.py:22
  27.3 17.7 %all-to-all-start.1 = ((bf16[8,64,512]{2,1,0:T(8,128)(2,1)}), bf16[8,64,512]{2,1,0:T(8,128)(2,1)S(1)}, u32[]{:S(2)}, u32[]{:S(2)}) async-start(bf16[8,64,512]{2,1,0:T(8,128)(2,1)} %broadcast_in_dim.4), calls=%async_computation.1 | async-start | bytes 1048576 | tf_op jit(solution)/shard_map/all_to_all | solution.py:26
  30.8 6.8 %collective-permute-start.1 = (bf16[32,4096]{1,0:T(8,128)(2,1)S(1)}, bf16[32,4096]{1,0:T(8,128)(2,1)S(1)}, u32[]{:S(2)}, u32[]{:S(2)}) collective-permute-start(bf16[32,4096]{1,0:T(8,128)(2,1)S(1)} %copy-done.2), channel_id=1, source_target_pairs={{0,16},{16,0},{1,17},{17,1},{2,18},{18,2},{3,19},{19,3},{4,20},{20... | collective-permute-start | bytes 786440 | tf_op jit(solution)/shard_map/ppermute | solution.py:22
  37.7 7.3 %copy-start.7 = (bf16[64,4096]{1,0:T(8,128)(2,1)}, bf16[64,4096]{1,0:T(8,128)(2,1)S(1)}, u32[]{:S(2)}) copy-start(bf16[64,4096]{1,0:T(8,128)(2,1)S(1)} %constant_dynamic-update-slice_fusion.basis_ref) | copy-start | bytes 1572868
  45.0 0.8 copy-start.4
  60.2 7.4 %collective-permute-start.2 = (f32[8,192,256]{2,1,0:T(8,128)}, f32[8,192,256]{2,1,0:T(8,128)S(1)}, u32[]{:S(2)}, u32[]{:S(2)}) collective-permute-start(f32[8,192,256]{2,1,0:T(8,128)} %get-tuple-element.8), channel_id=1, source_target_pairs={{0,1},{1,0},{2,3},{3,2},{4,5},{5,4},{6,7},{7,6},{8,9},{9,8},{10,11... | collective-permute-start | bytes 4718600 | tf_op jit(solution)/shard_map/ppermute | solution.py:22
  70.3 17.2 %all-to-all-start.2 = ((bf16[8,192,256]{2,1,0:T(8,128)(2,1)}), bf16[8,192,256]{2,1,0:T(8,128)(2,1)S(1)}, u32[]{:S(2)}, u32[]{:S(2)}) async-start(bf16[8,192,256]{2,1,0:T(8,128)(2,1)} %add_convert_fusion), calls=%async_computation.2 | async-start | bytes 1572864 | tf_op jit(solution)/shard_map/all_to_all | solution.py:26
  103.2 3.8 %copy-start.3 = (bf16[8,192,256]{2,1,0:T(8,128)(2,1)}, bf16[8,192,256]{2,1,0:T(8,128)(2,1)S(1)}, u32[]{:S(2)}) copy-start(bf16[8,192,256]{2,1,0:T(8,128)(2,1)S(1)} %all_to_all.35.near_ref) | copy-start | bytes 2359300
  103.2 3.8 %collective-permute-start.3 = (bf16[8,192,256]{2,1,0:T(8,128)(2,1)S(1)}, bf16[8,192,256]{2,1,0:T(8,128)(2,1)S(1)}, u32[]{:S(2)}, u32[]{:S(2)}) collective-permute-start(bf16[8,192,256]{2,1,0:T(8,128)(2,1)S(1)} %all_to_all.35.near_ref), channel_id=1, source_target_pairs={{0,1},{1,0},{2,3},{3,2},{4,5},{5,4},{6,7},{7,6},{8,9},{9,8},{10,11... | collective-permute-start | bytes 2359304 | tf_op jit(solution)/shard_map/ppermute | solution.py:22
  107.0 0.9 copy-start.9
  118.1 41.8 %all-to-all-start.4 = ((bf16[8,16,24,256]{3,2,1,0:T(8,128)(2,1)}), bf16[8,16,24,256]{3,2,1,0:T(8,128)(2,1)S(1)}, u32[]{:S(2)}, u32[]{:S(2)}) async-start(bf16[8,16,24,256]{3,2,1,0:T(8,128)(2,1)} %respond.1), calls=%async_computation.4 | async-start | bytes 3145728 | tf_op jit(solution)/shard_map/all_to_all | solution.py:26
  160.1 11.7 %copy-start.6 = (f32[256,256]{1,0:T(8,128)S(1)}, f32[256,256]{1,0:T(8,128)}, u32[]{:S(2)}) copy-start(f32[256,256]{1,0:T(8,128)} %param.10) | copy-start | bytes 786436
  160.4 5.1 %collective-permute-start.4 = (bf16[16,12,256]{2,0,1:T(8,128)(2,1)S(1)}, bf16[16,12,256]{2,0,1:T(8,128)(2,1)S(1)}, u32[]{:S(2)}, u32[]{:S(2)}) collective-permute-start(bf16[16,12,256]{2,0,1:T(8,128)(2,1)S(1)} %select_convert_fusion), channel_id=1, source_target_pairs={{0,16},{16,0},{1,17},{17,1},{2,18},{18,2},{3,19},{19,3},{4,20},{20... | collective-permute-start | bytes 294920 | tf_op jit(solution)/shard_map/ppermute | solution.py:22
  168.5 8.7 %all-to-all-start.5 = ((bf16[8,16,384]{2,1,0:T(8,128)(2,1)}), bf16[8,16,384]{2,1,0:T(8,128)(2,1)S(1)}, u32[]{:S(2)}, u32[]{:S(2)}) async-start(bf16[8,16,384]{2,1,0:T(8,128)(2,1)} %columns_kernel.1), calls=%async_computation.5 | async-start | bytes 196608 | tf_op jit(solution)/shard_map/all_to_all | solution.py:26
  177.2 7.7 %copy-start.5 = (bf16[8,16,384]{2,1,0:T(8,128)(2,1)}, bf16[8,16,384]{2,1,0:T(8,128)(2,1)S(1)}, u32[]{:S(2)}) copy-start(bf16[8,16,384]{2,1,0:T(8,128)(2,1)S(1)} %all-to-all-done.5.near_ref) | copy-start | bytes 294916
  177.2 7.7 %collective-permute-start.5 = (bf16[8,16,384]{2,1,0:T(8,128)(2,1)S(1)}, bf16[8,16,384]{2,1,0:T(8,128)(2,1)S(1)}, u32[]{:S(2)}, u32[]{:S(2)}) collective-permute-start(bf16[8,16,384]{2,1,0:T(8,128)(2,1)S(1)} %all-to-all-done.5.near_ref), channel_id=1, source_target_pairs={{0,1},{1,0},{2,3},{3,2},{4,5},{5,4},{6,7},{7,6},{8,9},{9,8},{10,11... | collective-permute-start | bytes 294920 | tf_op jit(solution)/shard_map/ppermute | solution.py:22
  184.9 0.6 copy-start.8

commit v2 on v1

v2 whole, which is shorter than its diff:
```python
import functools

import jax
import jax.numpy as jnp
from jax import lax
from jax.experimental import pallas as pl
from jax.experimental.pallas import tpu as pltpu
from jax.sharding import Mesh
from jax.sharding import PartitionSpec as P

SIDE = 256
Z, XH, Y, XL, CORE = "z", "x_hi", "y", "x_lo", "core"
CELL = (Y, XL, CORE)
ORB = (Z, XH)
CHIP = (Y, XL)
F32, BF16 = jnp.float32, jnp.bfloat16
HIGH = lax.Precision.HIGHEST
SWAP = ((0, 1), (1, 0))


def swapped(shard, axis):
    return lax.ppermute(shard, axis, SWAP)


def exchanged(parts, axes):
    return lax.all_to_all(parts, axes, split_axis=0, concat_axis=0, tiled=True)


def products(occ, basis, first, count):
    rows = [occ[first + n : first + n + 1, :] * basis for n in range(count)]
    return jnp.concatenate(rows, axis=0)


def project_kernel(occ_ref, basis_ref, pot_ref, *out_refs, group):
    blocks, count, width = occ_ref.shape
    for n in range(count // group):
        total = None
        for k in range(blocks):
            cut = slice(k * width, (k + 1) * width)
            pairs = products(occ_ref[k], basis_ref[:, cut], n * group, group)
            term = lax.dot_general(
                pot_ref[:, cut], pairs, (((1,), (1,)), ((), ())), preferred_element_type=F32
            )
            total = term if total is None else total + term
        first = 0
        for ref in out_refs:
            ref[n] = total[first : first + ref.shape[1]]
            first += ref.shape[1]


def project(occ, basis, pot, group, per_step, chunks):
    blocks, slots, width = occ.shape
    rows, points = basis.shape
    nv = pot.shape[0]
    out_count = per_step // group
    lanes = group * rows
    return pl.pallas_call(
        functools.partial(project_kernel, group=group),
        grid=(slots // per_step,),
        in_specs=[
            pl.BlockSpec((blocks, per_step, width), lambda t: (0, t, 0)),
            pl.BlockSpec((rows, points), lambda t: (0, 0)),
            pl.BlockSpec((nv, points), lambda t: (0, 0)),
        ],
        out_specs=[pl.BlockSpec((out_count, c, lanes), lambda t: (t, 0, 0)) for c in chunks],
        out_shape=[jax.ShapeDtypeStruct((slots // group, c, lanes), F32) for c in chunks],
        cost_estimate=pl.CostEstimate(
            flops=2 * slots * rows * points * nv, bytes_accessed=6_000_000, transcendentals=0
        ),
        name="project",
    )(occ, basis, pot)


def respond_kernel(far_occ, near_occ, basis_ref, far_ref, near_ref, sent_ref, kept_ref, *, group):
    total = None
    for occ_ref, ref in ((far_occ, far_ref), (near_occ, near_ref)):
        for b in range(ref.shape[0]):
            pairs = products(occ_ref[0], basis_ref[...], b * group, group)
            term = jnp.dot(ref[b], pairs, preferred_element_type=F32)
            total = term if total is None else total + term
    first = 0
    for ref in (sent_ref, kept_ref):
        owners, lines, per_owner, side = ref.shape
        for n in range(owners):
            for r in range(lines):
                piece = total[first : first + per_owner, r * side : (r + 1) * side]
                ref[n, r] = piece.astype(ref.dtype)
            first += per_owner


def respond(far_occ, near_occ, basis, far, near, group, owners):
    blocks, slots, width = far_occ.shape
    rows, points = basis.shape
    count, nv, lanes = far.shape
    lines = width // SIDE
    per_owner = nv // owners // 2
    dims = (owners, points // SIDE, per_owner, SIDE)
    occ_spec = pl.BlockSpec((1, slots, width), lambda k: (k, 0, 0))
    guess_spec = pl.BlockSpec((count, nv, lanes), lambda k: (0, 0, 0))
    out_spec = pl.BlockSpec((owners, lines, per_owner, SIDE), lambda k: (0, k, 0, 0))
    return pl.pallas_call(
        functools.partial(respond_kernel, group=group),
        grid=(blocks,),
        in_specs=[
            occ_spec,
            occ_spec,
            pl.BlockSpec((rows, width), lambda k: (0, k)),
            guess_spec,
            guess_spec,
        ],
        out_specs=[out_spec, out_spec],
        out_shape=[jax.ShapeDtypeStruct(dims, BF16), jax.ShapeDtypeStruct(dims, F32)],
        cost_estimate=pl.CostEstimate(
            flops=4 * slots * rows * points * nv, bytes_accessed=6_000_000, transcendentals=0
        ),
        name="respond",
    )(far_occ, near_occ, basis, far, near)


def columns_kernel(plane_ref, cols_ref, out_ref):
    count, lines, side = plane_ref.shape
    mixed = lax.dot_general(
        plane_ref[...].reshape(count * lines, side),
        cols_ref[...],
        (((1,), (1,)), ((), ())),
        precision=HIGH,
        preferred_element_type=F32,
    )
    out_ref[...] = mixed.reshape(count, lines, side).astype(out_ref.dtype)


def in_three(block):
    high = block.astype(BF16)
    rest = block - high.astype(F32)
    mid = rest.astype(BF16)
    low = (rest - mid.astype(F32)).astype(BF16)
    return high, mid, low


def rows_kernel(near_ref, far_ref, mix_near_ref, mix_far_ref, out_ref):
    chips, count, lines, side = near_ref.shape
    mixes = [jnp.concatenate(in_three(m[...]), axis=0) for m in (mix_near_ref, mix_far_ref)]
    for n in range(count):
        total = None
        for ref, mix in zip((near_ref, far_ref), mixes):
            block = jnp.concatenate([ref[k, n] for k in range(chips)], axis=0)
            term = jnp.dot(mix, block, preferred_element_type=F32)
            total = term if total is None else total + term
        out_ref[n] = total[:lines] + (total[lines : 2 * lines] + total[2 * lines :])


def small_call(kernel, out, *args):
    return pl.pallas_call(kernel, out_shape=out, name=kernel.__name__)(*args)


def body(potentials, orbitals, levels, occ_index, coul_rows, coul_cols):
    nv, points = potentials.shape
    mine = orbitals.shape[0]
    norb, nocc = levels.shape[0], occ_index.shape[0]
    nz, nx, ny, nl, nc = (lax.axis_size(a) for a in (Z, XH, Y, XL, CORE))
    z, xh, y, xl, core = (lax.axis_index(a) for a in (Z, XH, Y, XL, CORE))
    chips = ny * nl
    chip = y * nl + xl
    width = points // nz
    slots = nocc // nx
    half = slots // nc
    group = half // chips
    lines = points // SIDE
    volume = points * chips * nc
    per_owner = nv // (nz * nx)
    big = per_owner * 2 // 3
    sizes = (big, per_owner - big)

    partner = swapped(orbitals, XH)
    by_points = exchanged(jnp.moveaxis(orbitals.reshape(mine, nz, width), 1, 0), Z)
    by_points = by_points.reshape(nz * mine, width)
    held = jnp.arange(nz * mine, dtype=jnp.int32)
    held = (held // mine * nx + xh) * mine + held % mine

    def slots_of(side):
        parts = [
            lax.dynamic_slice_in_dim(occ_index, side * slots + c * half, half)
            for c in (1 - core, core)
        ]
        return jnp.concatenate(parts)

    def selected(wanted):
        chosen = (wanted[:, None] == held[None, :]).astype(BF16)
        return jnp.dot(chosen, by_points, preferred_element_type=F32).astype(BF16)

    occ_part = selected(slots_of(xh)) + swapped(selected(slots_of(1 - xh)), XH)

    def spread(part, axes, count):
        return exchanged(jnp.broadcast_to(part, (count, *part.shape)), axes)

    far_occ = spread(occ_part[:half], Z, nz)
    near_occ = spread(occ_part[half:], Z, nz)

    place = jnp.arange(nv, dtype=jnp.int32)
    sources, first = [], 0
    for size in sizes:
        n = jnp.arange(nx * nz * size, dtype=jnp.int32)
        side = (xh + 1 + n // (nz * size)) % nx
        owner = n // size % nz * nx + side
        sources.append(owner * per_owner + first + n % size)
        first += size
    order = (jnp.concatenate(sources)[:, None] == place[None, :]).astype(BF16)
    pot = jnp.dot(order, potentials, preferred_element_type=F32).astype(BF16)
    basis = jnp.concatenate([orbitals, partner], axis=0)

    labels = jnp.arange(norb, dtype=jnp.int32)
    empty = 1.0 - jnp.any(occ_index[:, None] == labels[None, :], axis=0).astype(F32)
    own_slots = lax.dynamic_slice_in_dim(
        occ_index, xh * slots + core * half + chip * group, group
    )
    own_levels = jnp.sum(
        jnp.where(own_slots[:, None] == labels[None, :], levels[None, :], 0.0), axis=1
    )

    def of_basis(values):
        starts = [(z * nx + side) * mine for side in (xh, 1 - xh)]
        return jnp.concatenate([lax.dynamic_slice_in_dim(values, s, mine) for s in starts])

    weight = -2.0 * of_basis(empty)[None, :] / (own_levels[:, None] + of_basis(levels)[None, :])
    weight = (weight / volume).reshape(1, group * nx * mine)

    my_rows = lax.dynamic_slice_in_dim(coul_rows, (chip * nc + core) * lines, lines)
    my_rows = my_rows.reshape(lines, chips, nc, lines)
    mixes = [
        lax.dynamic_index_in_dim(my_rows, c, 2, keepdims=False).reshape(lines, chips * lines)
        for c in (core, 1 - core)
    ]
    far_occ, pot, weight, mixes = lax.optimization_barrier((far_occ, pot, weight, mixes))

    chunk_rows = [nx * nz * size for size in sizes]
    per_step = min(half, 16)
    far = project(far_occ, basis, pot, group, per_step, chunk_rows)
    near = project(near_occ, basis, pot, group, per_step, chunk_rows)

    screened = []
    for far_part, near_part in zip(far, near):
        summed = (near_part + swapped(far_part, CORE)).astype(BF16)
        intersection = jnp.sum(exchanged(summed, CHIP).astype(F32), axis=0)
        guess = (intersection * weight).astype(BF16)
        near_guess = spread(guess, CHIP, chips)
        far_guess = swapped(near_guess, CORE)
        sent, kept = respond(far_occ, near_occ, basis, far_guess, near_guess, group, nz)
        part = (kept + swapped(sent, XH).astype(F32)).astype(BF16)
        plane = jnp.swapaxes(jnp.sum(exchanged(part, Z).astype(F32), axis=0), 0, 1)
        columns = small_call(
            columns_kernel, jax.ShapeDtypeStruct(plane.shape, BF16), plane, coul_cols
        )
        near_cols = spread(columns, CHIP, chips)
        far_cols = swapped(near_cols, CORE)
        out = jax.ShapeDtypeStruct(plane.shape, F32)
        screened.append(small_call(rows_kernel, out, near_cols, far_cols, *mixes))
    return jnp.concatenate(screened, axis=0)


def solution(mesh):
    torus = Mesh(mesh.devices.reshape(8, 2, 4, 2, 2), (Z, XH, Y, XL, CORE))
    return jax.shard_map(
        body,
        mesh=torus,
        in_specs=(P(None, CELL), P(ORB, CELL), P(), P(), P(), P()),
        out_specs=P(ORB, CELL, None),
        check_vma=False,
    )
```

time: 201 us -> 222 us (1.10)
  waiting for transfers between devices: 74.4 us -> 55.3 us
  starting transfers between devices: 43.8 us -> 60.4 us
  blocking collectives: 26.2 us -> 39.3 us
  Pallas kernels: 30.5 us -> 42 us
  local copies, waits for them, and re-layouts: 19.9 us -> 14 us
  other arithmetic: 4.28 us -> 6.56 us
    all_to_all x5 -> x8, waiting for transfers between devices: 63.6 us -> 40.6 us  [exchanged(): return lax.all_to_all(parts, axes, split_axis=0, concat_axis=0, tiled=True)]
    all_to_all x2 -> x3, blocking collectives: 26.2 us -> 39.3 us  [exchanged(): return lax.all_to_all(parts, axes, split_axis=0, concat_axis=0, tiled=True)]
    all_to_all x5 -> x8, starting transfers between devices: 24.6 us -> 35 us  [exchanged(): return lax.all_to_all(parts, axes, split_axis=0, concat_axis=0, tiled=True)]
    gather x6 -> x0, local copies, waits for them, and re-layouts: 9.25 us -> none  [the longest x1 1.95 us: body(): levels[other]]
    pallas_call x1 -> x2, Pallas kernels: 10.2 us -> 17.4 us  [respond(): pl.pallas_call(functools.partial(respond_kernel, group=group), grid=(bloc...]
    ppermute x6 -> x10, starting transfers between devices: 19.3 us -> 25.3 us  [swapped(): return lax.ppermute(shard, axis, SWAP)]
    ppermute x6 -> x10, waiting for transfers between devices: 10.8 us -> 14.7 us  [swapped(): return lax.ppermute(shard, axis, SWAP)]
    broadcast_in_dim x2 -> x6, local copies, waits for them, and re-layouts: 0.91 us -> 4.79 us  [spread(): return exchanged(jnp.broadcast_to(part, (count, *part.shape)), axes)]
  transfers between devices with their start and end apart: 11 -> 18, of which waited for: 10 -> 11; matrix products, arithmetic and copies ran while one was open for 8% -> 7% of each run, Pallas kernels for 0% -> 14%
where the time goes in v2:
time: 222 us; the launch traced here: 220 us
  starting transfers between devices  60.4 us (27%)
  waiting for transfers between devices  55.3 us (25%)
  Pallas kernels  42 us (19%)
  blocking collectives  39.3 us (18%)
  local copies, waits for them, and re-layouts  14 us (6%)
  other arithmetic  6.56 us (3%)
    all_to_all x8, waiting for transfers between devices, exchanged(): return lax.all_to_all(parts, axes, split_axis=0, concat_axis=0, tiled=True)  40.6 us
    all_to_all x3, blocking collectives, exchanged(): return lax.all_to_all(parts, axes, split_axis=0, concat_axis=0, tiled=True)  39.3 us
    all_to_all x8, starting transfers between devices, exchanged(): return lax.all_to_all(parts, axes, split_axis=0, concat_axis=0, tiled=True)  35 us
    ppermute x10, starting transfers between devices, swapped(): return lax.ppermute(shard, axis, SWAP)  25.3 us
    pallas_call x2, Pallas kernels, respond(): pl.pallas_call(functools.partial(respond_kernel, group=group), grid=(bloc...  17.4 us
    pallas_call x2, Pallas kernels, project(): pl.pallas_call(functools.partial(project_kernel, group=group), grid=(slot...  16.5 us
    ppermute x10, waiting for transfers between devices, swapped(): return lax.ppermute(shard, axis, SWAP)  14.7 us
    pallas_call x4, Pallas kernels, small_call(): return pl.pallas_call(kernel, out_shape=out, name=kernel.__name__)(*args)  8.03 us
  transfers between devices with their start and end apart: 18, of which 11 were waited for; matrix products, arithmetic and copies ran while one was open for 7% of the time, Pallas kernels for 14%

profile of v2, /device:TPU:1, one launch (start us, length us, event | category | flops | bytes accessed | tf_op | source)
XLA Modules:
  0.0 219.9 jit_solution(1025960377616324394)
XLA Ops:
  0.0 3.6 %collective-permute-start.1 = (bf16[32,4096]{1,0:T(8,128)(2,1)}, bf16[32,4096]{1,0:T(8,128)(2,1)S(1)}, u32[]{:S(2)}, u32[]{:S(2)}) collective-permute-start(bf16[32,4096]{1,0:T(8,128)(2,1)} %param.7), channel_id=1, source_target_pairs={{0,16},{16,0},{1,17},{17,1},{2,18},{18,2},{3,19},{19,3},{4,20},{20... | collective-permute-start | bytes 786440 | tf_op jit(solution)/shard_map/ppermute | solution.py:22
  5.5 8.2 %all-to-all-start = ((bf16[8,32,512]{2,1,0:T(8,128)(2,1)}), bf16[8,32,512]{2,1,0:T(8,128)(2,1)S(1)}, u32[]{:S(2)}, u32[]{:S(2)}) async-start(bf16[8,32,512]{2,1,0:T(8,128)(2,1)} %copy.11), calls=%async_computation | async-start | bytes 524288 | tf_op jit(solution)/shard_map/all_to_all | solution.py:26
  17.4 6.5 %all-to-all-done = bf16[8,32,512]{2,1,0:T(8,128)(2,1)S(1)} async-done(((bf16[8,32,512]{2,1,0:T(8,128)(2,1)}), bf16[8,32,512]{2,1,0:T(8,128)(2,1)S(1)}, u32[]{:S(2)}, u32[]{:S(2)}) %all-to-all-start) | async-done | bytes 262176 | tf_op jit(solution)/shard_map/all_to_all | solution.py:26
  24.6 4.2 %collective-permute-done = bf16[64,512]{1,0:T(8,128)(2,1)S(1)} collective-permute-done((bf16[64,512]{1,0:T(8,128)(2,1)S(1)}, bf16[64,512]{1,0:T(8,128)(2,1)S(1)}, u32[]{:S(2)}, u32[]{:S(2)}) %collective-permute-start) | collective-permute-done | bytes 65568 | tf_op jit(solution)/shard_map/ppermute | solution.py:22
  29.8 3.4 %all-to-all-start.1 = ((bf16[8,32,512]{2,1,0:T(8,128)(2,1)}), bf16[8,32,512]{2,1,0:T(8,128)(2,1)S(1)}, u32[]{:S(2)}, u32[]{:S(2)}) async-start(bf16[8,32,512]{2,1,0:T(8,128)(2,1)} %broadcast_in_dim.24), calls=%async_computation.1 | async-start | bytes 524288 | tf_op jit(solution)/shard_map/all_to_all | solution.py:26
  35.1 7.5 %all-to-all-done.1.occ_ref.far_occ = bf16[8,32,512]{2,1,0:T(8,128)(2,1)S(1)} async-done(((bf16[8,32,512]{2,1,0:T(8,128)(2,1)}), bf16[8,32,512]{2,1,0:T(8,128)(2,1)S(1)}, u32[]{:S(2)}, u32[]{:S(2)}) %all-to-all-start.1) | async-done | bytes 262176 | tf_op jit(solution)/shard_map/all_to_all | solution.py:26
  43.3 8.2 %project.3 = (f32[8,128,256]{2,1,0:T(8,128)}, f32[8,64,256]{2,1,0:T(8,128)}) custom-call(bf16[8,32,512]{2,1,0:T(8,128)(2,1)} %copy-done.10, bf16[64,4096]{1,0:T(8,128)(2,1)} %copy-done.12, bf16[192,4096]{1,0:T(8,128)(2,1)} %convolution_convert_fusion.pot_ref), custom_call_target="tpu_custom_call" | custom-call | flops 3221225472 | bytes 6000000 | tf_op jit(solution)/shard_map/project/pallas_call | solution.py:57
  51.5 4.8 %collective-permute-start.2 = (f32[8,128,256]{2,1,0:T(8,128)}, f32[8,128,256]{2,1,0:T(8,128)S(1)}, u32[]{:S(2)}, u32[]{:S(2)}) collective-permute-start(f32[8,128,256]{2,1,0:T(8,128)} %get-tuple-element.21), channel_id=1, source_target_pairs={{0,1},{1,0},{2,3},{3,2},{4,5},{5,4},{6,7},{7,6},{8,9},{9,8},{10,11... | collective-permute-start | bytes 3145736 | tf_op jit(solution)/shard_map/ppermute | solution.py:22
  56.4 15.5 %all_to_all.55.occ_ref.near_occ = bf16[8,32,512]{2,1,0:T(8,128)(2,1)} all-to-all(bf16[8,32,512]{2,1,0:T(8,128)(2,1)S(1)} %broadcast_in_dim.27), channel_id=1, replica_groups=mesh['z'=8,'x_hi'=2,'y'=4,'x_lo'=2,'core'=2] {'z'}, dimensions={0} | all-to-all | bytes 524288 | tf_op jit(solution)/shard_map/all_to_all | solution.py:26
  71.8 8.3 %project.2 = (f32[8,128,256]{2,1,0:T(8,128)}, f32[8,64,256]{2,1,0:T(8,128)}) custom-call(bf16[8,32,512]{2,1,0:T(8,128)(2,1)} %all_to_all.55.occ_ref.near_occ, bf16[64,4096]{1,0:T(8,128)(2,1)} %copy-done.12, bf16[192,4096]{1,0:T(8,128)(2,1)} %convolution_convert_fusion.pot_ref), custom_call_target="tpu_custom_call" | custom-call | flops 3221225472 | bytes 6000000 | tf_op jit(solution)/shard_map/project/pallas_call | solution.py:57
  81.4 13.3 %all_to_all.56 = bf16[8,128,256]{2,1,0:T(8,128)(2,1)S(1)} all-to-all(bf16[8,128,256]{2,1,0:T(8,128)(2,1)S(1)} %add_convert_fusion.1), channel_id=1, replica_groups=mesh['z'=8,'x_hi'=2,'y'=4,'x_lo'=2,'core'=2] {'y','x_lo'}, dimensions={0} | all-to-all | bytes 1048576 | tf_op jit(solution)/shard_map/all_to_all | solution.py:26
  95.7 3.5 %all-to-all-start.4 = ((bf16[8,128,256]{2,1,0:T(8,128)(2,1)}), bf16[8,128,256]{2,1,0:T(8,128)(2,1)S(1)}, u32[]{:S(2)}, u32[]{:S(2)}) async-start(bf16[8,128,256]{2,1,0:T(8,128)(2,1)} %broadcast_in_dim.48), calls=%async_computation.4 | async-start | bytes 1048576 | tf_op jit(solution)/shard_map/all_to_all | solution.py:26
  101.1 6.3 %all-to-all-done.4.near_ref = bf16[8,128,256]{2,1,0:T(8,128)(2,1)S(1)} async-done(((bf16[8,128,256]{2,1,0:T(8,128)(2,1)}), bf16[8,128,256]{2,1,0:T(8,128)(2,1)S(1)}, u32[]{:S(2)}, u32[]{:S(2)}) %all-to-all-start.4) | async-done | bytes 524320 | tf_op jit(solution)/shard_map/all_to_all | solution.py:26
  107.4 2.7 %collective-permute-start.3 = (bf16[8,128,256]{2,1,0:T(8,128)(2,1)S(1)}, bf16[8,128,256]{2,1,0:T(8,128)(2,1)}, u32[]{:S(2)}, u32[]{:S(2)}) collective-permute-start(bf16[8,128,256]{2,1,0:T(8,128)(2,1)S(1)} %all-to-all-done.4.near_ref), channel_id=1, source_target_pairs={{0,1},{1,0},{2,3},{3,2},{4,5},{5,4},{6,7},{7,6},{8,9},{9,8},{10,11... | collective-permute-start | bytes 1572872 | tf_op jit(solution)/shard_map/ppermute | solution.py:22
  110.9 3.4 %all-to-all-start.7 = ((bf16[8,64,256]{2,1,0:T(8,128)(2,1)}), bf16[8,64,256]{2,1,0:T(8,128)(2,1)S(1)}, u32[]{:S(2)}, u32[]{:S(2)}) async-start(bf16[8,64,256]{2,1,0:T(8,128)(2,1)} %add_convert_fusion.3), calls=%async_computation.7 | async-start | bytes 524288 | tf_op jit(solution)/shard_map/all_to_all | solution.py:26
  114.4 8.6 %respond.2 = (bf16[8,16,8,256]{3,2,1,0:T(8,128)(2,1)}, f32[8,16,8,256]{3,2,1,0:T(8,128)}) custom-call(bf16[8,32,512]{2,1,0:T(8,128)(2,1)} %copy-done.10, bf16[8,32,512]{2,1,0:T(8,128)(2,1)} %all_to_all.55.occ_ref.near_occ, bf16[64,4096]{1,0:T(8,128)(2,1)} %copy-done.12, bf16[8,128,256]{2,1,0:T(8,128)(2,1)} %collective-permute-done.3.far_ref, ...), custom_call_target="tpu_custom_call" | custom-call | flops 4294967296 | bytes 6000000 | tf_op jit(solution)/shard_map/respond/pallas_call | solution.py:101
  125.5 4.5 %all-to-all-start.8 = ((bf16[8,64,256]{2,1,0:T(8,128)(2,1)}), bf16[8,64,256]{2,1,0:T(8,128)(2,1)S(1)}, u32[]{:S(2)}, u32[]{:S(2)}) async-start(bf16[8,64,256]{2,1,0:T(8,128)(2,1)} %broadcast_in_dim.50), calls=%async_computation.8 | async-start | bytes 524288 | tf_op jit(solution)/shard_map/all_to_all | solution.py:26
  130.0 8.1 %collective-permute-done.4 = bf16[8,16,8,256]{3,2,1,0:T(8,128)(2,1)S(1)} collective-permute-done((bf16[8,16,8,256]{3,2,1,0:T(8,128)(2,1)}, bf16[8,16,8,256]{3,2,1,0:T(8,128)(2,1)S(1)}, u32[]{:S(2)}, u32[]{:S(2)}) %collective-permute-start.4) | collective-permute-done | bytes 524320 | tf_op jit(solution)/shard_map/ppermute | solution.py:22
  139.0 3.2 %all-to-all-done.8.near_ref = bf16[8,64,256]{2,1,0:T(8,128)(2,1)S(1)} async-done(((bf16[8,64,256]{2,1,0:T(8,128)(2,1)}), bf16[8,64,256]{2,1,0:T(8,128)(2,1)S(1)}, u32[]{:S(2)}, u32[]{:S(2)}) %all-to-all-start.8) | async-done | bytes 262176 | tf_op jit(solution)/shard_map/all_to_all | solution.py:26
  142.3 3.5 %all-to-all-start.5 = ((bf16[8,16,8,256]{3,2,1,0:T(8,128)(2,1)}), bf16[8,16,8,256]{3,2,1,0:T(8,128)(2,1)S(1)}, u32[]{:S(2)}, u32[]{:S(2)}) async-start(bf16[8,16,8,256]{3,2,1,0:T(8,128)(2,1)} %add_convert_fusion), calls=%async_computation.5 | async-start | bytes 1048576 | tf_op jit(solution)/shard_map/all_to_all | solution.py:26
  149.0 8.9 %respond.3 = (bf16[8,16,4,256]{3,2,1,0:T(4,128)(2,1)}, f32[8,16,4,256]{3,2,1,0:T(4,128)}) custom-call(bf16[8,32,512]{2,1,0:T(8,128)(2,1)} %copy-done.10, bf16[8,32,512]{2,1,0:T(8,128)(2,1)} %all_to_all.55.occ_ref.near_occ, bf16[64,4096]{1,0:T(8,128)(2,1)} %copy-done.12, bf16[8,64,256]{2,1,0:T(8,128)(2,1)} %copy-done.15, bf16[8,64,256]{2,1,0:T(8,128)(2,1)} %copy-done.11), custom_call_target="tpu_custom_call" | custom-call | flops 2147483648 | bytes 6000000 | tf_op jit(solution)/shard_map/respond/pallas_call | solution.py:101
  157.8 2.7 %collective-permute-start.8 = (bf16[8,16,4,256]{3,2,1,0:T(4,128)(2,1)}, bf16[8,16,4,256]{3,2,1,0:T(4,128)(2,1)S(1)}, u32[]{:S(2)}, u32[]{:S(2)}) collective-permute-start(bf16[8,16,4,256]{3,2,1,0:T(4,128)(2,1)} %get-tuple-element.30), channel_id=1, source_target_pairs={{0,16},{16,0},{1,17},{17,1},{2,18},{18,2},{3,19},{19,3},{4,20},{20... | collective-permute-start | bytes 786440 | tf_op jit(solution)/shard_map/ppermute | solution.py:22
  160.5 2.2 all-to-all-done.5
  163.5 2.1 columns_kernel.2
  167.2 3.5 %all-to-all-start.6 = ((bf16[8,8,16,256]{3,2,1,0:T(8,128)(2,1)}), bf16[8,8,16,256]{3,2,1,0:T(8,128)(2,1)S(1)}, u32[]{:S(2)}, u32[]{:S(2)}) async-start(bf16[8,8,16,256]{3,2,1,0:T(8,128)(2,1)} %broadcast_in_dim.49), calls=%async_computation.6 | async-start | bytes 1048576 | tf_op jit(solution)/shard_map/all_to_all | solution.py:26
  171.6 7.8 %all-to-all-done.6.near_ref = bf16[8,8,16,256]{3,2,1,0:T(8,128)(2,1)S(1)} async-done(((bf16[8,8,16,256]{3,2,1,0:T(8,128)(2,1)}), bf16[8,8,16,256]{3,2,1,0:T(8,128)(2,1)S(1)}, u32[]{:S(2)}, u32[]{:S(2)}) %all-to-all-start.6) | async-done | bytes 524320 | tf_op jit(solution)/shard_map/all_to_all | solution.py:26
  179.4 5.1 %all-to-all-start.9 = ((bf16[8,16,4,256]{3,2,1,0:T(4,128)(2,1)}), bf16[8,16,4,256]{3,2,1,0:T(4,128)(2,1)S(1)}, u32[]{:S(2)}, u32[]{:S(2)}) async-start(bf16[8,16,4,256]{3,2,1,0:T(4,128)(2,1)} %add_convert_fusion.2), calls=%async_computation.9 | async-start | bytes 524288 | tf_op jit(solution)/shard_map/all_to_all | solution.py:26
  184.5 2.1 collective-permute-start.5
  186.6 7.1 %all-to-all-done.9 = bf16[8,16,4,256]{3,2,1,0:T(4,128)(2,1)S(1)} async-done(((bf16[8,16,4,256]{3,2,1,0:T(4,128)(2,1)}), bf16[8,16,4,256]{3,2,1,0:T(4,128)(2,1)S(1)}, u32[]{:S(2)}, u32[]{:S(2)}) %all-to-all-start.9) | async-done | bytes 262176 | tf_op jit(solution)/shard_map/all_to_all | solution.py:26
  197.2 10.5 %all_to_all.57.near_ref = bf16[8,4,16,256]{3,2,1,0:T(8,128)(2,1)S(1)} all-to-all(bf16[8,4,16,256]{3,2,1,0:T(8,128)(2,1)S(1)} %broadcast_in_dim.51), channel_id=1, replica_groups=mesh['z'=8,'x_hi'=2,'y'=4,'x_lo'=2,'core'=2] {'y','x_lo'}, dimensions={0} | all-to-all | bytes 524288 | tf_op jit(solution)/shard_map/all_to_all | solution.py:26
  207.7 3.9 %collective-permute-start.9 = (bf16[8,4,16,256]{3,2,1,0:T(8,128)(2,1)S(1)}, bf16[8,4,16,256]{3,2,1,0:T(8,128)(2,1)S(1)}, u32[]{:S(2)}, u32[]{:S(2)}) collective-permute-start(bf16[8,4,16,256]{3,2,1,0:T(8,128)(2,1)S(1)} %all_to_all.57.near_ref), channel_id=1, source_target_pairs={{0,1},{1,0},{2,3},{3,2},{4,5},{5,4},{6,7},{7,6},{8,9},{9,8},{10,11... | collective-permute-start | bytes 786440 | tf_op jit(solution)/shard_map/ppermute | solution.py:22
  216.2 2.1 rows_kernel.2
  (95 shorter events, 34.4 us)
Async XLA Ops:
  0.0 15.1 %copy-start = (bf16[192,4096]{1,0:T(8,128)(2,1)S(1)}, bf16[192,4096]{1,0:T(8,128)(2,1)}, u32[]{:S(2)}) copy-start(bf16[192,4096]{1,0:T(8,128)(2,1)} %param.6) | copy-start | bytes 4718596
  0.0 13.8 %copy-start.13 = (s32[128]{0:T(128)S(1)}, s32[128]{0:T(128)}, u32[]{:S(2)}) copy-start(s32[128]{0:T(128)} %param.9) | copy-start | bytes 1540
  0.0 14.0 %copy-start.14 = (f32[512]{0:T(512)S(1)}, f32[512]{0:T(512)}, u32[]{:S(2)}) copy-start(f32[512]{0:T(512)} %param.8) | copy-start | bytes 6148
  0.0 35.1 %collective-permute-start.1 = (bf16[32,4096]{1,0:T(8,128)(2,1)}, bf16[32,4096]{1,0:T(8,128)(2,1)S(1)}, u32[]{:S(2)}, u32[]{:S(2)}) collective-permute-start(bf16[32,4096]{1,0:T(8,128)(2,1)} %param.7), channel_id=1, source_target_pairs={{0,16},{16,0},{1,17},{17,1},{2,18},{18,2},{3,19},{19,3},{4,20},{20... | collective-permute-start | bytes 786440 | tf_op jit(solution)/shard_map/ppermute | solution.py:22
  5.5 18.4 %all-to-all-start = ((bf16[8,32,512]{2,1,0:T(8,128)(2,1)}), bf16[8,32,512]{2,1,0:T(8,128)(2,1)S(1)}, u32[]{:S(2)}, u32[]{:S(2)}) async-start(bf16[8,32,512]{2,1,0:T(8,128)(2,1)} %copy.11), calls=%async_computation | async-start | bytes 524288 | tf_op jit(solution)/shard_map/all_to_all | solution.py:26
  15.1 2.3 %copy-start.4 = (bf16[32,4096]{1,0:T(8,128)(2,1)S(1)}, bf16[32,4096]{1,0:T(8,128)(2,1)}, u32[]{:S(2)}) copy-start(bf16[32,4096]{1,0:T(8,128)(2,1)} %param.7) | copy-start | bytes 786436
  24.2 4.7 %collective-permute-start = (bf16[64,512]{1,0:T(8,128)(2,1)S(1)}, bf16[64,512]{1,0:T(8,128)(2,1)S(1)}, u32[]{:S(2)}, u32[]{:S(2)}) collective-permute-start(bf16[64,512]{1,0:T(8,128)(2,1)S(1)} %convolution_convert_fusion.1), channel_id=1, source_target_pairs={{0,16},{16,0},{1,17},{17,1},{2,18},{18,2},{3,19},{19,3},{4,20},{20... | collective-permute-start | bytes 196616 | tf_op jit(solution)/shard_map/ppermute | solution.py:22
  29.8 12.8 %all-to-all-start.1 = ((bf16[8,32,512]{2,1,0:T(8,128)(2,1)}), bf16[8,32,512]{2,1,0:T(8,128)(2,1)S(1)}, u32[]{:S(2)}, u32[]{:S(2)}) async-start(bf16[8,32,512]{2,1,0:T(8,128)(2,1)} %broadcast_in_dim.24), calls=%async_computation.1 | async-start | bytes 524288 | tf_op jit(solution)/shard_map/all_to_all | solution.py:26
  35.1 7.5 %copy-start.12 = (bf16[64,4096]{1,0:T(8,128)(2,1)}, bf16[64,4096]{1,0:T(8,128)(2,1)S(1)}, u32[]{:S(2)}) copy-start(bf16[64,4096]{1,0:T(8,128)(2,1)S(1)} %constant_dynamic-update-slice_fusion.basis_ref) | copy-start | bytes 1572868
  42.6 0.7 copy-start.10
  51.5 28.5 %collective-permute-start.2 = (f32[8,128,256]{2,1,0:T(8,128)}, f32[8,128,256]{2,1,0:T(8,128)S(1)}, u32[]{:S(2)}, u32[]{:S(2)}) collective-permute-start(f32[8,128,256]{2,1,0:T(8,128)} %get-tuple-element.21), channel_id=1, source_target_pairs={{0,1},{1,0},{2,3},{3,2},{4,5},{5,4},{6,7},{7,6},{8,9},{9,8},{10,11... | collective-permute-start | bytes 3145736 | tf_op jit(solution)/shard_map/ppermute | solution.py:22
  81.4 28.8 %copy-start.6 = (f32[8,64,256]{2,1,0:T(8,128)S(1)}, f32[8,64,256]{2,1,0:T(8,128)}, u32[]{:S(2)}) copy-start(f32[8,64,256]{2,1,0:T(8,128)} %get-tuple-element.27) | copy-start | bytes 1572868
  95.7 11.7 %all-to-all-start.4 = ((bf16[8,128,256]{2,1,0:T(8,128)(2,1)}), bf16[8,128,256]{2,1,0:T(8,128)(2,1)S(1)}, u32[]{:S(2)}, u32[]{:S(2)}) async-start(bf16[8,128,256]{2,1,0:T(8,128)(2,1)} %broadcast_in_dim.48), calls=%async_computation.4 | async-start | bytes 1048576 | tf_op jit(solution)/shard_map/all_to_all | solution.py:26
  99.2 11.0 %collective-permute-start.6 = (f32[8,64,256]{2,1,0:T(8,128)}, f32[8,64,256]{2,1,0:T(8,128)S(1)}, u32[]{:S(2)}, u32[]{:S(2)}) collective-permute-start(f32[8,64,256]{2,1,0:T(8,128)} %get-tuple-element.28), channel_id=1, source_target_pairs={{0,1},{1,0},{2,3},{3,2},{4,5},{5,4},{6,7},{7,6},{8,9},{9,8},{10,11... | collective-permute-start | bytes 1572872 | tf_op jit(solution)/shard_map/ppermute | solution.py:22
  107.4 6.9 %copy-start.7 = (bf16[8,128,256]{2,1,0:T(8,128)(2,1)}, bf16[8,128,256]{2,1,0:T(8,128)(2,1)S(1)}, u32[]{:S(2)}) copy-start(bf16[8,128,256]{2,1,0:T(8,128)(2,1)S(1)} %all-to-all-done.4.near_ref) | copy-start | bytes 1572868
  107.4 6.9 %collective-permute-start.3 = (bf16[8,128,256]{2,1,0:T(8,128)(2,1)S(1)}, bf16[8,128,256]{2,1,0:T(8,128)(2,1)}, u32[]{:S(2)}, u32[]{:S(2)}) collective-permute-start(bf16[8,128,256]{2,1,0:T(8,128)(2,1)S(1)} %all-to-all-done.4.near_ref), channel_id=1, source_target_pairs={{0,1},{1,0},{2,3},{3,2},{4,5},{5,4},{6,7},{7,6},{8,9},{9,8},{10,11... | collective-permute-start | bytes 1572872 | tf_op jit(solution)/shard_map/ppermute | solution.py:22
  110.9 13.8 %all-to-all-start.7 = ((bf16[8,64,256]{2,1,0:T(8,128)(2,1)}), bf16[8,64,256]{2,1,0:T(8,128)(2,1)S(1)}, u32[]{:S(2)}, u32[]{:S(2)}) async-start(bf16[8,64,256]{2,1,0:T(8,128)(2,1)} %add_convert_fusion.3), calls=%async_computation.7 | async-start | bytes 524288 | tf_op jit(solution)/shard_map/all_to_all | solution.py:26
  122.9 15.1 %copy-start.3 = (f32[8,16,8,256]{3,2,1,0:T(8,128)S(1)}, f32[8,16,8,256]{3,2,1,0:T(8,128)}, u32[]{:S(2)}) copy-start(f32[8,16,8,256]{3,2,1,0:T(8,128)} %get-tuple-element.23) | copy-start | bytes 3145732
  123.0 15.1 %collective-permute-start.4 = (bf16[8,16,8,256]{3,2,1,0:T(8,128)(2,1)}, bf16[8,16,8,256]{3,2,1,0:T(8,128)(2,1)S(1)}, u32[]{:S(2)}, u32[]{:S(2)}) collective-permute-start(bf16[8,16,8,256]{3,2,1,0:T(8,128)(2,1)} %get-tuple-element.24), channel_id=1, source_target_pairs={{0,16},{16,0},{1,17},{17,1},{2,18},{18,2},{3,19},{19,3},{4,20},{20... | collective-permute-start | bytes 1572872 | tf_op jit(solution)/shard_map/ppermute | solution.py:22
  125.5 16.8 %all-to-all-start.8 = ((bf16[8,64,256]{2,1,0:T(8,128)(2,1)}), bf16[8,64,256]{2,1,0:T(8,128)(2,1)S(1)}, u32[]{:S(2)}, u32[]{:S(2)}) async-start(bf16[8,64,256]{2,1,0:T(8,128)(2,1)} %broadcast_in_dim.50), calls=%async_computation.8 | async-start | bytes 524288 | tf_op jit(solution)/shard_map/all_to_all | solution.py:26
  142.3 6.0 %copy-start.11 = (bf16[8,64,256]{2,1,0:T(8,128)(2,1)}, bf16[8,64,256]{2,1,0:T(8,128)(2,1)S(1)}, u32[]{:S(2)}) copy-start(bf16[8,64,256]{2,1,0:T(8,128)(2,1)S(1)} %all-to-all-done.8.near_ref) | copy-start | bytes 786436
  142.3 20.4 %all-to-all-start.5 = ((bf16[8,16,8,256]{3,2,1,0:T(8,128)(2,1)}), bf16[8,16,8,256]{3,2,1,0:T(8,128)(2,1)S(1)}, u32[]{:S(2)}, u32[]{:S(2)}) async-start(bf16[8,16,8,256]{3,2,1,0:T(8,128)(2,1)} %add_convert_fusion), calls=%async_computation.5 | async-start | bytes 1048576 | tf_op jit(solution)/shard_map/all_to_all | solution.py:26
  145.8 2.5 %collective-permute-start.7 = (bf16[8,64,256]{2,1,0:T(8,128)(2,1)S(1)}, bf16[8,64,256]{2,1,0:T(8,128)(2,1)S(1)}, u32[]{:S(2)}, u32[]{:S(2)}) collective-permute-start(bf16[8,64,256]{2,1,0:T(8,128)(2,1)S(1)} %all-to-all-done.8.near_ref), channel_id=1, source_target_pairs={{0,1},{1,0},{2,3},{3,2},{4,5},{5,4},{6,7},{7,6},{8,9},{9,8},{10,11... | collective-permute-start | bytes 786440 | tf_op jit(solution)/shard_map/ppermute | solution.py:22
  157.8 12.9 %copy-start.8 = (f32[8,16,4,256]{3,2,1,0:T(4,128)S(1)}, f32[8,16,4,256]{3,2,1,0:T(4,128)}, u32[]{:S(2)}) copy-start(f32[8,16,4,256]{3,2,1,0:T(4,128)} %get-tuple-element.29) | copy-start | bytes 1572868
  157.8 12.9 %collective-permute-start.8 = (bf16[8,16,4,256]{3,2,1,0:T(4,128)(2,1)}, bf16[8,16,4,256]{3,2,1,0:T(4,128)(2,1)S(1)}, u32[]{:S(2)}, u32[]{:S(2)}) collective-permute-start(bf16[8,16,4,256]{3,2,1,0:T(4,128)(2,1)} %get-tuple-element.30), channel_id=1, source_target_pairs={{0,16},{16,0},{1,17},{17,1},{2,18},{18,2},{3,19},{19,3},{4,20},{20... | collective-permute-start | bytes 786440 | tf_op jit(solution)/shard_map/ppermute | solution.py:22
  167.2 12.2 %all-to-all-start.6 = ((bf16[8,8,16,256]{3,2,1,0:T(8,128)(2,1)}), bf16[8,8,16,256]{3,2,1,0:T(8,128)(2,1)S(1)}, u32[]{:S(2)}, u32[]{:S(2)}) async-start(bf16[8,8,16,256]{3,2,1,0:T(8,128)(2,1)} %broadcast_in_dim.49), calls=%async_computation.6 | async-start | bytes 1048576 | tf_op jit(solution)/shard_map/all_to_all | solution.py:26
  179.4 36.0 %copy-start.1 = (bf16[8,8,16,256]{3,2,1,0:T(8,128)(2,1)}, bf16[8,8,16,256]{3,2,1,0:T(8,128)(2,1)S(1)}, u32[]{:S(2)}) copy-start(bf16[8,8,16,256]{3,2,1,0:T(8,128)(2,1)S(1)} %all-to-all-done.6.near_ref) | copy-start | bytes 1572868
  179.4 14.3 %all-to-all-start.9 = ((bf16[8,16,4,256]{3,2,1,0:T(4,128)(2,1)}), bf16[8,16,4,256]{3,2,1,0:T(4,128)(2,1)S(1)}, u32[]{:S(2)}, u32[]{:S(2)}) async-start(bf16[8,16,4,256]{3,2,1,0:T(4,128)(2,1)} %add_convert_fusion.2), calls=%async_computation.9 | async-start | bytes 524288 | tf_op jit(solution)/shard_map/all_to_all | solution.py:26
  184.5 30.9 %collective-permute-start.5 = (bf16[8,8,16,256]{3,2,1,0:T(8,128)(2,1)S(1)}, bf16[8,8,16,256]{3,2,1,0:T(8,128)(2,1)S(1)}, u32[]{:S(2)}, u32[]{:S(2)}) collective-permute-start(bf16[8,8,16,256]{3,2,1,0:T(8,128)(2,1)S(1)} %all-to-all-done.6.near_ref), channel_id=1, source_target_pairs={{0,1},{1,0},{2,3},{3,2},{4,5},{5,4},{6,7},{7,6},{8,9},{9,8},{10,11... | collective-permute-start | bytes 1572872 | tf_op jit(solution)/shard_map/ppermute | solution.py:22
  207.7 5.1 %copy-start.2 = (bf16[8,4,16,256]{3,2,1,0:T(8,128)(2,1)}, bf16[8,4,16,256]{3,2,1,0:T(8,128)(2,1)S(1)}, u32[]{:S(2)}) copy-start(bf16[8,4,16,256]{3,2,1,0:T(8,128)(2,1)S(1)} %all_to_all.57.near_ref) | copy-start | bytes 786436
  207.7 5.1 %collective-permute-start.9 = (bf16[8,4,16,256]{3,2,1,0:T(8,128)(2,1)S(1)}, bf16[8,4,16,256]{3,2,1,0:T(8,128)(2,1)S(1)}, u32[]{:S(2)}, u32[]{:S(2)}) collective-permute-start(bf16[8,4,16,256]{3,2,1,0:T(8,128)(2,1)S(1)} %all_to_all.57.near_ref), channel_id=1, source_target_pairs={{0,1},{1,0},{2,3},{3,2},{4,5},{5,4},{6,7},{7,6},{8,9},{9,8},{10,11... | collective-permute-start | bytes 786440 | tf_op jit(solution)/shard_map/ppermute | solution.py:22
  215.4 0.8 copy-start.5
  (2 other events, 1.4 us)

commit v3 on v2

v3 whole, which is shorter than its diff:
```python
import functools

import jax
import jax.numpy as jnp
from jax import lax
from jax.experimental import pallas as pl
from jax.experimental.pallas import tpu as pltpu
from jax.sharding import Mesh
from jax.sharding import PartitionSpec as P

SIDE = 256
Z, XH, Y, XL, CORE = "z", "x_hi", "y", "x_lo", "core"
CELL = (Y, XL, CORE)
ORB = (Z, XH)
CHIP = (Y, XL)
F32, BF16 = jnp.float32, jnp.bfloat16
HIGH = lax.Precision.HIGHEST
SWAP = ((0, 1), (1, 0))
ROOM = pltpu.CompilerParams(vmem_limit_bytes=32 * 2**20)


def swapped(shard, axis):
    return lax.ppermute(shard, axis, SWAP)


def exchanged(parts, axes):
    return lax.all_to_all(parts, axes, split_axis=0, concat_axis=0, tiled=True)


def products(occ, basis, first, count):
    rows = [occ[first + n : first + n + 1, :] * basis for n in range(count)]
    return jnp.concatenate(rows, axis=0)


def project_kernel(occ_ref, basis_ref, pot_ref, far_ref, near_ref, *, group):
    step, half = pl.program_id(0), pl.num_programs(0) // 2
    blocks, count, width = occ_ref.shape
    parts = []
    for first in range(0, count, group):
        total = None
        for k in range(blocks):
            cut = slice(k * width, (k + 1) * width)
            pairs = products(occ_ref[k], basis_ref[:, cut], first, group)
            term = lax.dot_general(
                pot_ref[:, cut], pairs, (((1,), (1,)), ((), ())), preferred_element_type=F32
            )
            total = term if total is None else total + term
        parts.append(total)

    @pl.when(step < half)
    def _():
        for n, total in enumerate(parts):
            far_ref[n] = total

    @pl.when(step >= half)
    def _():
        for n, total in enumerate(parts):
            near_ref[n] = total


def project(occ, basis, pot, group, per_step):
    blocks, slots, width = occ.shape
    rows, points = basis.shape
    nv = pot.shape[0]
    steps = slots // per_step
    half = steps // 2
    out_count = per_step // group
    lanes = group * rows
    out = jax.ShapeDtypeStruct((slots // 2 // group, nv, lanes), F32)
    return pl.pallas_call(
        functools.partial(project_kernel, group=group),
        grid=(steps,),
        in_specs=[
            pl.BlockSpec((blocks, per_step, width), lambda t: (0, t, 0)),
            pl.BlockSpec((rows, points), lambda t: (0, 0)),
            pl.BlockSpec((nv, points), lambda t: (0, 0)),
        ],
        out_specs=[
            pl.BlockSpec((out_count, nv, lanes), lambda t: (jnp.minimum(t, half - 1), 0, 0)),
            pl.BlockSpec((out_count, nv, lanes), lambda t: (jnp.maximum(t - half, 0), 0, 0)),
        ],
        out_shape=[out, out],
        cost_estimate=pl.CostEstimate(
            flops=2 * slots * rows * points * nv, bytes_accessed=10_000_000, transcendentals=0
        ),
        compiler_params=ROOM,
        name="project",
    )(occ, basis, pot)


def respond_kernel(own_occ, other_occ, basis_ref, far_ref, near_ref, out_ref, *, group):
    blocks = far_ref.shape[0]
    total = None
    for p, occ_ref in enumerate((own_occ, other_occ)):
        for h, ref in enumerate((far_ref, near_ref)):
            for b in range(blocks):
                pairs = products(occ_ref[0], basis_ref[...], (h * blocks + b) * group, group)
                term = jnp.dot(ref[b, p], pairs, preferred_element_type=F32)
                total = term if total is None else total + term
    owners, count, side = out_ref.shape
    per_owner = total.shape[0] // owners
    for n in range(owners):
        rows = total[n * per_owner : (n + 1) * per_owner]
        lines = [rows[:, r * side : (r + 1) * side] for r in range(count // per_owner)]
        out_ref[n] = jnp.concatenate(lines, axis=0).astype(out_ref.dtype)


def respond(own_occ, other_occ, basis, far, near, group, owners):
    blocks, slots, width = own_occ.shape
    rows, points = basis.shape
    nv = far.shape[2]
    occ_spec = pl.BlockSpec((1, slots, width), lambda k: (k, 0, 0))
    guess_spec = pl.BlockSpec(far.shape, lambda k: (0, 0, 0, 0))
    lines = nv // owners * (width // SIDE)
    return pl.pallas_call(
        functools.partial(respond_kernel, group=group),
        grid=(blocks,),
        in_specs=[
            occ_spec,
            occ_spec,
            pl.BlockSpec((rows, width), lambda k: (0, k)),
            guess_spec,
            guess_spec,
        ],
        out_specs=pl.BlockSpec((owners, lines, SIDE), lambda k: (0, k, 0)),
        out_shape=jax.ShapeDtypeStruct((owners, blocks * lines, SIDE), BF16),
        cost_estimate=pl.CostEstimate(
            flops=4 * slots * rows * points * nv, bytes_accessed=6_000_000, transcendentals=0
        ),
        compiler_params=ROOM,
        name="respond",
    )(own_occ, other_occ, basis, far, near)


def columns_kernel(parts_ref, cols_ref, out_ref):
    sources, size, side = parts_ref.shape
    copies, count, lines, _ = out_ref.shape
    plane = parts_ref[0].astype(F32)
    for s in range(1, sources):
        plane = plane + parts_ref[s].astype(F32)
    mixed = lax.dot_general(
        plane, cols_ref[...], (((1,), (1,)), ((), ())), precision=HIGH, preferred_element_type=F32
    ).astype(BF16)
    row = lax.broadcasted_iota(jnp.int32, (size, size), 0)
    column = lax.broadcasted_iota(jnp.int32, (size, size), 1)
    source = row % lines * count + row // lines
    swap = jnp.where(source == column, 1.0, 0.0).astype(BF16)
    block = jnp.dot(swap, mixed, preferred_element_type=F32).astype(BF16)
    block = block.reshape(count, lines, side)
    for n in range(copies):
        out_ref[n] = block


def in_three(block):
    high = block.astype(BF16)
    rest = block - high.astype(F32)
    mid = rest.astype(BF16)
    low = (rest - mid.astype(F32)).astype(BF16)
    return high, mid, low


def rows_kernel(near_ref, far_ref, mix_near_ref, mix_far_ref, out_ref):
    chips, count, lines, _ = near_ref.shape
    mixes = [jnp.concatenate(in_three(m[...]), axis=0) for m in (mix_near_ref, mix_far_ref)]
    for n in range(count):
        total = None
        for ref, mix in zip((near_ref, far_ref), mixes):
            block = jnp.concatenate([ref[k, n] for k in range(chips)], axis=0)
            term = jnp.dot(mix, block, preferred_element_type=F32)
            total = term if total is None else total + term
        out_ref[n] = total[:lines] + (total[lines : 2 * lines] + total[2 * lines :])


def small_call(kernel, out, *args):
    return pl.pallas_call(kernel, out_shape=out, compiler_params=ROOM)(*args)


def body(potentials, orbitals, levels, occ_index, coul_rows, coul_cols):
    nv, points = potentials.shape
    mine = orbitals.shape[0]
    norb, nocc = levels.shape[0], occ_index.shape[0]
    nz, nx, ny, nl, nc = (lax.axis_size(a) for a in (Z, XH, Y, XL, CORE))
    z, xh, y, xl, core = (lax.axis_index(a) for a in (Z, XH, Y, XL, CORE))
    chips = ny * nl
    chip = y * nl + xl
    width = points // nz
    slots = nocc // nx
    half = slots // nc
    group = half // chips
    lines = points // SIDE
    volume = points * chips * nc
    per_owner = nv // (nz * nx)

    partner = swapped(orbitals, XH)
    by_points = exchanged(jnp.moveaxis(orbitals.reshape(mine, nz, width), 1, 0), Z)
    by_points = by_points.reshape(nz * mine, width)
    held = jnp.arange(nz * mine, dtype=jnp.int32)
    held = (held // mine * nx + xh) * mine + held % mine

    def slots_of(side):
        parts = [
            lax.dynamic_slice_in_dim(occ_index, side * slots + c * half, half)
            for c in (1 - core, core)
        ]
        return jnp.concatenate(parts)

    def selected(wanted):
        chosen = (wanted[:, None] == held[None, :]).astype(BF16)
        return jnp.dot(chosen, by_points, preferred_element_type=F32).astype(BF16)

    def spread(part, axes, count):
        return exchanged(jnp.broadcast_to(part, (count, *part.shape)), axes)

    occ_part = selected(slots_of(xh)) + swapped(selected(slots_of(1 - xh)), XH)
    occ = spread(occ_part, Z, nz)

    place = jnp.arange(nv, dtype=jnp.int32)
    side = (xh + 1 + place // (nz * per_owner)) % nx
    source = (place // per_owner % nz * nx + side) * per_owner + place % per_owner
    order = (source[:, None] == place[None, :]).astype(BF16)
    pot = jnp.dot(order, potentials, preferred_element_type=F32).astype(BF16)
    first = jnp.where(xh == 0, orbitals, partner)
    second = jnp.where(xh == 0, partner, orbitals)
    basis = jnp.concatenate([first, second], axis=0)

    labels = jnp.arange(norb, dtype=jnp.int32)
    empty = 1.0 - jnp.any(occ_index[:, None] == labels[None, :], axis=0).astype(F32)
    own_slots = lax.dynamic_slice_in_dim(
        occ_index, xh * slots + core * half + chip * group, group
    )
    own_levels = jnp.sum(
        jnp.where(own_slots[:, None] == labels[None, :], levels[None, :], 0.0), axis=1
    )

    def of_basis(values):
        return lax.dynamic_slice_in_dim(values, z * nx * mine, nx * mine)

    weight = -2.0 * of_basis(empty)[None, :] / (own_levels[:, None] + of_basis(levels)[None, :])
    weight = (weight / volume).reshape(1, group * nx * mine)

    my_rows = lax.dynamic_slice_in_dim(coul_rows, (chip * nc + core) * lines, lines)
    my_rows = my_rows.reshape(lines, chips, nc, lines)
    mixes = [
        lax.dynamic_index_in_dim(my_rows, c, 2, keepdims=False).reshape(lines, chips * lines)
        for c in (core, 1 - core)
    ]
    occ, pot, weight, mixes = lax.optimization_barrier((occ, pot, weight, mixes))

    other_occ = swapped(occ, XH)
    far, near = project(occ, basis, pot, group, 16)
    near, other_occ = lax.optimization_barrier((near, other_occ))
    summed = (near + swapped(far, CORE)).astype(BF16)
    intersection = jnp.sum(exchanged(summed, CHIP).astype(F32), axis=0)
    guess = (intersection * weight).astype(BF16)

    given, kept = guess[: nv // nx], guess[nv // nx :]
    guesses = jnp.stack([kept, swapped(given, XH)])
    near_guess = spread(guesses, CHIP, chips)
    far_guess = swapped(near_guess, CORE)
    response = respond(occ, other_occ, basis, far_guess, near_guess, group, nz)

    out = jax.ShapeDtypeStruct((chips, per_owner, lines, SIDE), BF16)
    columns = small_call(columns_kernel, out, exchanged(response, Z), coul_cols)
    near_cols = exchanged(columns, CHIP)
    far_cols = swapped(near_cols, CORE)
    out = jax.ShapeDtypeStruct((per_owner, lines, SIDE), F32)
    return small_call(rows_kernel, out, near_cols, far_cols, *mixes)


def solution(mesh):
    torus = Mesh(mesh.devices.reshape(8, 2, 4, 2, 2), (Z, XH, Y, XL, CORE))
    return jax.shard_map(
        body,
        mesh=torus,
        in_specs=(P(None, CELL), P(ORB, CELL), P(), P(), P(), P()),
        out_specs=P(ORB, CELL, None),
        check_vma=False,
    )
```

time: 222 us -> 183 us (0.82)
  blocking collectives: 39.3 us -> 70 us
  starting transfers between devices: 60.4 us -> 31.4 us
  waiting for transfers between devices: 55.3 us -> 38.8 us
  Pallas kernels: 42 us -> 26.9 us
  local copies, waits for them, and re-layouts: 14 us -> 8.54 us
  other arithmetic: 6.56 us -> 3.49 us
    all_to_all x3 -> x4, blocking collectives: 39.3 us -> 70 us  [exchanged(): return lax.all_to_all(parts, axes, split_axis=0, concat_axis=0, tiled=True)]
    all_to_all x8 -> x2, starting transfers between devices: 35 us -> 12.3 us  [exchanged(): return lax.all_to_all(parts, axes, split_axis=0, concat_axis=0, tiled=True)]
    all_to_all x8 -> x2, waiting for transfers between devices: 40.6 us -> 20.1 us  [exchanged(): return lax.all_to_all(parts, axes, split_axis=0, concat_axis=0, tiled=True)]
    pallas_call x6 -> x3, Pallas kernels: 24.5 us -> 14.2 us  [the longest x1 12.5 us: project(): pl.pallas_call(functools.partial(project_kernel, group=group), grid=(step...]
    ppermute x10 -> x7, starting transfers between devices: 25.3 us -> 19.1 us  [swapped(): return lax.ppermute(shard, axis, SWAP)]
    pallas_call x2 -> x1, Pallas kernels: 17.4 us -> 12.7 us  [respond(): pl.pallas_call(functools.partial(respond_kernel, group=group), grid=(bloc...]
    ppermute x10 -> x7, waiting for transfers between devices: 14.7 us -> 18.6 us  [swapped(): return lax.ppermute(shard, axis, SWAP)]
    broadcast_in_dim x6 -> x2, local copies, waits for them, and re-layouts: 4.79 us -> 0.89 us  [spread(): return exchanged(jnp.broadcast_to(part, (count, *part.shape)), axes)]
  transfers between devices with their start and end apart: 18 -> 9, of which waited for: 11 -> 7; matrix products, arithmetic and copies ran while one was open for 7% -> 7% of each run, Pallas kernels for 14% -> 0%
where the time goes in v3:
time: 183 us; the launch traced here: 182 us
  blocking collectives  70 us (38%)
  waiting for transfers between devices  38.8 us (21%)
  starting transfers between devices  31.4 us (17%)
  Pallas kernels  26.9 us (15%)
  local copies, waits for them, and re-layouts  8.54 us (5%)
  other arithmetic  3.49 us (2%)
  matrix products  2.51 us (1%)
    all_to_all x4, blocking collectives, exchanged(): return lax.all_to_all(parts, axes, split_axis=0, concat_axis=0, tiled=True)  70 us
    all_to_all x2, waiting for transfers between devices, exchanged(): return lax.all_to_all(parts, axes, split_axis=0, concat_axis=0, tiled=True)  20.1 us
    ppermute x7, starting transfers between devices, swapped(): return lax.ppermute(shard, axis, SWAP)  19.1 us
    ppermute x7, waiting for transfers between devices, swapped(): return lax.ppermute(shard, axis, SWAP)  18.6 us
    pallas_call x1, Pallas kernels, respond(): pl.pallas_call(functools.partial(respond_kernel, group=group), grid=(bloc...  12.7 us
    pallas_call x1, Pallas kernels, project(): pl.pallas_call(functools.partial(project_kernel, group=group), grid=(step...  12.5 us
    all_to_all x2, starting transfers between devices, exchanged(): return lax.all_to_all(parts, axes, split_axis=0, concat_axis=0, tiled=True)  12.3 us
  transfers between devices with their start and end apart: 9, of which 7 were waited for; matrix products, arithmetic and copies ran while one was open for 7% of the time, Pallas kernels for 0%

profile of v3, /device:TPU:1, one launch (start us, length us, event | category | flops | bytes accessed | tf_op | source)
XLA Modules:
  0.0 181.8 jit_solution(2857073128957339021)
XLA Ops:
  0.0 3.6 %collective-permute-start.1 = (bf16[32,4096]{1,0:T(8,128)(2,1)}, bf16[32,4096]{1,0:T(8,128)(2,1)}, u32[]{:S(2)}, u32[]{:S(2)}) collective-permute-start(bf16[32,4096]{1,0:T(8,128)(2,1)} %param.7), channel_id=1, source_target_pairs={{0,16},{16,0},{1,17},{17,1},{2,18},{18,2},{3,19},{19,3},{4,20},{20... | collective-permute-start | bytes 786440 | tf_op jit(solution)/shard_map/ppermute | solution.py:23
  3.7 1.1 copy.10
  4.7 0.8 copy.9
  5.5 8.2 %all-to-all-start = ((bf16[8,32,512]{2,1,0:T(8,128)(2,1)}), bf16[8,32,512]{2,1,0:T(8,128)(2,1)S(1)}, u32[]{:S(2)}, u32[]{:S(2)}) async-start(bf16[8,32,512]{2,1,0:T(8,128)(2,1)} %copy.9), calls=%async_computation | async-start | bytes 524288 | tf_op jit(solution)/shard_map/all_to_all | solution.py:27
  15.9 8.1 %all-to-all-done = bf16[8,32,512]{2,1,0:T(8,128)(2,1)S(1)} async-done(((bf16[8,32,512]{2,1,0:T(8,128)(2,1)}), bf16[8,32,512]{2,1,0:T(8,128)(2,1)S(1)}, u32[]{:S(2)}, u32[]{:S(2)}) %all-to-all-start) | async-done | bytes 262176 | tf_op jit(solution)/shard_map/all_to_all | solution.py:27
  23.9 0.8 convolution_convert_fusion.1
  26.6 1.0 dynamic-slice_reduce_fusion
  27.7 0.9 reshape.146.mix_near_ref
  28.6 0.9 reshape.147.mix_far_ref
  29.7 1.1 fusion
  30.8 0.8 broadcast_in_dim.12
  31.6 4.1 %all-to-all-start.1 = ((bf16[8,64,512]{2,1,0:T(8,128)(2,1)}), bf16[8,64,512]{2,1,0:T(8,128)(2,1)}, u32[]{:S(2)}, u32[]{:S(2)}) async-start(bf16[8,64,512]{2,1,0:T(8,128)(2,1)} %broadcast_in_dim.12), calls=%async_computation.1 | async-start | bytes 1048576 | tf_op jit(solution)/shard_map/all_to_all | solution.py:27
  35.8 1.0 broadcast_select_fusion.1
  36.8 0.9 pad_maximum_fusion.basis_ref
  37.6 12.1 %all-to-all-done.1.occ_ref.own_occ = bf16[8,64,512]{2,1,0:T(8,128)(2,1)} async-done(((bf16[8,64,512]{2,1,0:T(8,128)(2,1)}), bf16[8,64,512]{2,1,0:T(8,128)(2,1)}, u32[]{:S(2)}, u32[]{:S(2)}) %all-to-all-start.1) | async-done | bytes 524320 | tf_op jit(solution)/shard_map/all_to_all | solution.py:27
  49.7 1.0 copy-done.1
  50.7 12.5 %project.1 = (f32[8,192,256]{2,1,0:T(8,128)S(1)}, f32[8,192,256]{2,1,0:T(8,128)S(1)}) custom-call(bf16[8,64,512]{2,1,0:T(8,128)(2,1)} %all-to-all-done.1.occ_ref.own_occ, bf16[64,4096]{1,0:T(8,128)(2,1)S(1)} %copy-done.1, bf16[192,4096]{1,0:T(8,128)(2,1)S(1)} %convolution_convert_fusion.pot_ref), custom_call_target="tpu_custom_call" | custom-call | flops 6442450944 | bytes 10000000 | tf_op jit(solution)/shard_map/project/pallas_call | solution.py:70
  63.2 4.6 %collective-permute-start.3 = (f32[8,192,256]{2,1,0:T(8,128)S(1)}, f32[8,192,256]{2,1,0:T(8,128)S(1)}, u32[]{:S(2)}, u32[]{:S(2)}) collective-permute-start(f32[8,192,256]{2,1,0:T(8,128)S(1)} %get-tuple-element.19), channel_id=1, source_target_pairs={{0,1},{1,0},{2,3},{3,2},{4,5},{5,4},{6,7},{7,6},{8,9},{9,8},{10,11... | collective-permute-start | bytes 4718600 | tf_op jit(solution)/shard_map/ppermute | solution.py:23
  67.8 2.5 %collective-permute-start.2 = (bf16[8,64,512]{2,1,0:T(8,128)(2,1)}, bf16[8,64,512]{2,1,0:T(8,128)(2,1)S(1)}, u32[]{:S(2)}, u32[]{:S(2)}) collective-permute-start(bf16[8,64,512]{2,1,0:T(8,128)(2,1)} %all-to-all-done.1.occ_ref.own_occ), channel_id=1, source_target_pairs={{0,16},{16,0},{1,17},{17,1},{2,18},{18,2},{3,19},{19,3},{4,20},{20... | collective-permute-start | bytes 1572872 | tf_op jit(solution)/shard_map/ppermute | solution.py:23
  70.3 12.6 %collective-permute-done.2.other_occ = bf16[8,64,512]{2,1,0:T(8,128)(2,1)S(1)} collective-permute-done((bf16[8,64,512]{2,1,0:T(8,128)(2,1)}, bf16[8,64,512]{2,1,0:T(8,128)(2,1)S(1)}, u32[]{:S(2)}, u32[]{:S(2)}) %collective-permute-start.2) | collective-permute-done | bytes 524320 | tf_op jit(solution)/shard_map/ppermute | solution.py:23
  83.2 16.4 %all_to_all.30 = bf16[8,192,256]{2,1,0:T(8,128)(2,1)S(1)} all-to-all(bf16[8,192,256]{2,1,0:T(8,128)(2,1)S(1)} %add_convert_fusion), channel_id=1, replica_groups=mesh['z'=8,'x_hi'=2,'y'=4,'x_lo'=2,'core'=2] {'y','x_lo'}, dimensions={0} | all-to-all | bytes 1572864 | tf_op jit(solution)/shard_map/all_to_all | solution.py:27
  99.8 2.5 %collective-permute-start.4 = (bf16[96,256]{1,0:T(8,128)(2,1)S(1)}, bf16[96,256]{1,0:T(8,128)(2,1)S(1)}, u32[]{:S(2)}, u32[]{:S(2)}) collective-permute-start(bf16[96,256]{1,0:T(8,128)(2,1)S(1)} %get-tuple-element.28), channel_id=1, source_target_pairs={{0,16},{16,0},{1,17},{17,1},{2,18},{18,2},{3,19},{19,3},{4,20},{20... | collective-permute-start | bytes 147464 | tf_op jit(solution)/shard_map/ppermute | solution.py:23
  102.3 2.0 %collective-permute-done.4 = bf16[96,256]{1,0:T(8,128)(2,1)S(1)} collective-permute-done((bf16[96,256]{1,0:T(8,128)(2,1)S(1)}, bf16[96,256]{1,0:T(8,128)(2,1)S(1)}, u32[]{:S(2)}, u32[]{:S(2)}) %collective-permute-start.4) | collective-permute-done | bytes 49184 | tf_op jit(solution)/shard_map/ppermute | solution.py:23
  104.4 13.0 %all_to_all.31.near_ref = bf16[8,2,96,256]{3,2,1,0:T(8,128)(2,1)S(1)} all-to-all(bf16[8,2,96,256]{3,2,1,0:T(8,128)(2,1)S(1)} %broadcast_in_dim.15), channel_id=1, replica_groups=mesh['z'=8,'x_hi'=2,'y'=4,'x_lo'=2,'core'=2] {'y','x_lo'}, dimensions={0} | all-to-all | bytes 1572864 | tf_op jit(solution)/shard_map/all_to_all | solution.py:27
  117.4 3.7 %collective-permute-start.5 = (bf16[8,2,96,256]{3,2,1,0:T(8,128)(2,1)S(1)}, bf16[8,2,96,256]{3,2,1,0:T(8,128)(2,1)S(1)}, u32[]{:S(2)}, u32[]{:S(2)}) collective-permute-start(bf16[8,2,96,256]{3,2,1,0:T(8,128)(2,1)S(1)} %all_to_all.31.near_ref), channel_id=1, source_target_pairs={{0,1},{1,0},{2,3},{3,2},{4,5},{5,4},{6,7},{7,6},{8,9},{9,8},{10,11... | collective-permute-start | bytes 2359304 | tf_op jit(solution)/shard_map/ppermute | solution.py:23
  121.2 1.9 %collective-permute-done.5.far_ref = bf16[8,2,96,256]{3,2,1,0:T(8,128)(2,1)S(1)} collective-permute-done((bf16[8,2,96,256]{3,2,1,0:T(8,128)(2,1)S(1)}, bf16[8,2,96,256]{3,2,1,0:T(8,128)(2,1)S(1)}, u32[]{:S(2)}, u32[]{:S(2)}) %collective-permute-start.5) | collective-permute-done | bytes 786464 | tf_op jit(solution)/shard_map/ppermute | solution.py:23
  123.1 12.7 %respond.1 = bf16[8,192,256]{2,1,0:T(8,128)(2,1)S(1)} custom-call(bf16[8,64,512]{2,1,0:T(8,128)(2,1)} %all-to-all-done.1.occ_ref.own_occ, bf16[8,64,512]{2,1,0:T(8,128)(2,1)S(1)} %collective-permute-done.2.other_occ, bf16[64,4096]{1,0:T(8,128)(2,1)S(1)} %copy-done.1, bf16[8,2,96,256]{3,2,1,0:T(8,128)(2,1)S(1)} %collective-permute-done.5.far_ref, ...), custom_call_target="tpu_custom_call" | custom-call | flops 6442450944 | bytes 6000000 | tf_op jit(solution)/shard_map/respond/pallas_call | solution.py:115
  135.9 26.1 %all_to_all.32.parts_ref = bf16[8,192,256]{2,1,0:T(8,128)(2,1)S(1)} all-to-all(bf16[8,192,256]{2,1,0:T(8,128)(2,1)S(1)} %respond.1), channel_id=1, replica_groups=mesh['z'=8,'x_hi'=2,'y'=4,'x_lo'=2,'core'=2] {'z'}, dimensions={0} | all-to-all | bytes 1572864 | tf_op jit(solution)/shard_map/all_to_all | solution.py:27
  162.6 14.5 %all_to_all.33.near_ref = bf16[8,12,16,256]{3,2,1,0:T(8,128)(2,1)S(1)} all-to-all(bf16[8,12,16,256]{3,2,1,0:T(8,128)(2,1)S(1)} %shard_map.64), channel_id=1, replica_groups=mesh['z'=8,'x_hi'=2,'y'=4,'x_lo'=2,'core'=2] {'y','x_lo'}, dimensions={0} | all-to-all | bytes 1572864 | tf_op jit(solution)/shard_map/all_to_all | solution.py:27
  177.1 1.8 collective-permute-start.6
  178.9 1.9 %collective-permute-done.6.far_ref = bf16[8,12,16,256]{3,2,1,0:T(8,128)(2,1)S(1)} collective-permute-done((bf16[8,12,16,256]{3,2,1,0:T(8,128)(2,1)S(1)}, bf16[8,12,16,256]{3,2,1,0:T(8,128)(2,1)S(1)}, u32[]{:S(2)}, u32[]{:S(2)}) %collective-permute-start.6) | collective-permute-done | bytes 786464 | tf_op jit(solution)/shard_map/ppermute | solution.py:23
  180.8 1.0 shard_map.65
  (42 shorter events, 5.4 us)
Async XLA Ops:
  0.0 15.3 %copy-start = (bf16[192,4096]{1,0:T(8,128)(2,1)S(1)}, bf16[192,4096]{1,0:T(8,128)(2,1)}, u32[]{:S(2)}) copy-start(bf16[192,4096]{1,0:T(8,128)(2,1)} %param.6) | copy-start | bytes 4718596
  0.0 13.7 %copy-start.4 = (s32[128]{0:T(128)S(1)}, s32[128]{0:T(128)}, u32[]{:S(2)}) copy-start(s32[128]{0:T(128)} %param.9) | copy-start | bytes 1540
  0.0 13.9 %copy-start.7 = (f32[512]{0:T(512)S(1)}, f32[512]{0:T(512)}, u32[]{:S(2)}) copy-start(f32[512]{0:T(512)} %param.8) | copy-start | bytes 6148
  0.0 35.7 %collective-permute-start.1 = (bf16[32,4096]{1,0:T(8,128)(2,1)}, bf16[32,4096]{1,0:T(8,128)(2,1)}, u32[]{:S(2)}, u32[]{:S(2)}) collective-permute-start(bf16[32,4096]{1,0:T(8,128)(2,1)} %param.7), channel_id=1, source_target_pairs={{0,16},{16,0},{1,17},{17,1},{2,18},{18,2},{3,19},{19,3},{4,20},{20... | collective-permute-start | bytes 786440 | tf_op jit(solution)/shard_map/ppermute | solution.py:23
  5.5 18.4 %all-to-all-start = ((bf16[8,32,512]{2,1,0:T(8,128)(2,1)}), bf16[8,32,512]{2,1,0:T(8,128)(2,1)S(1)}, u32[]{:S(2)}, u32[]{:S(2)}) async-start(bf16[8,32,512]{2,1,0:T(8,128)(2,1)} %copy.9), calls=%async_computation | async-start | bytes 524288 | tf_op jit(solution)/shard_map/all_to_all | solution.py:27
  13.7 12.0 %copy-start.5 = (s32[256]{0:T(256)}, s32[256]{0:T(256)S(1)}, u32[]{:S(2)}) copy-start(s32[256]{0:T(256)S(1)} %fusion.13) | copy-start | bytes 3076
  24.8 4.9 %collective-permute-start = (bf16[64,512]{1,0:T(8,128)(2,1)}, bf16[64,512]{1,0:T(8,128)(2,1)}, u32[]{:S(2)}, u32[]{:S(2)}) collective-permute-start(bf16[64,512]{1,0:T(8,128)(2,1)} %convolution_convert_fusion.1), channel_id=1, source_target_pairs={{0,16},{16,0},{1,17},{17,1},{2,18},{18,2},{3,19},{19,3},{4,20},{20... | collective-permute-start | bytes 196616 | tf_op jit(solution)/shard_map/ppermute | solution.py:23
  30.8 5.0 %copy-start.3 = (bf16[32,4096]{1,0:T(8,128)(2,1)S(1)}, bf16[32,4096]{1,0:T(8,128)(2,1)}, u32[]{:S(2)}) copy-start(bf16[32,4096]{1,0:T(8,128)(2,1)} %param.7) | copy-start | bytes 786436
  31.6 18.1 %all-to-all-start.1 = ((bf16[8,64,512]{2,1,0:T(8,128)(2,1)}), bf16[8,64,512]{2,1,0:T(8,128)(2,1)}, u32[]{:S(2)}, u32[]{:S(2)}) async-start(bf16[8,64,512]{2,1,0:T(8,128)(2,1)} %broadcast_in_dim.12), calls=%async_computation.1 | async-start | bytes 1048576 | tf_op jit(solution)/shard_map/all_to_all | solution.py:27
  49.7 1.0 copy-start.1
  63.2 19.7 %collective-permute-start.3 = (f32[8,192,256]{2,1,0:T(8,128)S(1)}, f32[8,192,256]{2,1,0:T(8,128)S(1)}, u32[]{:S(2)}, u32[]{:S(2)}) collective-permute-start(f32[8,192,256]{2,1,0:T(8,128)S(1)} %get-tuple-element.19), channel_id=1, source_target_pairs={{0,1},{1,0},{2,3},{3,2},{4,5},{5,4},{6,7},{7,6},{8,9},{9,8},{10,11... | collective-permute-start | bytes 4718600 | tf_op jit(solution)/shard_map/ppermute | solution.py:23
  67.8 15.1 %collective-permute-start.2 = (bf16[8,64,512]{2,1,0:T(8,128)(2,1)}, bf16[8,64,512]{2,1,0:T(8,128)(2,1)S(1)}, u32[]{:S(2)}, u32[]{:S(2)}) collective-permute-start(bf16[8,64,512]{2,1,0:T(8,128)(2,1)} %all-to-all-done.1.occ_ref.own_occ), channel_id=1, source_target_pairs={{0,16},{16,0},{1,17},{17,1},{2,18},{18,2},{3,19},{19,3},{4,20},{20... | collective-permute-start | bytes 1572872 | tf_op jit(solution)/shard_map/ppermute | solution.py:23
  83.2 16.5 %copy-start.6 = (f32[1,256]{1,0:T(1,128)S(1)}, f32[1,256]{1,0:T(1,128)}, u32[]{:S(2)}) copy-start(f32[1,256]{1,0:T(1,128)} %div.58) | copy-start | bytes 3076
  99.8 4.5 %collective-permute-start.4 = (bf16[96,256]{1,0:T(8,128)(2,1)S(1)}, bf16[96,256]{1,0:T(8,128)(2,1)S(1)}, u32[]{:S(2)}, u32[]{:S(2)}) collective-permute-start(bf16[96,256]{1,0:T(8,128)(2,1)S(1)} %get-tuple-element.28), channel_id=1, source_target_pairs={{0,16},{16,0},{1,17},{17,1},{2,18},{18,2},{3,19},{19,3},{4,20},{20... | collective-permute-start | bytes 147464 | tf_op jit(solution)/shard_map/ppermute | solution.py:23
  117.4 5.7 %collective-permute-start.5 = (bf16[8,2,96,256]{3,2,1,0:T(8,128)(2,1)S(1)}, bf16[8,2,96,256]{3,2,1,0:T(8,128)(2,1)S(1)}, u32[]{:S(2)}, u32[]{:S(2)}) collective-permute-start(bf16[8,2,96,256]{3,2,1,0:T(8,128)(2,1)S(1)} %all_to_all.31.near_ref), channel_id=1, source_target_pairs={{0,1},{1,0},{2,3},{3,2},{4,5},{5,4},{6,7},{7,6},{8,9},{9,8},{10,11... | collective-permute-start | bytes 2359304 | tf_op jit(solution)/shard_map/ppermute | solution.py:23
  135.8 26.1 %copy-start.2 = (f32[256,256]{1,0:T(8,128)S(1)}, f32[256,256]{1,0:T(8,128)}, u32[]{:S(2)}) copy-start(f32[256,256]{1,0:T(8,128)} %cols_ref.1) | copy-start | bytes 786436
  177.1 3.7 %collective-permute-start.6 = (bf16[8,12,16,256]{3,2,1,0:T(8,128)(2,1)S(1)}, bf16[8,12,16,256]{3,2,1,0:T(8,128)(2,1)S(1)}, u32[]{:S(2)}, u32[]{:S(2)}) collective-permute-start(bf16[8,12,16,256]{3,2,1,0:T(8,128)(2,1)S(1)} %all_to_all.33.near_ref), channel_id=1, source_target_pairs={{0,1},{1,0},{2,3},{3,2},{4,5},{5,4},{6,7},{7,6},{8,9},{9,8},{10,11... | collective-permute-start | bytes 2359304 | tf_op jit(solution)/shard_map/ppermute | solution.py:23

commit v4 on v3

v4 whole, which is shorter than its diff:
```python
import functools

import jax
import jax.numpy as jnp
from jax import lax
from jax.experimental import pallas as pl
from jax.experimental.pallas import tpu as pltpu
from jax.sharding import Mesh
from jax.sharding import PartitionSpec as P

SIDE = 256
Z, XH, Y, XL, CORE = "z", "x_hi", "y", "x_lo", "core"
CELL = (Y, XL, CORE)
ORB = (Z, XH)
CHIP = (Y, XL)
F32, BF16 = jnp.float32, jnp.bfloat16
HIGH = lax.Precision.HIGHEST
SWAP = ((0, 1), (1, 0))
ROOM = pltpu.CompilerParams(vmem_limit_bytes=20 * 2**20)


def swapped(shard, axis):
    return lax.ppermute(shard, axis, SWAP)


def exchanged(parts, axes):
    return lax.all_to_all(parts, axes, split_axis=0, concat_axis=0, tiled=True)


def split_kernel(rows_ref, out_ref):
    width = out_ref.shape[2]
    for k in range(out_ref.shape[0]):
        out_ref[k] = rows_ref[:, k * width : (k + 1) * width]


def pick_kernel(wanted_ref, rows_ref, out_ref):
    count, stored = wanted_ref.shape[0], rows_ref.shape[0]
    label = lax.broadcasted_iota(jnp.int32, (count, stored), 1)
    chosen = jnp.where(wanted_ref[...] == label, 1.0, 0.0).astype(BF16)
    picked = jnp.dot(chosen, rows_ref[...], preferred_element_type=F32).astype(BF16)
    slots = out_ref.shape[1]
    for k in range(out_ref.shape[0]):
        n = k % (count // slots)
        out_ref[k] = picked[n * slots : (n + 1) * slots]


def join_kernel(near_ref, far_ref, out_ref):
    out_ref[...] = (near_ref[...] + far_ref[...]).astype(out_ref.dtype)


def products(occ, places, parts):
    return jnp.concatenate([occ[n : n + 1, :] * part for n in places for part in parts], axis=0)


def project_kernel(occ_ref, first_ref, second_ref, pot_ref, out_ref, *, group):
    blocks, count, width = occ_ref.shape
    for n in range(count // group):
        total = None
        for k in range(blocks):
            cut = slice(k * width, (k + 1) * width)
            parts = (first_ref[:, cut], second_ref[:, cut])
            pairs = products(occ_ref[k], range(n * group, (n + 1) * group), parts)
            term = lax.dot_general(
                pot_ref[:, cut], pairs, (((1,), (1,)), ((), ())), preferred_element_type=F32
            )
            total = term if total is None else total + term
        out_ref[n] = total


def project(occ, start, steps, first, second, pot, group):
    blocks, _, width = occ.shape
    rows, points = first.shape
    nv = pot.shape[0]
    per_step = 16
    outs, lanes = per_step // group, 2 * group * rows
    row_spec = pl.BlockSpec((rows, points), lambda t: (0, 0))
    return pl.pallas_call(
        functools.partial(project_kernel, group=group),
        grid=(steps,),
        in_specs=[
            pl.BlockSpec((blocks, per_step, width), lambda t: (0, start + t, 0)),
            row_spec,
            row_spec,
            pl.BlockSpec((nv, points), lambda t: (0, 0)),
        ],
        out_specs=pl.BlockSpec((outs, nv, lanes), lambda t: (t, 0, 0)),
        out_shape=jax.ShapeDtypeStruct((outs * steps, nv, lanes), F32),
        cost_estimate=pl.CostEstimate(
            flops=4 * steps * per_step * rows * points * nv,
            bytes_accessed=4_000_000,
            transcendentals=0,
        ),
        compiler_params=ROOM,
        name="project",
    )(occ, first, second, pot)


def respond_kernel(own_occ, other_occ, first_ref, second_ref, far_ref, near_ref, out_ref, *, group):
    blocks, _, nv, _ = far_ref.shape
    owners, _, side = out_ref.shape
    per_owner = nv // owners
    lines = []
    for r in range(own_occ.shape[0]):
        cut = slice(r * side, (r + 1) * side)
        parts = (first_ref[:, cut], second_ref[:, cut])
        total = None
        for p, occ_ref in enumerate((own_occ, other_occ)):
            for h, ref in enumerate((far_ref, near_ref)):
                for b in range(blocks):
                    base = (h * blocks + b) * group
                    pairs = products(occ_ref[r], range(base, base + group), parts)
                    term = jnp.dot(ref[b, p], pairs, preferred_element_type=F32)
                    total = term if total is None else total + term
        lines.append(total)
    for n in range(owners):
        rows = [line[n * per_owner : (n + 1) * per_owner] for line in lines]
        out_ref[n] = jnp.concatenate(rows, axis=0).astype(out_ref.dtype)


def respond(own_occ, other_occ, start, steps, first, second, far, near, group, owners):
    _, slots, width = own_occ.shape
    rows, _ = first.shape
    nv = far.shape[2]
    occ_spec = pl.BlockSpec((2, slots, width), lambda k: (start + k, 0, 0))
    row_spec = pl.BlockSpec((rows, 2 * width), lambda k: (0, start + k))
    guess_spec = pl.BlockSpec(far.shape, lambda k: (0, 0, 0, 0))
    lines = 2 * nv // owners
    return pl.pallas_call(
        functools.partial(respond_kernel, group=group),
        grid=(steps,),
        in_specs=[occ_spec, occ_spec, row_spec, row_spec, guess_spec, guess_spec],
        out_specs=pl.BlockSpec((owners, lines, SIDE), lambda k: (0, k, 0)),
        out_shape=jax.ShapeDtypeStruct((owners, steps * lines, SIDE), BF16),
        cost_estimate=pl.CostEstimate(
            flops=16 * slots * rows * width * steps * nv,
            bytes_accessed=3_000_000,
            transcendentals=0,
        ),
        compiler_params=ROOM,
        name="respond",
    )(own_occ, other_occ, first, second, far, near)


def columns_kernel(top_ref, bottom_ref, cols_ref, out_ref):
    copies, count, lines, side = out_ref.shape
    size = count * lines
    planes = []
    for ref in (top_ref, bottom_ref):
        plane = ref[0].astype(F32)
        for s in range(1, ref.shape[0]):
            plane = plane + ref[s].astype(F32)
        planes.append(plane)
    plane = jnp.concatenate(planes, axis=0)
    mixed = lax.dot_general(
        plane, cols_ref[...], (((1,), (1,)), ((), ())), precision=HIGH, preferred_element_type=F32
    ).astype(BF16)
    row = lax.broadcasted_iota(jnp.int32, (size, size), 0)
    column = lax.broadcasted_iota(jnp.int32, (size, size), 1)
    source = row % lines * count + row // lines
    swap = jnp.where(source == column, 1.0, 0.0).astype(BF16)
    block = jnp.dot(swap, mixed, preferred_element_type=F32).astype(BF16)
    block = block.reshape(count, lines, side)
    for n in range(copies):
        out_ref[n] = block


def in_three(block):
    high = block.astype(BF16)
    rest = block - high.astype(F32)
    mid = rest.astype(BF16)
    low = (rest - mid.astype(F32)).astype(BF16)
    return high, mid, low


def rows_kernel(near_ref, far_ref, mix_near_ref, mix_far_ref, out_ref):
    chips, count, lines, _ = near_ref.shape
    mixes = [jnp.concatenate(in_three(m[...]), axis=0) for m in (mix_near_ref, mix_far_ref)]
    for n in range(count):
        total = None
        for ref, mix in zip((near_ref, far_ref), mixes):
            block = jnp.concatenate([ref[k, n] for k in range(chips)], axis=0)
            term = jnp.dot(mix, block, preferred_element_type=F32)
            total = term if total is None else total + term
        out_ref[n] = total[:lines] + (total[lines : 2 * lines] + total[2 * lines :])


def small_call(kernel, out, *args):
    return pl.pallas_call(kernel, out_shape=out, compiler_params=ROOM)(*args)


def body(potentials, orbitals, levels, occ_index, coul_rows, coul_cols):
    nv, points = potentials.shape
    mine = orbitals.shape[0]
    norb, nocc = levels.shape[0], occ_index.shape[0]
    nz, nx, ny, nl, nc = (lax.axis_size(a) for a in (Z, XH, Y, XL, CORE))
    z, xh, y, xl, core = (lax.axis_index(a) for a in (Z, XH, Y, XL, CORE))
    chips = ny * nl
    chip = y * nl + xl
    width = points // (nz * nx)
    slots = nocc // nx
    half = slots // nc
    group = half // chips
    lines = points // SIDE
    volume = points * chips * nc
    per_owner = nv // (nz * nx)

    blocks = jax.ShapeDtypeStruct((nz * nx, mine, width), BF16)
    by_points = exchanged(small_call(split_kernel, blocks, orbitals), ORB)
    partner = swapped(orbitals, XH)

    def part_of(values, start, count):
        return lax.dynamic_slice_in_dim(values, start, count)

    starts = [s * slots + c * half for s in range(nx) for c in (1 - core, core)]
    wanted = jnp.concatenate([part_of(occ_index, s, half) for s in starts])[:, None]
    copies = jax.ShapeDtypeStruct((nz * nx, slots, width), BF16)
    spread = small_call(pick_kernel, copies, wanted, by_points.reshape(norb, width))
    occ = exchanged(spread, ORB)

    place = jnp.arange(nv, dtype=jnp.int32)
    side = (xh + 1 + place // (nz * per_owner)) % nx
    source = (place // per_owner % nz * nx + side) * per_owner + place % per_owner
    order = (source[:, None] == place[None, :]).astype(BF16)
    pot = jnp.dot(order, potentials, preferred_element_type=F32).astype(BF16)
    first = jnp.where(xh == 0, orbitals, partner)
    second = jnp.where(xh == 0, partner, orbitals)

    labels = jnp.arange(norb, dtype=jnp.int32)
    empty = 1.0 - jnp.any(occ_index[:, None] == labels[None, :], axis=0).astype(F32)
    own_slots = part_of(occ_index, xh * slots + core * half + chip * group, group)
    own_levels = jnp.sum(
        jnp.where(own_slots[:, None] == labels[None, :], levels[None, :], 0.0), axis=1
    )
    stored = z * nx * mine
    basis_empty = part_of(empty, stored, nx * mine)
    basis_levels = part_of(levels, stored, nx * mine)
    weight = -2.0 * basis_empty[None, :] / (own_levels[:, None] + basis_levels[None, :])
    weight = (weight / volume).reshape(1, group * nx * mine)

    my_rows = part_of(coul_rows, (chip * nc + core) * lines, lines)
    my_rows = my_rows.reshape(lines, chips, nc, lines)
    mixes = [
        lax.dynamic_index_in_dim(my_rows, c, 2, keepdims=False).reshape(lines, chips * lines)
        for c in (core, 1 - core)
    ]
    held_back = (occ, pot, first, second, weight, mixes)
    occ, pot, first, second, weight, mixes = lax.optimization_barrier(held_back)

    other_occ = swapped(occ, XH)
    rest = (first, second, pot, group)
    far = project(occ, 0, half // 16, *rest)
    far = swapped(far, CORE)
    near = project(occ, half // 16, half // 16, *rest)
    near, other_occ = lax.optimization_barrier((near, other_occ))
    summed = small_call(join_kernel, jax.ShapeDtypeStruct(near.shape, BF16), near, far)
    intersection = jnp.sum(exchanged(summed, CHIP).astype(F32), axis=0)
    guess = (intersection * weight).astype(BF16)

    given, kept = guess[: nv // nx], guess[nv // nx :]
    guesses = jnp.stack([kept, swapped(given, XH)])
    near_guess = exchanged(jnp.broadcast_to(guesses, (chips, *guesses.shape)), CHIP)
    far_guess = swapped(near_guess, CORE)
    parts = []
    for n in range(2):
        response = respond(
            occ, other_occ, n * lines // 4, lines // 4, first, second, far_guess, near_guess,
            group, nz,
        )
        parts.append(exchanged(response, Z))

    out = jax.ShapeDtypeStruct((chips, per_owner, lines, SIDE), BF16)
    columns = small_call(columns_kernel, out, *parts, coul_cols)
    near_cols = exchanged(columns, CHIP)
    far_cols = swapped(near_cols, CORE)
    out = jax.ShapeDtypeStruct((per_owner, lines, SIDE), F32)
    return small_call(rows_kernel, out, near_cols, far_cols, *mixes)


def solution(mesh):
    torus = Mesh(mesh.devices.reshape(8, 2, 4, 2, 2), (Z, XH, Y, XL, CORE))
    return jax.shard_map(
        body,
        mesh=torus,
        in_specs=(P(None, CELL), P(ORB, CELL), P(), P(), P(), P()),
        out_specs=P(ORB, CELL, None),
        check_vma=False,
    )
```

time: 183 us -> 178 us (0.973)
  blocking collectives: 70 us -> 58.6 us
  local copies, waits for them, and re-layouts: 8.54 us -> 14.9 us
  waiting for transfers between devices: 38.8 us -> 33.8 us
  Pallas kernels: 26.9 us -> 31.1 us
  starting transfers between devices: 31.4 us -> 34.1 us
  matrix products: 2.51 us -> 0.61 us
    all_to_all x4, blocking collectives: 70 us -> 58.6 us  [exchanged(): return lax.all_to_all(parts, axes, split_axis=0, concat_axis=0, tiled=True)]
    unnamed x17 -> x26, local copies, waits for them, and re-layouts: 2.14 us -> 7.88 us
    ppermute x7 -> x6, waiting for transfers between devices: 18.6 us -> 14.2 us  [swapped(): return lax.ppermute(shard, axis, SWAP)]
    all_to_all x2 -> x3, starting transfers between devices: 12.3 us -> 16.1 us  [exchanged(): return lax.all_to_all(parts, axes, split_axis=0, concat_axis=0, tiled=True)]
    dynamic_slice x4, local copies, waits for them, and re-layouts: 0.96 us -> 3.1 us  [part_of(): return lax.dynamic_slice_in_dim(values, start, count)]
    pallas_call x2 -> x5, Pallas kernels: 1.71 us -> 3.6 us  [small_call(): return pl.pallas_call(kernel, out_shape=out, compiler_params=ROOM)(*args)]
    dot_general x2 -> x0, matrix products: 1.89 us -> none  [selected(): return jnp.dot(chosen, by_points, preferred_element_type=F32).astype(BF16)]
    pallas_call x1 -> x2, Pallas kernels: 12.7 us -> 14.3 us  [respond(): pl.pallas_call(functools.partial(respond_kernel, group=group), grid=(step...]
  transfers between devices with their start and end apart: 9 -> 9, of which waited for: 7 -> 7; matrix products, arithmetic and copies ran while one was open for 7% -> 6% of each run, Pallas kernels for 0% -> 9%
where the time goes in v4:
time: 178 us; the launch traced here: 177 us
  blocking collectives  58.6 us (33%)
  starting transfers between devices  34.1 us (19%)
  waiting for transfers between devices  33.8 us (19%)
  Pallas kernels  31.1 us (17%)
  local copies, waits for them, and re-layouts  14.9 us (8%)
  other arithmetic  3.79 us (2%)
    all_to_all x4, blocking collectives, exchanged(): return lax.all_to_all(parts, axes, split_axis=0, concat_axis=0, tiled=True)  58.6 us
    all_to_all x3, waiting for transfers between devices, exchanged(): return lax.all_to_all(parts, axes, split_axis=0, concat_axis=0, tiled=True)  19.6 us
    ppermute x6, starting transfers between devices, swapped(): return lax.ppermute(shard, axis, SWAP)  18 us
    all_to_all x3, starting transfers between devices, exchanged(): return lax.all_to_all(parts, axes, split_axis=0, concat_axis=0, tiled=True)  16.1 us
    pallas_call x2, Pallas kernels, respond(): pl.pallas_call(functools.partial(respond_kernel, group=group), grid=(step...  14.3 us
    ppermute x6, waiting for transfers between devices, swapped(): return lax.ppermute(shard, axis, SWAP)  14.2 us
    pallas_call x2, Pallas kernels, project(): pl.pallas_call(functools.partial(project_kernel, group=group), grid=(step...  13.2 us
    unnamed x26, local copies, waits for them, and re-layouts  7.88 us
  transfers between devices with their start and end apart: 9, of which 7 were waited for; matrix products, arithmetic and copies ran while one was open for 6% of the time, Pallas kernels for 9%

profile of v4, /device:TPU:1, one launch (start us, length us, event | category | flops | bytes accessed | tf_op | source)
XLA Modules:
  0.0 177.1 jit_solution(3806179127269574161)
XLA Ops:
  0.0 3.6 %collective-permute-start = (bf16[32,4096]{1,0:T(8,128)(2,1)}, bf16[32,4096]{1,0:T(8,128)(2,1)}, u32[]{:S(2)}, u32[]{:S(2)}) collective-permute-start(bf16[32,4096]{1,0:T(8,128)(2,1)} %rows_ref.1), channel_id=1, source_target_pairs={{0,16},{16,0},{1,17},{17,1},{2,18},{18,2},{3,19},{19,3},{4,20},{20... | collective-permute-start | bytes 786440 | tf_op jit(solution)/shard_map/ppermute | solution.py:23
  3.6 1.0 copy-done.1
  5.3 8.3 %all-to-all-start = ((bf16[16,32,256]{2,1,0:T(8,128)(2,1)}), bf16[16,32,256]{2,1,0:T(8,128)(2,1)S(1)}, u32[]{:S(2)}, u32[]{:S(2)}) async-start(bf16[16,32,256]{2,1,0:T(8,128)(2,1)} %shard_map.64), calls=%async_computation | async-start | bytes 524288 | tf_op jit(solution)/shard_map/all_to_all | solution.py:27
  18.6 6.6 %all-to-all-done = bf16[16,32,256]{2,1,0:T(8,128)(2,1)S(1)} async-done(((bf16[16,32,256]{2,1,0:T(8,128)(2,1)}), bf16[16,32,256]{2,1,0:T(8,128)(2,1)S(1)}, u32[]{:S(2)}, u32[]{:S(2)}) %all-to-all-start) | async-done | bytes 262176 | tf_op jit(solution)/shard_map/all_to_all | solution.py:27
  25.3 1.0 shard_map.65
  26.3 4.4 %all-to-all-start.1 = ((bf16[16,64,256]{2,1,0:T(8,128)(2,1)}), bf16[16,64,256]{2,1,0:T(8,128)(2,1)}, u32[]{:S(2)}, u32[]{:S(2)}) async-start(bf16[16,64,256]{2,1,0:T(8,128)(2,1)} %shard_map.65), calls=%async_computation.1 | async-start | bytes 1048576 | tf_op jit(solution)/shard_map/all_to_all | solution.py:27
  32.3 1.0 dynamic-slice_reduce_fusion
  35.2 1.8 %broadcast_select_fusion = (bf16[32,4096]{1,0:T(8,128)(2,1)}, bf16[32,4096]{1,0:T(8,128)(2,1)}) fusion(bf16[32,4096]{1,0:T(8,128)(2,1)} %collective-permute-done, bf16[32,4096]{1,0:T(8,128)(2,1)S(1)} %copy-done.2, pred[]{:T(512)S(6)} %eq.50), kind=kLoop, calls=%fused_computation.4 | loop fusion | flops 262144 | bytes 1048577 | tf_op jit(solution)/shard_map/jit(_where)/select_n | solution.py:226
  37.0 8.8 %all-to-all-done.1.occ_ref.own_occ = bf16[16,64,256]{2,1,0:T(8,128)(2,1)} async-done(((bf16[16,64,256]{2,1,0:T(8,128)(2,1)}), bf16[16,64,256]{2,1,0:T(8,128)(2,1)}, u32[]{:S(2)}, u32[]{:S(2)}) %all-to-all-start.1) | async-done | bytes 524320 | tf_op jit(solution)/shard_map/all_to_all | solution.py:27
  45.7 0.9 copy-done.4
  47.6 6.6 %project.3 = f32[8,192,256]{2,1,0:T(8,128)S(1)} custom-call(bf16[16,64,256]{2,1,0:T(8,128)(2,1)} %all-to-all-done.1.occ_ref.own_occ, bf16[32,4096]{1,0:T(8,128)(2,1)S(1)} %copy-done.6, bf16[32,4096]{1,0:T(8,128)(2,1)S(1)} %copy-done.4, bf16[192,4096]{1,0:T(8,128)(2,1)S(1)} %convolution_convert_fusion.pot_ref), custom_call_target="tpu_custom_call" | custom-call | flops 3221225472 | bytes 4000000 | tf_op jit(solution)/shard_map/project/pallas_call | solution.py:77
  54.2 4.7 %collective-permute-start.2 = (f32[8,192,256]{2,1,0:T(8,128)S(1)}, f32[8,192,256]{2,1,0:T(8,128)S(1)}, u32[]{:S(2)}, u32[]{:S(2)}) collective-permute-start(f32[8,192,256]{2,1,0:T(8,128)S(1)} %project.3), channel_id=1, source_target_pairs={{0,1},{1,0},{2,3},{3,2},{4,5},{5,4},{6,7},{7,6},{8,9},{9,8},{10,11... | collective-permute-start | bytes 4718600 | tf_op jit(solution)/shard_map/ppermute | solution.py:23
  59.0 1.0 collective-permute-start.1
  59.9 6.6 %project.2.near_ref = f32[8,192,256]{2,1,0:T(8,128)S(1)} custom-call(bf16[16,64,256]{2,1,0:T(8,128)(2,1)} %all-to-all-done.1.occ_ref.own_occ, bf16[32,4096]{1,0:T(8,128)(2,1)S(1)} %copy-done.6, bf16[32,4096]{1,0:T(8,128)(2,1)S(1)} %copy-done.4, bf16[192,4096]{1,0:T(8,128)(2,1)S(1)} %convolution_convert_fusion.pot_ref), custom_call_target="tpu_custom_call" | custom-call | flops 3221225472 | bytes 4000000 | tf_op jit(solution)/shard_map/project/pallas_call | solution.py:77
  66.6 7.5 %collective-permute-done.1.other_occ = bf16[16,64,256]{2,1,0:T(8,128)(2,1)S(1)} collective-permute-done((bf16[16,64,256]{2,1,0:T(8,128)(2,1)}, bf16[16,64,256]{2,1,0:T(8,128)(2,1)S(1)}, u32[]{:S(2)}, u32[]{:S(2)}) %collective-permute-start.1) | collective-permute-done | bytes 524320 | tf_op jit(solution)/shard_map/ppermute | solution.py:23
  74.2 16.6 %all_to_all.35 = bf16[8,192,256]{2,1,0:T(8,128)(2,1)S(1)} all-to-all(bf16[8,192,256]{2,1,0:T(8,128)(2,1)S(1)} %shard_map.66), channel_id=1, replica_groups=mesh['z'=8,'x_hi'=2,'y'=4,'x_lo'=2,'core'=2] {'y','x_lo'}, dimensions={0} | all-to-all | bytes 1572864 | tf_op jit(solution)/shard_map/all_to_all | solution.py:27
  90.9 1.7 collective-permute-start.3
  92.6 2.9 %collective-permute-done.3 = bf16[96,256]{1,0:T(8,128)(2,1)S(1)} collective-permute-done((bf16[96,256]{1,0:T(8,128)(2,1)S(1)}, bf16[96,256]{1,0:T(8,128)(2,1)S(1)}, u32[]{:S(2)}, u32[]{:S(2)}) %collective-permute-start.3) | collective-permute-done | bytes 49184 | tf_op jit(solution)/shard_map/ppermute | solution.py:23
  95.6 13.0 %all_to_all.36.near_ref = bf16[8,2,96,256]{3,2,1,0:T(8,128)(2,1)S(1)} all-to-all(bf16[8,2,96,256]{3,2,1,0:T(8,128)(2,1)S(1)} %broadcast_in_dim.19), channel_id=1, replica_groups=mesh['z'=8,'x_hi'=2,'y'=4,'x_lo'=2,'core'=2] {'y','x_lo'}, dimensions={0} | all-to-all | bytes 1572864 | tf_op jit(solution)/shard_map/all_to_all | solution.py:27
  108.6 3.7 %collective-permute-start.4 = (bf16[8,2,96,256]{3,2,1,0:T(8,128)(2,1)S(1)}, bf16[8,2,96,256]{3,2,1,0:T(8,128)(2,1)S(1)}, u32[]{:S(2)}, u32[]{:S(2)}) collective-permute-start(bf16[8,2,96,256]{3,2,1,0:T(8,128)(2,1)S(1)} %all_to_all.36.near_ref), channel_id=1, source_target_pairs={{0,1},{1,0},{2,3},{3,2},{4,5},{5,4},{6,7},{7,6},{8,9},{9,8},{10,11... | collective-permute-start | bytes 2359304 | tf_op jit(solution)/shard_map/ppermute | solution.py:23
  112.3 1.9 %collective-permute-done.4.far_ref = bf16[8,2,96,256]{3,2,1,0:T(8,128)(2,1)S(1)} collective-permute-done((bf16[8,2,96,256]{3,2,1,0:T(8,128)(2,1)S(1)}, bf16[8,2,96,256]{3,2,1,0:T(8,128)(2,1)S(1)}, u32[]{:S(2)}, u32[]{:S(2)}) %collective-permute-start.4) | collective-permute-done | bytes 786464 | tf_op jit(solution)/shard_map/ppermute | solution.py:23
  114.3 7.4 %respond.3 = bf16[8,96,256]{2,1,0:T(8,128)(2,1)} custom-call(bf16[16,64,256]{2,1,0:T(8,128)(2,1)} %all-to-all-done.1.occ_ref.own_occ, bf16[16,64,256]{2,1,0:T(8,128)(2,1)S(1)} %collective-permute-done.1.other_occ, bf16[32,4096]{1,0:T(8,128)(2,1)S(1)} %copy-done.6, bf16[32,4096]{1,0:T(8,128)(2,1)S(1)} %copy-done.4, ...), custom_call_target="tpu_custom_call" | custom-call | flops 3221225472 | bytes 3000000 | tf_op jit(solution)/shard_map/respond/pallas_call | solution.py:128
  122.6 3.5 %all-to-all-start.5 = ((bf16[8,96,256]{2,1,0:T(8,128)(2,1)}), bf16[8,96,256]{2,1,0:T(8,128)(2,1)S(1)}, u32[]{:S(2)}, u32[]{:S(2)}) async-start(bf16[8,96,256]{2,1,0:T(8,128)(2,1)} %respond.3), calls=%async_computation.5 | async-start | bytes 786432 | tf_op jit(solution)/shard_map/all_to_all | solution.py:27
  128.0 1.1 copy-done.9
  129.1 1.0 copy-done.11
  130.1 6.8 %respond.2 = bf16[8,96,256]{2,1,0:T(8,128)(2,1)S(1)} custom-call(bf16[16,64,256]{2,1,0:T(8,128)(2,1)} %all-to-all-done.1.occ_ref.own_occ, bf16[16,64,256]{2,1,0:T(8,128)(2,1)S(1)} %copy-done.11, bf16[32,4096]{1,0:T(8,128)(2,1)S(1)} %copy-done.7, bf16[32,4096]{1,0:T(8,128)(2,1)S(1)} %copy-done.5, bf16[8,2,96,256]{3,2,1,0:T(8,128)(2,1)S(1)} %copy-done.9, ...), custom_call_target="tpu_custom_call" | custom-call | flops 3221225472 | bytes 3000000 | tf_op jit(solution)/shard_map/respond/pallas_call | solution.py:128
  137.0 4.2 %all-to-all-done.5.bottom_ref = bf16[8,96,256]{2,1,0:T(8,128)(2,1)S(1)} async-done(((bf16[8,96,256]{2,1,0:T(8,128)(2,1)}), bf16[8,96,256]{2,1,0:T(8,128)(2,1)S(1)}, u32[]{:S(2)}, u32[]{:S(2)}) %all-to-all-start.5) | async-done | bytes 393248 | tf_op jit(solution)/shard_map/all_to_all | solution.py:27
  141.1 16.0 %all_to_all.37.top_ref = bf16[8,96,256]{2,1,0:T(8,128)(2,1)S(1)} all-to-all(bf16[8,96,256]{2,1,0:T(8,128)(2,1)S(1)} %respond.2), channel_id=1, replica_groups=mesh['z'=8,'x_hi'=2,'y'=4,'x_lo'=2,'core'=2] {'z'}, dimensions={0} | all-to-all | bytes 786432 | tf_op jit(solution)/shard_map/all_to_all | solution.py:27
  157.8 13.0 %all_to_all.38.near_ref = bf16[8,12,16,256]{3,2,1,0:T(8,128)(2,1)S(1)} all-to-all(bf16[8,12,16,256]{3,2,1,0:T(8,128)(2,1)S(1)} %shard_map.67), channel_id=1, replica_groups=mesh['z'=8,'x_hi'=2,'y'=4,'x_lo'=2,'core'=2] {'y','x_lo'}, dimensions={0} | all-to-all | bytes 1572864 | tf_op jit(solution)/shard_map/all_to_all | solution.py:27
  170.8 3.3 %collective-permute-start.5 = (bf16[8,12,16,256]{3,2,1,0:T(8,128)(2,1)S(1)}, bf16[8,12,16,256]{3,2,1,0:T(8,128)(2,1)S(1)}, u32[]{:S(2)}, u32[]{:S(2)}) collective-permute-start(bf16[8,12,16,256]{3,2,1,0:T(8,128)(2,1)S(1)} %all_to_all.38.near_ref), channel_id=1, source_target_pairs={{0,1},{1,0},{2,3},{3,2},{4,5},{5,4},{6,7},{7,6},{8,9},{9,8},{10,11... | collective-permute-start | bytes 2359304 | tf_op jit(solution)/shard_map/ppermute | solution.py:23
  174.1 1.9 %collective-permute-done.5.far_ref = bf16[8,12,16,256]{3,2,1,0:T(8,128)(2,1)S(1)} collective-permute-done((bf16[8,12,16,256]{3,2,1,0:T(8,128)(2,1)S(1)}, bf16[8,12,16,256]{3,2,1,0:T(8,128)(2,1)S(1)}, u32[]{:S(2)}, u32[]{:S(2)}) %collective-permute-start.5) | collective-permute-done | bytes 786464 | tf_op jit(solution)/shard_map/ppermute | solution.py:23
  176.0 1.1 shard_map.68
  (49 shorter events, 14.0 us)
Async XLA Ops:
  0.0 17.9 %copy-start = (bf16[192,4096]{1,0:T(8,128)(2,1)S(1)}, bf16[192,4096]{1,0:T(8,128)(2,1)}, u32[]{:S(2)}) copy-start(bf16[192,4096]{1,0:T(8,128)(2,1)} %param.6) | copy-start | bytes 4718596
  0.0 35.2 %collective-permute-start = (bf16[32,4096]{1,0:T(8,128)(2,1)}, bf16[32,4096]{1,0:T(8,128)(2,1)}, u32[]{:S(2)}, u32[]{:S(2)}) collective-permute-start(bf16[32,4096]{1,0:T(8,128)(2,1)} %rows_ref.1), channel_id=1, source_target_pairs={{0,16},{16,0},{1,17},{17,1},{2,18},{18,2},{3,19},{19,3},{4,20},{20... | collective-permute-start | bytes 786440 | tf_op jit(solution)/shard_map/ppermute | solution.py:23
  3.6 1.0 copy-start.1
  5.3 20.0 %all-to-all-start = ((bf16[16,32,256]{2,1,0:T(8,128)(2,1)}), bf16[16,32,256]{2,1,0:T(8,128)(2,1)S(1)}, u32[]{:S(2)}, u32[]{:S(2)}) async-start(bf16[16,32,256]{2,1,0:T(8,128)(2,1)} %shard_map.64), calls=%async_computation | async-start | bytes 524288 | tf_op jit(solution)/shard_map/all_to_all | solution.py:27
  26.3 8.9 %copy-start.2 = (bf16[32,4096]{1,0:T(8,128)(2,1)S(1)}, bf16[32,4096]{1,0:T(8,128)(2,1)}, u32[]{:S(2)}) copy-start(bf16[32,4096]{1,0:T(8,128)(2,1)} %rows_ref.1) | copy-start | bytes 786436
  26.3 19.4 %all-to-all-start.1 = ((bf16[16,64,256]{2,1,0:T(8,128)(2,1)}), bf16[16,64,256]{2,1,0:T(8,128)(2,1)}, u32[]{:S(2)}, u32[]{:S(2)}) async-start(bf16[16,64,256]{2,1,0:T(8,128)(2,1)} %shard_map.65), calls=%async_computation.1 | async-start | bytes 1048576 | tf_op jit(solution)/shard_map/all_to_all | solution.py:27
  45.7 1.0 copy-start.4
  46.7 0.9 copy-start.6
  54.2 19.8 %collective-permute-start.2 = (f32[8,192,256]{2,1,0:T(8,128)S(1)}, f32[8,192,256]{2,1,0:T(8,128)S(1)}, u32[]{:S(2)}, u32[]{:S(2)}) collective-permute-start(f32[8,192,256]{2,1,0:T(8,128)S(1)} %project.3), channel_id=1, source_target_pairs={{0,1},{1,0},{2,3},{3,2},{4,5},{5,4},{6,7},{7,6},{8,9},{9,8},{10,11... | collective-permute-start | bytes 4718600 | tf_op jit(solution)/shard_map/ppermute | solution.py:23
  59.0 15.1 %collective-permute-start.1 = (bf16[16,64,256]{2,1,0:T(8,128)(2,1)}, bf16[16,64,256]{2,1,0:T(8,128)(2,1)S(1)}, u32[]{:S(2)}, u32[]{:S(2)}) collective-permute-start(bf16[16,64,256]{2,1,0:T(8,128)(2,1)} %all-to-all-done.1.occ_ref.own_occ), channel_id=1, source_target_pairs={{0,16},{16,0},{1,17},{17,1},{2,18},{18,2},{3,19},{19,3},{4,20},{20... | collective-permute-start | bytes 1572872 | tf_op jit(solution)/shard_map/ppermute | solution.py:23
  74.1 40.2 %copy-start.10 = (bf16[16,64,256]{2,1,0:T(8,128)(2,1)}, bf16[16,64,256]{2,1,0:T(8,128)(2,1)S(1)}, u32[]{:S(2)}) copy-start(bf16[16,64,256]{2,1,0:T(8,128)(2,1)S(1)} %collective-permute-done.1.other_occ) | copy-start | bytes 1572868
  74.2 16.7 %copy-start.12 = (f32[1,256]{1,0:T(1,128)S(1)}, f32[1,256]{1,0:T(1,128)}, u32[]{:S(2)}) copy-start(f32[1,256]{1,0:T(1,128)} %div.48) | copy-start | bytes 3076
  90.9 4.5 %collective-permute-start.3 = (bf16[96,256]{1,0:T(8,128)(2,1)S(1)}, bf16[96,256]{1,0:T(8,128)(2,1)S(1)}, u32[]{:S(2)}, u32[]{:S(2)}) collective-permute-start(bf16[96,256]{1,0:T(8,128)(2,1)S(1)} %get-tuple-element.28), channel_id=1, source_target_pairs={{0,16},{16,0},{1,17},{17,1},{2,18},{18,2},{3,19},{19,3},{4,20},{20... | collective-permute-start | bytes 147464 | tf_op jit(solution)/shard_map/ppermute | solution.py:23
  108.6 5.7 %collective-permute-start.4 = (bf16[8,2,96,256]{3,2,1,0:T(8,128)(2,1)S(1)}, bf16[8,2,96,256]{3,2,1,0:T(8,128)(2,1)S(1)}, u32[]{:S(2)}, u32[]{:S(2)}) collective-permute-start(bf16[8,2,96,256]{3,2,1,0:T(8,128)(2,1)S(1)} %all_to_all.36.near_ref), channel_id=1, source_target_pairs={{0,1},{1,0},{2,3},{3,2},{4,5},{5,4},{6,7},{7,6},{8,9},{9,8},{10,11... | collective-permute-start | bytes 2359304 | tf_op jit(solution)/shard_map/ppermute | solution.py:23
  121.7 0.9 copy-start.8
  122.6 18.5 %all-to-all-start.5 = ((bf16[8,96,256]{2,1,0:T(8,128)(2,1)}), bf16[8,96,256]{2,1,0:T(8,128)(2,1)S(1)}, u32[]{:S(2)}, u32[]{:S(2)}) async-start(bf16[8,96,256]{2,1,0:T(8,128)(2,1)} %respond.3), calls=%async_computation.5 | async-start | bytes 786432 | tf_op jit(solution)/shard_map/all_to_all | solution.py:27
  126.1 1.0 copy-start.5
  127.0 0.9 copy-start.7
  128.0 1.1 copy-start.9
  129.1 1.0 copy-start.11
  130.1 27.0 %copy-start.3 = (f32[256,256]{1,0:T(8,128)S(1)}, f32[256,256]{1,0:T(8,128)}, u32[]{:S(2)}) copy-start(f32[256,256]{1,0:T(8,128)} %cols_ref.1) | copy-start | bytes 786436
  170.8 5.2 %collective-permute-start.5 = (bf16[8,12,16,256]{3,2,1,0:T(8,128)(2,1)S(1)}, bf16[8,12,16,256]{3,2,1,0:T(8,128)(2,1)S(1)}, u32[]{:S(2)}, u32[]{:S(2)}) collective-permute-start(bf16[8,12,16,256]{3,2,1,0:T(8,128)(2,1)S(1)} %all_to_all.38.near_ref), channel_id=1, source_target_pairs={{0,1},{1,0},{2,3},{3,2},{4,5},{5,4},{6,7},{7,6},{8,9},{9,8},{10,11... | collective-permute-start | bytes 2359304 | tf_op jit(solution)/shard_map/ppermute | solution.py:23

commit v5 on v4

--- a/solution.py
+++ b/solution.py
@@ -42,6 +42,13 @@
     for k in range(out_ref.shape[0]):
         n = k % (count // slots)
         out_ref[k] = picked[n * slots : (n + 1) * slots]
+
+
+def order_kernel(source_ref, rows_ref, out_ref):
+    count = source_ref.shape[0]
+    label = lax.broadcasted_iota(jnp.int32, (count, count), 1)
+    order = jnp.where(source_ref[...] == label, 1.0, 0.0).astype(BF16)
+    out_ref[...] = jnp.dot(order, rows_ref[...], preferred_element_type=F32).astype(BF16)
 
 
 def join_kernel(near_ref, far_ref, out_ref):
@@ -67,11 +74,14 @@
         out_ref[n] = total
 
 
-def project(occ, start, steps, first, second, pot, group):
-    blocks, _, width = occ.shape
+def project(occ, start, first, second, pot, group):
+    blocks, slots, width = occ.shape
+    slots //= 2
     rows, points = first.shape
     nv = pot.shape[0]
     per_step = 16
+    steps = slots // per_step
+    start *= steps
     outs, lanes = per_step // group, 2 * group * rows
     row_spec = pl.BlockSpec((rows, points), lambda t: (0, 0))
     return pl.pallas_call(
@@ -95,20 +105,22 @@
     )(occ, first, second, pot)
 
 
-def respond_kernel(own_occ, other_occ, first_ref, second_ref, far_ref, near_ref, out_ref, *, group):
+def respond_kernel(*refs, group):
+    *occ_refs, first_ref, second_ref, far_ref, near_ref, out_ref = refs
     blocks, _, nv, _ = far_ref.shape
     owners, _, side = out_ref.shape
     per_owner = nv // owners
     lines = []
-    for r in range(own_occ.shape[0]):
+    for r in range(occ_refs[0].shape[0]):
         cut = slice(r * side, (r + 1) * side)
         parts = (first_ref[:, cut], second_ref[:, cut])
         total = None
-        for p, occ_ref in enumerate((own_occ, other_occ)):
+        for p, occ_ref in enumerate(occ_refs):
             for h, ref in enumerate((far_ref, near_ref)):
                 for b in range(blocks):
                     base = (h * blocks + b) * group
-                    pairs = products(occ_ref[r], range(base, base + group), parts)
+                    places = range(base, base + group)
+                    pairs = products(occ_ref[r], places, parts[:: 1 - 2 * p])
                     term = jnp.dot(ref[b, p], pairs, preferred_element_type=F32)
                     total = term if total is None else total + term
         lines.append(total)
@@ -117,40 +129,37 @@
         out_ref[n] = jnp.concatenate(rows, axis=0).astype(out_ref.dtype)
 
 
-def respond(own_occ, other_occ, start, steps, first, second, far, near, group, owners):
-    _, slots, width = own_occ.shape
-    rows, _ = first.shape
+def respond(occs, first, second, far, near, group, owners):
+    count, slots, width = occs[0].shape
+    rows, points = first.shape
     nv = far.shape[2]
-    occ_spec = pl.BlockSpec((2, slots, width), lambda k: (start + k, 0, 0))
-    row_spec = pl.BlockSpec((rows, 2 * width), lambda k: (0, start + k))
+    steps = count // 2
+    occ_spec = pl.BlockSpec((2, slots, width), lambda k: (k, 0, 0))
+    row_spec = pl.BlockSpec((rows, 2 * width), lambda k: (0, k))
     guess_spec = pl.BlockSpec(far.shape, lambda k: (0, 0, 0, 0))
     lines = 2 * nv // owners
     return pl.pallas_call(
         functools.partial(respond_kernel, group=group),
         grid=(steps,),
-        in_specs=[occ_spec, occ_spec, row_spec, row_spec, guess_spec, guess_spec],
+        in_specs=[occ_spec] * len(occs) + [row_spec, row_spec, guess_spec, guess_spec],
         out_specs=pl.BlockSpec((owners, lines, SIDE), lambda k: (0, k, 0)),
         out_shape=jax.ShapeDtypeStruct((owners, steps * lines, SIDE), BF16),
         cost_estimate=pl.CostEstimate(
-            flops=16 * slots * rows * width * steps * nv,
-            bytes_accessed=3_000_000,
+            flops=4 * len(occs) * slots * rows * points * nv,
+            bytes_accessed=6_000_000,
             transcendentals=0,
         ),
         compiler_params=ROOM,
         name="respond",
-    )(own_occ, other_occ, first, second, far, near)
-
-
-def columns_kernel(top_ref, bottom_ref, cols_ref, out_ref):
+    )(*occs, first, second, far, near)
+
+
+def columns_kernel(parts_ref, cols_ref, out_ref):
     copies, count, lines, side = out_ref.shape
     size = count * lines
-    planes = []
-    for ref in (top_ref, bottom_ref):
-        plane = ref[0].astype(F32)
-        for s in range(1, ref.shape[0]):
-            plane = plane + ref[s].astype(F32)
-        planes.append(plane)
-    plane = jnp.concatenate(planes, axis=0)
+    plane = parts_ref[0].astype(F32)
+    for s in range(1, parts_ref.shape[0]):
+        plane = plane + parts_ref[s].astype(F32)
     mixed = lax.dot_general(
         plane, cols_ref[...], (((1,), (1,)), ((), ())), precision=HIGH, preferred_element_type=F32
     ).astype(BF16)
@@ -205,8 +214,8 @@
     per_owner = nv // (nz * nx)
 
     blocks = jax.ShapeDtypeStruct((nz * nx, mine, width), BF16)
+    partner = swapped(orbitals, XH)
     by_points = exchanged(small_call(split_kernel, blocks, orbitals), ORB)
-    partner = swapped(orbitals, XH)
 
     def part_of(values, start, count):
         return lax.dynamic_slice_in_dim(values, start, count)
@@ -220,10 +229,8 @@
     place = jnp.arange(nv, dtype=jnp.int32)
     side = (xh + 1 + place // (nz * per_owner)) % nx
     source = (place // per_owner % nz * nx + side) * per_owner + place % per_owner
-    order = (source[:, None] == place[None, :]).astype(BF16)
-    pot = jnp.dot(order, potentials, preferred_element_type=F32).astype(BF16)
-    first = jnp.where(xh == 0, orbitals, partner)
-    second = jnp.where(xh == 0, partner, orbitals)
+    out = jax.ShapeDtypeStruct(potentials.shape, BF16)
+    pot = small_call(order_kernel, out, source[:, None], potentials)
 
     labels = jnp.arange(norb, dtype=jnp.int32)
     empty = 1.0 - jnp.any(occ_index[:, None] == labels[None, :], axis=0).astype(F32)
@@ -231,9 +238,9 @@
     own_levels = jnp.sum(
         jnp.where(own_slots[:, None] == labels[None, :], levels[None, :], 0.0), axis=1
     )
-    stored = z * nx * mine
-    basis_empty = part_of(empty, stored, nx * mine)
-    basis_levels = part_of(levels, stored, nx * mine)
+    stored = [(z * nx + n) * mine for n in (xh, 1 - xh)]
+    basis_empty = jnp.concatenate([part_of(empty, n, mine) for n in stored])
+    basis_levels = jnp.concatenate([part_of(levels, n, mine) for n in stored])
     weight = -2.0 * basis_empty[None, :] / (own_levels[:, None] + basis_levels[None, :])
     weight = (weight / volume).reshape(1, group * nx * mine)
 
@@ -243,14 +250,13 @@
         lax.dynamic_index_in_dim(my_rows, c, 2, keepdims=False).reshape(lines, chips * lines)
         for c in (core, 1 - core)
     ]
-    held_back = (occ, pot, first, second, weight, mixes)
-    occ, pot, first, second, weight, mixes = lax.optimization_barrier(held_back)
-
+    occ, pot, weight, mixes = lax.optimization_barrier((occ, pot, weight, mixes))
+
+    rest = (orbitals, partner, pot, group)
     other_occ = swapped(occ, XH)
-    rest = (first, second, pot, group)
-    far = project(occ, 0, half // 16, *rest)
+    far = project(occ, 0, *rest)
     far = swapped(far, CORE)
-    near = project(occ, half // 16, half // 16, *rest)
+    near = project(occ, 1, *rest)
     near, other_occ = lax.optimization_barrier((near, other_occ))
     summed = small_call(join_kernel, jax.ShapeDtypeStruct(near.shape, BF16), near, far)
     intersection = jnp.sum(exchanged(summed, CHIP).astype(F32), axis=0)
@@ -260,16 +266,10 @@
     guesses = jnp.stack([kept, swapped(given, XH)])
     near_guess = exchanged(jnp.broadcast_to(guesses, (chips, *guesses.shape)), CHIP)
     far_guess = swapped(near_guess, CORE)
-    parts = []
-    for n in range(2):
-        response = respond(
-            occ, other_occ, n * lines // 4, lines // 4, first, second, far_guess, near_guess,
-            group, nz,
-        )
-        parts.append(exchanged(response, Z))
+    response = respond((occ, other_occ), orbitals, partner, far_guess, near_guess, group, nz)
 
     out = jax.ShapeDtypeStruct((chips, per_owner, lines, SIDE), BF16)
-    columns = small_call(columns_kernel, out, *parts, coul_cols)
+    columns = small_call(columns_kernel, out, exchanged(response, Z), coul_cols)
     near_cols = exchanged(columns, CHIP)
     far_cols = swapped(near_cols, CORE)
     out = jax.ShapeDtypeStruct((per_owner, lines, SIDE), F32)

time: 178 us -> 173 us (0.972)
  local copies, waits for them, and re-layouts: 14.9 us -> 4.08 us
  blocking collectives: 58.6 us -> 69.4 us
  starting transfers between devices: 34.1 us -> 30.3 us
  waiting for transfers between devices: 33.8 us -> 36.3 us
  other arithmetic: 3.79 us -> 1.53 us
    all_to_all x4, blocking collectives: 58.6 us -> 69.4 us  [exchanged(): return lax.all_to_all(parts, axes, split_axis=0, concat_axis=0, tiled=True)]
    unnamed x26 -> x16, local copies, waits for them, and re-layouts: 7.88 us -> 1.97 us
    ppermute x6, starting transfers between devices: 18 us -> 14.4 us  [swapped(): return lax.ppermute(shard, axis, SWAP)]
    dynamic_slice x4, local copies, waits for them, and re-layouts: 3.1 us -> 1.03 us  [part_of(): return lax.dynamic_slice_in_dim(values, start, count)]
    pallas_call x2 -> x1, Pallas kernels: 14.3 us -> 12.7 us  [respond(): pl.pallas_call(functools.partial(respond_kernel, group=group), grid=(step...]
    all_to_all x3 -> x2, waiting for transfers between devices: 19.6 us -> 20.8 us  [exchanged(): return lax.all_to_all(parts, axes, split_axis=0, concat_axis=0, tiled=True)]
    pallas_call x5 -> x6, Pallas kernels: 3.6 us -> 4.2 us  [small_call(): return pl.pallas_call(kernel, out_shape=out, compiler_params=ROOM)(*args)]
    all_to_all x3 -> x2, starting transfers between devices: 16.1 us -> 15.9 us  [exchanged(): return lax.all_to_all(parts, axes, split_axis=0, concat_axis=0, tiled=True)]
  transfers between devices with their start and end apart: 9 -> 8, of which waited for: 7 -> 6; matrix products, arithmetic and copies ran while one was open for 6% -> 2% of each run, Pallas kernels for 9% -> 5%
where the time goes in v5:
time: 173 us; the launch traced here: 172 us
  blocking collectives  69.4 us (40%)
  waiting for transfers between devices  36.3 us (21%)
  Pallas kernels  30.4 us (18%)
  starting transfers between devices  30.3 us (18%)
  local copies, waits for them, and re-layouts  4.08 us (2%)
    all_to_all x4, blocking collectives, exchanged(): return lax.all_to_all(parts, axes, split_axis=0, concat_axis=0, tiled=True)  69.4 us
    all_to_all x2, waiting for transfers between devices, exchanged(): return lax.all_to_all(parts, axes, split_axis=0, concat_axis=0, tiled=True)  20.8 us
    all_to_all x2, starting transfers between devices, exchanged(): return lax.all_to_all(parts, axes, split_axis=0, concat_axis=0, tiled=True)  15.9 us
    ppermute x6, waiting for transfers between devices, swapped(): return lax.ppermute(shard, axis, SWAP)  15.5 us
    ppermute x6, starting transfers between devices, swapped(): return lax.ppermute(shard, axis, SWAP)  14.4 us
    pallas_call x2, Pallas kernels, project(): pl.pallas_call(functools.partial(project_kernel, group=group), grid=(step...  13.5 us
    pallas_call x1, Pallas kernels, respond(): pl.pallas_call(functools.partial(respond_kernel, group=group), grid=(step...  12.7 us
    pallas_call x6, Pallas kernels, small_call(): return pl.pallas_call(kernel, out_shape=out, compiler_params=ROOM)(*args)  4.2 us
  transfers between devices with their start and end apart: 8, of which 6 were waited for; matrix products, arithmetic and copies ran while one was open for 2% of the time, Pallas kernels for 5%

profile of v5, /device:TPU:1, one launch (start us, length us, event | category | flops | bytes accessed | tf_op | source)
XLA Modules:
  0.0 172.2 jit_solution(4221226321979111972)
XLA Ops:
  0.0 1.0 copy-done.3
  1.0 0.7 shard_map.64
  1.7 11.7 %all-to-all-start = ((bf16[16,32,256]{2,1,0:T(8,128)(2,1)}), bf16[16,32,256]{2,1,0:T(8,128)(2,1)S(1)}, u32[]{:S(2)}, u32[]{:S(2)}) async-start(bf16[16,32,256]{2,1,0:T(8,128)(2,1)} %shard_map.64), calls=%async_computation | async-start | bytes 524288 | tf_op jit(solution)/shard_map/all_to_all | solution.py:27
  13.4 2.9 %collective-permute-start = (bf16[32,4096]{1,0:T(8,128)(2,1)}, bf16[32,4096]{1,0:T(8,128)(2,1)}, u32[]{:S(2)}, u32[]{:S(2)}) collective-permute-start(bf16[32,4096]{1,0:T(8,128)(2,1)} %refs_2_.1), channel_id=1, source_target_pairs={{0,16},{16,0},{1,17},{17,1},{2,18},{18,2},{3,19},{19,3},{4,20},{20... | collective-permute-start | bytes 786440 | tf_op jit(solution)/shard_map/ppermute | solution.py:23
  16.3 0.9 fusion.19
  17.4 0.8 fusion
  18.1 7.4 %all-to-all-done = bf16[16,32,256]{2,1,0:T(8,128)(2,1)S(1)} async-done(((bf16[16,32,256]{2,1,0:T(8,128)(2,1)}), bf16[16,32,256]{2,1,0:T(8,128)(2,1)S(1)}, u32[]{:S(2)}, u32[]{:S(2)}) %all-to-all-start) | async-done | bytes 262176 | tf_op jit(solution)/shard_map/all_to_all | solution.py:27
  25.5 1.0 shard_map.65
  26.5 4.2 %all-to-all-start.1 = ((bf16[16,64,256]{2,1,0:T(8,128)(2,1)}), bf16[16,64,256]{2,1,0:T(8,128)(2,1)}, u32[]{:S(2)}, u32[]{:S(2)}) async-start(bf16[16,64,256]{2,1,0:T(8,128)(2,1)} %shard_map.65), calls=%async_computation.1 | async-start | bytes 1048576 | tf_op jit(solution)/shard_map/all_to_all | solution.py:27
  31.5 0.2 reshape.228
  31.7 0.4 dynamic-slice_reduce_fusion
  32.4 0.6 shard_map.66.pot_ref
  33.0 13.5 %all-to-all-done.1.occ_ref.refs_0_ = bf16[16,64,256]{2,1,0:T(8,128)(2,1)} async-done(((bf16[16,64,256]{2,1,0:T(8,128)(2,1)}), bf16[16,64,256]{2,1,0:T(8,128)(2,1)}, u32[]{:S(2)}, u32[]{:S(2)}) %all-to-all-start.1) | async-done | bytes 524320 | tf_op jit(solution)/shard_map/all_to_all | solution.py:27
  46.5 0.9 copy-done.4
  47.5 6.8 %project.3 = f32[8,192,256]{2,1,0:T(8,128)S(1)} custom-call(bf16[16,64,256]{2,1,0:T(8,128)(2,1)} %all-to-all-done.1.occ_ref.refs_0_, bf16[32,4096]{1,0:T(8,128)(2,1)S(1)} %copy-done.4, bf16[32,4096]{1,0:T(8,128)(2,1)} %collective-permute-done.second_ref.refs_3_, bf16[192,4096]{1,0:T(8,128)(2,1)S(1)} %shard_map.66.pot_ref), custom_call_target="tpu_custom_call" | custom-call | flops 3221225472 | bytes 4000000 | tf_op jit(solution)/shard_map/project/pallas_call | solution.py:87
  54.2 4.7 %collective-permute-start.2 = (f32[8,192,256]{2,1,0:T(8,128)S(1)}, f32[8,192,256]{2,1,0:T(8,128)S(1)}, u32[]{:S(2)}, u32[]{:S(2)}) collective-permute-start(f32[8,192,256]{2,1,0:T(8,128)S(1)} %project.3), channel_id=1, source_target_pairs={{0,1},{1,0},{2,3},{3,2},{4,5},{5,4},{6,7},{7,6},{8,9},{9,8},{10,11... | collective-permute-start | bytes 4718600 | tf_op jit(solution)/shard_map/ppermute | solution.py:23
  59.0 0.3 collective-permute-start.1
  59.2 6.7 %project.2.near_ref = f32[8,192,256]{2,1,0:T(8,128)S(1)} custom-call(bf16[16,64,256]{2,1,0:T(8,128)(2,1)} %all-to-all-done.1.occ_ref.refs_0_, bf16[32,4096]{1,0:T(8,128)(2,1)S(1)} %copy-done.5, bf16[32,4096]{1,0:T(8,128)(2,1)} %collective-permute-done.second_ref.refs_3_, bf16[192,4096]{1,0:T(8,128)(2,1)S(1)} %shard_map.66.pot_ref), custom_call_target="tpu_custom_call" | custom-call | flops 3221225472 | bytes 4000000 | tf_op jit(solution)/shard_map/project/pallas_call | solution.py:87
  66.0 8.1 %collective-permute-done.1.refs_1_ = bf16[16,64,256]{2,1,0:T(8,128)(2,1)S(1)} collective-permute-done((bf16[16,64,256]{2,1,0:T(8,128)(2,1)}, bf16[16,64,256]{2,1,0:T(8,128)(2,1)S(1)}, u32[]{:S(2)}, u32[]{:S(2)}) %collective-permute-start.1) | collective-permute-done | bytes 524320 | tf_op jit(solution)/shard_map/ppermute | solution.py:23
  74.2 15.8 %all_to_all.30 = bf16[8,192,256]{2,1,0:T(8,128)(2,1)S(1)} all-to-all(bf16[8,192,256]{2,1,0:T(8,128)(2,1)S(1)} %shard_map.67), channel_id=1, replica_groups=mesh['z'=8,'x_hi'=2,'y'=4,'x_lo'=2,'core'=2] {'y','x_lo'}, dimensions={0} | all-to-all | bytes 1572864 | tf_op jit(solution)/shard_map/all_to_all | solution.py:27
  90.1 1.0 collective-permute-start.3
  91.1 3.6 %collective-permute-done.3 = bf16[96,256]{1,0:T(8,128)(2,1)S(1)} collective-permute-done((bf16[96,256]{1,0:T(8,128)(2,1)S(1)}, bf16[96,256]{1,0:T(8,128)(2,1)S(1)}, u32[]{:S(2)}, u32[]{:S(2)}) %collective-permute-start.3) | collective-permute-done | bytes 49184 | tf_op jit(solution)/shard_map/ppermute | solution.py:23
  94.7 13.0 %all_to_all.31.refs_5_ = bf16[8,2,96,256]{3,2,1,0:T(8,128)(2,1)S(1)} all-to-all(bf16[8,2,96,256]{3,2,1,0:T(8,128)(2,1)S(1)} %broadcast_in_dim.30), channel_id=1, replica_groups=mesh['z'=8,'x_hi'=2,'y'=4,'x_lo'=2,'core'=2] {'y','x_lo'}, dimensions={0} | all-to-all | bytes 1572864 | tf_op jit(solution)/shard_map/all_to_all | solution.py:27
  107.8 3.7 %collective-permute-start.4 = (bf16[8,2,96,256]{3,2,1,0:T(8,128)(2,1)S(1)}, bf16[8,2,96,256]{3,2,1,0:T(8,128)(2,1)S(1)}, u32[]{:S(2)}, u32[]{:S(2)}) collective-permute-start(bf16[8,2,96,256]{3,2,1,0:T(8,128)(2,1)S(1)} %all_to_all.31.refs_5_), channel_id=1, source_target_pairs={{0,1},{1,0},{2,3},{3,2},{4,5},{5,4},{6,7},{7,6},{8,9},{9,8},{10,11... | collective-permute-start | bytes 2359304 | tf_op jit(solution)/shard_map/ppermute | solution.py:23
  111.5 1.9 %collective-permute-done.4.refs_4_ = bf16[8,2,96,256]{3,2,1,0:T(8,128)(2,1)S(1)} collective-permute-done((bf16[8,2,96,256]{3,2,1,0:T(8,128)(2,1)S(1)}, bf16[8,2,96,256]{3,2,1,0:T(8,128)(2,1)S(1)}, u32[]{:S(2)}, u32[]{:S(2)}) %collective-permute-start.4) | collective-permute-done | bytes 786464 | tf_op jit(solution)/shard_map/ppermute | solution.py:23
  113.4 12.7 %respond.1 = bf16[8,192,256]{2,1,0:T(8,128)(2,1)S(1)} custom-call(bf16[16,64,256]{2,1,0:T(8,128)(2,1)} %all-to-all-done.1.occ_ref.refs_0_, bf16[16,64,256]{2,1,0:T(8,128)(2,1)S(1)} %collective-permute-done.1.refs_1_, bf16[32,4096]{1,0:T(8,128)(2,1)S(1)} %copy-done.5, bf16[32,4096]{1,0:T(8,128)(2,1)} %collective-permute-done.second_ref.refs_3_, ...), custom_call_target="tpu_custom_call" | custom-call | flops 6442450944 | bytes 6000000 | tf_op jit(solution)/shard_map/respond/pallas_call | solution.py:141
  126.2 26.1 %all_to_all.32.parts_ref = bf16[8,192,256]{2,1,0:T(8,128)(2,1)S(1)} all-to-all(bf16[8,192,256]{2,1,0:T(8,128)(2,1)S(1)} %respond.1), channel_id=1, replica_groups=mesh['z'=8,'x_hi'=2,'y'=4,'x_lo'=2,'core'=2] {'z'}, dimensions={0} | all-to-all | bytes 1572864 | tf_op jit(solution)/shard_map/all_to_all | solution.py:27
  152.2 0.7 shard_map.68
  152.9 14.5 %all_to_all.33.near_ref = bf16[8,12,16,256]{3,2,1,0:T(8,128)(2,1)S(1)} all-to-all(bf16[8,12,16,256]{3,2,1,0:T(8,128)(2,1)S(1)} %shard_map.68), channel_id=1, replica_groups=mesh['z'=8,'x_hi'=2,'y'=4,'x_lo'=2,'core'=2] {'y','x_lo'}, dimensions={0} | all-to-all | bytes 1572864 | tf_op jit(solution)/shard_map/all_to_all | solution.py:27
  167.4 1.8 %collective-permute-start.5 = (bf16[8,12,16,256]{3,2,1,0:T(8,128)(2,1)S(1)}, bf16[8,12,16,256]{3,2,1,0:T(8,128)(2,1)S(1)}, u32[]{:S(2)}, u32[]{:S(2)}) collective-permute-start(bf16[8,12,16,256]{3,2,1,0:T(8,128)(2,1)S(1)} %all_to_all.33.near_ref), channel_id=1, source_target_pairs={{0,1},{1,0},{2,3},{3,2},{4,5},{5,4},{6,7},{7,6},{8,9},{9,8},{10,11... | collective-permute-start | bytes 2359304 | tf_op jit(solution)/shard_map/ppermute | solution.py:23
  169.2 1.9 %collective-permute-done.5.far_ref = bf16[8,12,16,256]{3,2,1,0:T(8,128)(2,1)S(1)} collective-permute-done((bf16[8,12,16,256]{3,2,1,0:T(8,128)(2,1)S(1)}, bf16[8,12,16,256]{3,2,1,0:T(8,128)(2,1)S(1)}, u32[]{:S(2)}, u32[]{:S(2)}) %collective-permute-start.5) | collective-permute-done | bytes 786464 | tf_op jit(solution)/shard_map/ppermute | solution.py:23
  171.1 1.0 shard_map.69
  (36 shorter events, 1.5 us)
Async XLA Ops:
  0.0 31.5 %copy-start = (f32[256,256]{1,0:T(8,128)S(1)}, f32[256,256]{1,0:T(8,128)}, u32[]{:S(2)}) copy-start(f32[256,256]{1,0:T(8,128)} %param.10) | copy-start | bytes 786436
  0.0 1.0 copy-start.3
  1.0 29.8 %copy-start.6 = (s32[128]{0:T(128)S(1)}, s32[128]{0:T(128)}, u32[]{:S(2)}) copy-start(s32[128]{0:T(128)} %param.9) | copy-start | bytes 1540
  1.0 29.9 %copy-start.7 = (f32[512]{0:T(512)S(1)}, f32[512]{0:T(512)}, u32[]{:S(2)}) copy-start(f32[512]{0:T(512)} %param.8) | copy-start | bytes 6148
  1.7 30.7 %copy-start.1 = (bf16[192,4096]{1,0:T(8,128)(2,1)S(1)}, bf16[192,4096]{1,0:T(8,128)(2,1)}, u32[]{:S(2)}) copy-start(bf16[192,4096]{1,0:T(8,128)(2,1)} %rows_ref.3) | copy-start | bytes 4718596
  1.7 23.8 %all-to-all-start = ((bf16[16,32,256]{2,1,0:T(8,128)(2,1)}), bf16[16,32,256]{2,1,0:T(8,128)(2,1)S(1)}, u32[]{:S(2)}, u32[]{:S(2)}) async-start(bf16[16,32,256]{2,1,0:T(8,128)(2,1)} %shard_map.64), calls=%async_computation | async-start | bytes 524288 | tf_op jit(solution)/shard_map/all_to_all | solution.py:27
  13.4 33.1 %collective-permute-start = (bf16[32,4096]{1,0:T(8,128)(2,1)}, bf16[32,4096]{1,0:T(8,128)(2,1)}, u32[]{:S(2)}, u32[]{:S(2)}) collective-permute-start(bf16[32,4096]{1,0:T(8,128)(2,1)} %refs_2_.1), channel_id=1, source_target_pairs={{0,16},{16,0},{1,17},{17,1},{2,18},{18,2},{3,19},{19,3},{4,20},{20... | collective-permute-start | bytes 786440 | tf_op jit(solution)/shard_map/ppermute | solution.py:23
  26.5 20.0 %all-to-all-start.1 = ((bf16[16,64,256]{2,1,0:T(8,128)(2,1)}), bf16[16,64,256]{2,1,0:T(8,128)(2,1)}, u32[]{:S(2)}, u32[]{:S(2)}) async-start(bf16[16,64,256]{2,1,0:T(8,128)(2,1)} %shard_map.65), calls=%async_computation.1 | async-start | bytes 1048576 | tf_op jit(solution)/shard_map/all_to_all | solution.py:27
  46.5 1.0 copy-start.4
  47.5 11.8 %copy-start.5 = (bf16[32,4096]{1,0:T(8,128)(2,1)S(1)}, bf16[32,4096]{1,0:T(8,128)(2,1)}, u32[]{:S(2)}) copy-start(bf16[32,4096]{1,0:T(8,128)(2,1)} %refs_2_.1) | copy-start | bytes 786436
  54.2 19.8 %collective-permute-start.2 = (f32[8,192,256]{2,1,0:T(8,128)S(1)}, f32[8,192,256]{2,1,0:T(8,128)S(1)}, u32[]{:S(2)}, u32[]{:S(2)}) collective-permute-start(f32[8,192,256]{2,1,0:T(8,128)S(1)} %project.3), channel_id=1, source_target_pairs={{0,1},{1,0},{2,3},{3,2},{4,5},{5,4},{6,7},{7,6},{8,9},{9,8},{10,11... | collective-permute-start | bytes 4718600 | tf_op jit(solution)/shard_map/ppermute | solution.py:23
  59.0 15.1 %collective-permute-start.1 = (bf16[16,64,256]{2,1,0:T(8,128)(2,1)}, bf16[16,64,256]{2,1,0:T(8,128)(2,1)S(1)}, u32[]{:S(2)}, u32[]{:S(2)}) collective-permute-start(bf16[16,64,256]{2,1,0:T(8,128)(2,1)} %all-to-all-done.1.occ_ref.refs_0_), channel_id=1, source_target_pairs={{0,16},{16,0},{1,17},{17,1},{2,18},{18,2},{3,19},{19,3},{4,20},{20... | collective-permute-start | bytes 1572872 | tf_op jit(solution)/shard_map/ppermute | solution.py:23
  90.1 4.5 %collective-permute-start.3 = (bf16[96,256]{1,0:T(8,128)(2,1)S(1)}, bf16[96,256]{1,0:T(8,128)(2,1)S(1)}, u32[]{:S(2)}, u32[]{:S(2)}) collective-permute-start(bf16[96,256]{1,0:T(8,128)(2,1)S(1)} %get-tuple-element.22), channel_id=1, source_target_pairs={{0,16},{16,0},{1,17},{17,1},{2,18},{18,2},{3,19},{19,3},{4,20},{20... | collective-permute-start | bytes 147464 | tf_op jit(solution)/shard_map/ppermute | solution.py:23
  107.8 5.7 %collective-permute-start.4 = (bf16[8,2,96,256]{3,2,1,0:T(8,128)(2,1)S(1)}, bf16[8,2,96,256]{3,2,1,0:T(8,128)(2,1)S(1)}, u32[]{:S(2)}, u32[]{:S(2)}) collective-permute-start(bf16[8,2,96,256]{3,2,1,0:T(8,128)(2,1)S(1)} %all_to_all.31.refs_5_), channel_id=1, source_target_pairs={{0,1},{1,0},{2,3},{3,2},{4,5},{5,4},{6,7},{7,6},{8,9},{9,8},{10,11... | collective-permute-start | bytes 2359304 | tf_op jit(solution)/shard_map/ppermute | solution.py:23
  126.2 26.1 %copy-start.2 = (f32[256,256]{1,0:T(8,128)S(1)}, f32[256,256]{1,0:T(8,128)}, u32[]{:S(2)}) copy-start(f32[256,256]{1,0:T(8,128)} %cols_ref.1) | copy-start | bytes 786436
  167.4 3.7 %collective-permute-start.5 = (bf16[8,12,16,256]{3,2,1,0:T(8,128)(2,1)S(1)}, bf16[8,12,16,256]{3,2,1,0:T(8,128)(2,1)S(1)}, u32[]{:S(2)}, u32[]{:S(2)}) collective-permute-start(bf16[8,12,16,256]{3,2,1,0:T(8,128)(2,1)S(1)} %all_to_all.33.near_ref), channel_id=1, source_target_pairs={{0,1},{1,0},{2,3},{3,2},{4,5},{5,4},{6,7},{7,6},{8,9},{9,8},{10,11... | collective-permute-start | bytes 2359304 | tf_op jit(solution)/shard_map/ppermute | solution.py:23
